TPU v7x, 128 devices: a whole 4x4x4 slice. The times are simulated.
128 devices in a mesh: section: 16 (over z_lo, y, core), ep: 8 (over z_hi, x).
Axes of the slice: x: 4, y: 4, z: 4 (z_hi: 2, z_lo: 2; z = z_hi * 2 + z_lo), core: 2. Of those that a mesh axis runs over, the one named last changes fastest.
Arguments:
- fwd_input: bfloat16 [16, 1024, 3584], P('section', 'ep'), may hold values from -6 to 6
- bwd_input: bfloat16 [16, 1024, 3584], P('section', 'ep'), may hold values from -6 to 6
- bwd_grad: bfloat16 [16, 1024, 3584], P('section', 'ep'), may hold values from -6 to 6
- fwd_ids: int32 [16, 1024, 2], P('section', 'ep'), may hold values from 0 to 7, all different within a row; in each aligned block of 128 rows (0 to 127, 128 to 255, ...) at most 48 rows name the same one
- bwd_ids: int32 [16, 1024, 2], P('section', 'ep'), may hold values from 0 to 7, all different within a row; in each aligned block of 128 rows (0 to 127, 128 to 255, ...) at most 48 rows name the same one
- norm_gain: float32 [16, 3584], P('section'), may hold values from 0.5 to 1.5
- router: bfloat16 [16, 3584, 8], P('section'), may hold values from -0.09375 to 0.09375
- gate_w: bfloat16 [16, 8, 3584, 1024], P('section', 'ep'), may hold values from -0.09375 to 0.09375
- up_w: bfloat16 [16, 8, 3584, 1024], P('section', 'ep'), may hold values from -0.09375 to 0.09375
- down_w: bfloat16 [16, 8, 1024, 3584], P('section', 'ep'), may hold values from -0.1875 to 0.1875
Outputs:
- fwd_next: bfloat16 [16, 1024, 3584], P('section', 'ep')
- bwd_prev: bfloat16 [16, 1024, 3584], P('section', 'ep')
Inputs may be any that keep to these rules, and one draw needn't show every extreme that they name: `fwd_ids`: each token names 2 different experts of 0 to 7; among the 128 tokens of one index of ep in one section no expert is named more than 48 times, a bound that some block reaches. `bwd_ids`: each token names 2 different experts of 0 to 7; among the 128 tokens of one index of ep in one section no expert is named more than 48 times, a bound that some block reaches.
All inputs are finite; a program needn't handle non-finite values.
Results may differ from a plain program's by a relative error of at most 0.0035.
Values may be sent and summed in bfloat16 or wider, within the bound.
No kernel may reach another device: no remote copies, remote signals or barrier semaphores. Data moves between devices by JAX's collectives and lax.ppermute only.
A program may use at most 128 MiB of HBM per device.

v0:
```python
import functools
import jax
import jax.numpy as jnp
from jax import lax
from jax.experimental import pallas as pl
from jax.experimental.pallas import tpu as pltpu
from jax.sharding import PartitionSpec as P


NORM_EPSILON = 1e-06
ROUTE_SCALE = 2.5

T = 128
D = 3584
F = 1024
CAP = 48
NX = 4
NZ = 2
ROWS = NX * NZ * CAP
TF = 256
TD = 512
EXT = 128
f32 = jnp.float32
bf16 = jnp.bfloat16
NT = (((1,), (1,)), ((), ()))


def call(body, outs, ins, grid=None, in_specs=None, out_specs=None, scratch=(), flops=0, after=None):
    kwargs = {}
    if after is not None:
        inner, count = body, len(ins)
        ins = (*ins, after)
        in_specs = [*in_specs, pl.BlockSpec(memory_space=pl.ANY)]

        def body(*refs):
            inner(*refs[:count], *refs[count + 1 :])

    if grid is not None:
        kwargs["grid"] = grid
    if in_specs is not None:
        kwargs["in_specs"] = in_specs
    if out_specs is not None:
        kwargs["out_specs"] = out_specs
    moved = sum(a.size * a.dtype.itemsize for a in ins) + sum(o.size * o.dtype.itemsize for o in outs)
    return pl.pallas_call(
        body,
        out_shape=outs,
        scratch_shapes=list(scratch),
        cost_estimate=pl.CostEstimate(flops=int(flops), bytes_accessed=int(moved), transcendentals=0),
        **kwargs,
    )(*ins)


def vspec(shape, index=None):
    fixed = index if index is not None else (0,) * len(shape)
    return pl.BlockSpec(shape, lambda *_: fixed)


def chip():
    return pl.BlockSpec(memory_space=pltpu.VMEM)


def sspec():
    return pl.BlockSpec(memory_space=pltpu.SMEM)


def shape(*dims, dtype=bf16):
    return jax.ShapeDtypeStruct(dims, dtype)


def slots_of(named, place_ref):
    half, column = place_ref[0], place_ref[1]
    lane = lax.broadcasted_iota(jnp.int32, (T, T), 1)
    row = lax.broadcasted_iota(jnp.int32, (T, T), 0)
    member = jnp.where((lane == named[0]) | (lane == named[1]), 1.0, 0.0).astype(bf16)
    before = jnp.where(lane < row, 1.0, 0.0).astype(bf16)
    rank = jnp.dot(before, member, preferred_element_type=f32)
    slots = []
    for name in named:
        own_rank = jnp.sum(jnp.where(lane == name, rank, 0.0), axis=1, keepdims=True)
        step = ((name - column) & (NX - 1)).astype(f32)
        slots.append(jnp.where((name >> 2) == half, step * CAP + own_rank, -1.0))
    return slots


def names_of(ids_ref, first):
    return [ids_ref[:, first + k : first + k + 1] for k in range(2)]


def pack(slots, row_tile, outs, weights=None):
    lane = lax.broadcasted_iota(jnp.int32, (T, 256), 1).astype(f32)
    hits = [lane == slot for slot in slots]
    chosen = jnp.transpose(jnp.where(hits[0] | hits[1], 1.0, 0.0))[: NX * CAP].astype(bf16)
    if weights is not None:
        scale = jnp.where(hits[0], weights[0], 0.0) + jnp.where(hits[1], weights[1], 0.0)
        scale = ROUTE_SCALE * jnp.sum(jnp.transpose(scale), axis=1, keepdims=True)[: NX * CAP]
    for n in range(D // TD):
        cols = slice(n * TD, (n + 1) * TD)
        picked = jnp.dot(chosen, row_tile(cols), preferred_element_type=f32)
        if weights is not None:
            picked = scale * picked
        picked = picked.astype(bf16)
        for step in range(NX):
            outs[step][:, cols] = picked[step * CAP : (step + 1) * CAP]


def prep_grad_body(aux_ref, rows_ref, *outs):
    aux = aux_ref[...]
    pack([aux[:, 0:1], aux[:, 1:2]], lambda cols: rows_ref[:, cols], outs, [aux[:, 2:3], aux[:, 3:4]])


def prep_norm_body(first, place_ref, ids_ref, rows_ref, gain_ref, router_ref, *refs):
    outs, aux_ref, normed_ref = refs[:NX], refs[NX], refs[NX + 1]
    named = names_of(ids_ref, first)
    slots = slots_of(named, place_ref)
    total = jnp.zeros((T, 1), f32)
    for n in range(D // TD):
        tile = rows_ref[:, n * TD : (n + 1) * TD].astype(f32)
        total = total + jnp.sum(tile * tile, axis=1, keepdims=True)
    inverse = lax.rsqrt(total / D + NORM_EPSILON)
    for n in range(D // TD):
        cols = slice(n * TD, (n + 1) * TD)
        normed_ref[:, cols] = (rows_ref[:, cols].astype(f32) * inverse * gain_ref[:, cols]).astype(bf16)
    pack(slots, lambda cols: normed_ref[:, cols], outs)
    logits = lax.dot_general(normed_ref[...], router_ref[...], NT, preferred_element_type=f32)
    scores = jax.nn.sigmoid(logits)
    lane = lax.broadcasted_iota(jnp.int32, scores.shape, 1)
    picked = [jnp.sum(jnp.where(lane == name, scores, 0.0), axis=1, keepdims=True) for name in named]
    both = picked[0] + picked[1]
    columns = slots + [p / both for p in picked] + picked + [both, inverse] + [name.astype(f32) for name in named]
    lane = lax.broadcasted_iota(jnp.int32, (T, 128), 1)
    aux = jnp.zeros((T, 128), f32)
    for i, column in enumerate(columns):
        aux = jnp.where(lane == i, column, aux)
    aux_ref[...] = aux


def gather_rows(pieces, rows_ref):
    for step in range(NX):
        for z in range(NZ):
            at = (step * NZ + z) * CAP
            rows_ref[at : at + CAP, :] = pieces[z * NX + step][...]


def lift_body(*refs):
    pieces, gate_ref, up_ref, a_ref, b_ref, rows_ref = refs[:8], refs[8], refs[9], refs[10], refs[11], refs[12]

    @pl.when(pl.program_id(0) == 0)
    def _():
        gather_rows(pieces, rows_ref)

    rows = rows_ref[...]
    a_ref[...] = jnp.dot(rows, gate_ref[...], preferred_element_type=f32)
    b_ref[...] = jnp.dot(rows, up_ref[...], preferred_element_type=f32)


def hidden_grad_body(*refs):
    pieces, down_ref, a_ref, b_ref = refs[:8], refs[8], refs[9], refs[10]
    d_gate_ref, d_up_ref, dot_ref, rows_ref = refs[11:]

    @pl.when(pl.program_id(0) == 0)
    def _():
        gather_rows(pieces, rows_ref)
        dot_ref[...] = jnp.zeros_like(dot_ref)

    d_act = lax.dot_general(rows_ref[...], down_ref[...], NT, preferred_element_type=f32)
    a, b = a_ref[...], b_ref[...]
    s = jax.nn.sigmoid(a)
    active = (a * s * b).astype(bf16).astype(f32)
    both = active * d_act
    dot_ref[...] += both[:, :128] + both[:, 128:]
    d_gate_ref[...] = (d_act * b * s * (1.0 + a * (1.0 - s))).astype(bf16)
    d_up_ref[...] = (d_act * a * s).astype(bf16)


def back_body(d_gate_ref, d_up_ref, dot_ref, gate_ref, up_ref, *outs):
    i = pl.program_id(0)
    back = lax.dot_general(d_gate_ref[...], gate_ref[...], NT, preferred_element_type=f32)
    back = back + lax.dot_general(d_up_ref[...], up_ref[...], NT, preferred_element_type=f32)
    back = back.astype(bf16)
    for step in range(NX):
        outs[step][:, pl.ds(pl.multiple_of(i * TD, TD), TD)] = back[step * NZ * CAP : (step + 1) * NZ * CAP]

    @pl.when(i == 0)
    def _():
        dots = jnp.sum(dot_ref[...], axis=1, keepdims=True)
        high = dots.astype(bf16).astype(f32)
        lane = lax.broadcasted_iota(jnp.int32, (ROWS, EXT), 1)
        extra = jnp.where(lane == 0, high, jnp.where(lane == 1, dots - high, 0.0)).astype(bf16)
        for step in range(NX):
            outs[step][:, D:] = extra[step * NZ * CAP : (step + 1) * NZ * CAP]


def hidden_body(*refs):
    pieces, gate_ref, up_ref, out_ref, rows_ref = refs[:8], refs[8], refs[9], refs[10], refs[11]

    @pl.when(pl.program_id(0) == 0)
    def _():
        gather_rows(pieces, rows_ref)

    rows = rows_ref[...]
    a = jnp.dot(rows, gate_ref[...], preferred_element_type=f32)
    b = jnp.dot(rows, up_ref[...], preferred_element_type=f32)
    out_ref[...] = (a * jax.nn.sigmoid(a) * b).astype(bf16)


def down_body(active_ref, down_ref, *outs):
    i = pl.program_id(0)
    out = jnp.dot(active_ref[...], down_ref[...], preferred_element_type=f32).astype(bf16)
    for z in range(NZ):
        for step in range(NX):
            at = (step * NZ + z) * CAP
            outs[z * NX + step][:, pl.ds(pl.multiple_of(i * TD, TD), TD)] = out[at : at + CAP]


def split_weights(values):
    high = values.astype(bf16)
    return high, (values - high.astype(f32)).astype(bf16)


def hits_of(aux):
    lane = lax.broadcasted_iota(jnp.int32, (T, 256), 1).astype(f32)
    return [lane == aux[:, k : k + 1] for k in range(2)]


def stack_pieces(pieces, rows_ref):
    for step in range(NX):
        rows_ref[step * CAP : (step + 1) * CAP, :] = pieces[step][...]
    rows_ref[NX * CAP :, :] = jnp.zeros((256 - NX * CAP, rows_ref.shape[1]), bf16)


def mix_body(with_input, aux_ref, *refs):
    pieces, base_ref, out_ref, rows_ref = refs[:NX], refs[NX], refs[NX + 1], refs[NX + 2]
    stack_pieces(pieces, rows_ref)
    aux = aux_ref[...]
    hits = hits_of(aux)
    weights = jnp.where(hits[0], aux[:, 2:3], 0.0) + jnp.where(hits[1], aux[:, 3:4], 0.0)
    high, low = split_weights(ROUTE_SCALE * weights)
    for n in range(D // TD):
        cols = slice(n * TD, (n + 1) * TD)
        rows = rows_ref[:, cols]
        total = jnp.dot(high, rows, preferred_element_type=f32) + jnp.dot(low, rows, preferred_element_type=f32)
        if with_input:
            total = total + base_ref[:, cols].astype(f32)
        out_ref[:, cols] = total.astype(bf16)


def grad_input_body(with_input, aux_ref, hidden_ref, gain_ref, router_ref, *refs):
    pieces, base_ref, out_ref, rows_ref, scaled_ref = refs[:NX], refs[NX], refs[NX + 1], refs[NX + 2], refs[NX + 3]
    stack_pieces(pieces, rows_ref)
    aux = aux_ref[...]
    hits = [jnp.where(hit, 1.0, 0.0) for hit in hits_of(aux)]
    named = (hits[0] + hits[1]).astype(bf16)
    extra = rows_ref[:, D:]
    pulls = []
    for hit in hits:
        found = jnp.dot(hit.astype(bf16), extra, preferred_element_type=f32)
        pulls.append(found[:, 0:1] + found[:, 1:2])
    inverse = aux[:, 7:8]
    lane = lax.broadcasted_iota(jnp.int32, (T, router_ref.shape[0]), 1).astype(f32)
    d_logits = jnp.zeros(lane.shape, f32)
    for k in range(2):
        weight, score = aux[:, 2 + k : 3 + k], aux[:, 4 + k : 5 + k]
        term = (pulls[k] - weight * (pulls[0] + pulls[1])) * (1.0 - score)
        d_logits = d_logits + jnp.where(lane == aux[:, 8 + k : 9 + k], term, 0.0)
    log_high, log_low = split_weights(d_logits)
    against = jnp.zeros((T, 1), f32)
    for n in range(D // TD):
        cols = slice(n * TD, (n + 1) * TD)
        rows = rows_ref[:, cols]
        route = router_ref[:, cols]
        total = jnp.dot(named, rows, preferred_element_type=f32)
        total = total + jnp.dot(log_high, route, preferred_element_type=f32)
        total = total + jnp.dot(log_low, route, preferred_element_type=f32)
        scaled = total * gain_ref[:, cols]
        scaled_ref[:, cols] = scaled
        against = against + jnp.sum(scaled * hidden_ref[:, cols].astype(f32), axis=1, keepdims=True)
    pull = inverse * inverse * inverse * against / D
    for n in range(D // TD):
        cols = slice(n * TD, (n + 1) * TD)
        out = inverse * scaled_ref[:, cols] - hidden_ref[:, cols].astype(f32) * pull
        if with_input:
            out = out + base_ref[:, cols].astype(f32)
        out_ref[:, cols] = out.astype(bf16)


def ep_route(dz, dx):
    route = []
    for i in range(NZ * NX):
        z, x = divmod(i, NX)
        route.append((i, ((z + dz) % NZ) * NX + (x + dx) % NX))
    return route


def relay_route(sections, ds, dz):
    route = []
    for s in range(sections):
        for i in range(NZ * NX):
            z, x = divmod(i, NX)
            route.append((s * NZ * NX + i, ((s + ds) % sections) * NZ * NX + ((z + dz) % NZ) * NX + x))
    return route


def across(block):
    return lax.ppermute(block, "ep", ep_route(1, 0))


def spread(pieces):
    moved = list(pieces)
    for dx in (1, 3, 2):
        moved[dx] = lax.ppermute(pieces[dx], "ep", ep_route(0, dx))
    return moved


def collect(pieces):
    moved = list(pieces)
    for dx in (1, 3, 2):
        moved[dx] = lax.ppermute(pieces[dx], "ep", ep_route(0, -dx))
    return moved


def relay(block, ds, dz):
    return lax.ppermute(block, ("section", "ep"), relay_route(lax.axis_size("section"), ds, dz))


def step(
    fwd_input, bwd_input, bwd_grad, fwd_ids, bwd_ids, norm_gain, router, gate_w, up_w, down_w
):
    h_f, h_b, g = fwd_input[0], bwd_input[0], bwd_grad[0]
    gate, up, down = gate_w[0, 0], up_w[0, 0], down_w[0, 0]
    router_t = jnp.pad(router[0].T, ((0, 8), (0, 0)))
    own_ids = jnp.concatenate([bwd_ids[0], fwd_ids[0]], axis=1)
    index = lax.axis_index("ep")
    place = jnp.stack([index // NX, index % NX]).astype(jnp.int32)

    far_ids = across(own_ids)
    far_b = across(h_b)
    far_g = across(g)
    far_f = across(h_f)

    packed = [shape(CAP, D)] * NX
    aux_shape = shape(T, 128, dtype=f32)
    full = vspec((T, D))
    aux_spec = chip()
    piece_specs = [chip()] * NX
    pack_flops = 2 * NX * CAP * T * D

    def prep_grad(where, rows, aux):
        return call(
            prep_grad_body, packed, (aux, rows), grid=(1,), in_specs=[aux_spec, chip() if where == "far" else full], out_specs=piece_specs,
            flops=pack_flops,
        )

    def prep_norm(where, rows, ids, first, after=None):
        outs = call(
            functools.partial(prep_norm_body, first), packed + [aux_shape],
            (place, ids, rows, norm_gain, router_t), grid=(1,),
            in_specs=[sspec(), chip(), chip() if "far" in where else full, vspec((1, D)), vspec((16, D))],
            out_specs=piece_specs + [aux_spec], scratch=[pltpu.VMEM((T, D), bf16)],
            flops=pack_flops, after=after,
        )
        return outs[:NX], outs[NX]

    packed_b, aux_b = prep_norm("b_own", h_b, own_ids, 0)
    b_own = spread(packed_b)
    packed_g = prep_grad("own", g, aux_b)
    g_own = spread(packed_g)
    packed_bf, aux_b_far = prep_norm("b_far", far_b, far_ids, 0, packed_g[0])
    b_far = spread(packed_bf)
    packed_gf = prep_grad("far", far_g, aux_b_far)
    g_far = spread(packed_gf)
    packed_f, aux_f = prep_norm("f_own", h_f, own_ids, 2, packed_gf[0])
    f_own = spread(packed_f)

    eight = [chip()] * 8
    rows_scratch = pltpu.VMEM((ROWS, D), bf16)
    wide = pl.BlockSpec((D, TF), lambda i: (0, i))
    hidden_spec = pl.BlockSpec((ROWS, TF), lambda i: (0, i))
    dots_spec = vspec((ROWS, 128))
    hidden_f32 = shape(ROWS, F, dtype=f32)
    mat_flops = 2 * ROWS * D * F

    a, b = call(
        lift_body, [hidden_f32] * 2, (*b_own, *b_far, gate, up), grid=(F // TF,),
        in_specs=eight + [wide, wide], out_specs=[hidden_spec] * 2, scratch=[rows_scratch],
        flops=2 * mat_flops, after=packed_f[0],
    )
    packed_ff, aux_f_far = prep_norm("f_far", far_f, far_ids, 2, a)
    f_far = spread(packed_ff)
    d_gate, d_up, dots = call(
        hidden_grad_body, [shape(ROWS, F), shape(ROWS, F), shape(ROWS, 128, dtype=f32)],
        (*g_own, *g_far, down, a, b), grid=(F // TF,),
        in_specs=eight + [pl.BlockSpec((TF, D), lambda i: (i, 0)), hidden_spec, hidden_spec],
        out_specs=[hidden_spec, hidden_spec, dots_spec], scratch=[rows_scratch], flops=mat_flops,
        after=packed_ff[0],
    )
    tall = pl.BlockSpec((TD, F), lambda i: (i, 0))
    returned = call(
        back_body, [shape(NZ * CAP, D + EXT)] * NX, (d_gate, d_up, dots, gate, up), grid=(D // TD,),
        in_specs=[vspec((ROWS, F)), vspec((ROWS, F)), dots_spec, tall, tall],
        out_specs=[chip()] * NX, flops=2 * mat_flops,
    )
    back = collect(returned)

    (active,) = call(
        hidden_body, [shape(ROWS, F)], (*f_own, *f_far, gate, up), grid=(F // TF,),
        in_specs=eight + [wide, wide], out_specs=[hidden_spec], scratch=[rows_scratch],
        flops=2 * mat_flops, after=returned[0],
    )
    outputs = call(
        down_body, [shape(CAP, D)] * 8, (active, down), grid=(D // TD,),
        in_specs=[vspec((ROWS, F)), pl.BlockSpec((F, TD), lambda i: (0, i))], out_specs=eight,
        flops=mat_flops,
    )
    y_far = collect(outputs[NX:])
    y_own = collect(outputs[:NX])

    def mix(pieces, aux, base, with_input, after):
        return call(
            functools.partial(mix_body, with_input), [shape(T, D)], (aux, *pieces, base), grid=(1,),
            in_specs=[aux_spec] + piece_specs + [full if with_input else vspec((16, D))],
            out_specs=[full], scratch=[pltpu.VMEM((256, D), bf16)], flops=2 * pack_flops, after=after,
        )[0]

    def grad_input(z, aux, hidden, base, with_input, after):
        halves = [vspec((CAP, D + EXT), (z, 0))] * NX
        return call(
            functools.partial(grad_input_body, with_input), [shape(T, D)],
            (aux, hidden, norm_gain, router_t, *back, base), grid=(1,),
            in_specs=[aux_spec, full, vspec((1, D)), vspec((16, D))] + halves
            + [full if with_input else vspec((16, D))],
            out_specs=[full], scratch=[pltpu.VMEM((256, D + EXT), bf16), pltpu.VMEM((T, D), f32)],
            flops=2 * pack_flops, after=after,
        )[0]

    part_far = grad_input(1, aux_b_far, far_b, far_b, False, outputs[0])
    prev_far = relay(part_far, -1, 1)
    part_own = grad_input(0, aux_b, h_b, g, True, part_far)
    prev_own = relay(part_own, -1, 0)
    mix_far = mix(y_far, aux_f_far, far_f, False, part_own)
    next_far = relay(mix_far, 1, 1)
    mix_own = mix(y_own, aux_f, h_f, True, mix_far)
    next_own = relay(mix_own, 1, 0)

    def join(a, b):
        return (a.astype(f32) + b.astype(f32)).astype(bf16)

    return (join(next_own, next_far)[None], join(prev_own, prev_far)[None])


def solution(mesh):
    placed = (
        P("section", "ep", None),
        P("section", "ep", None),
        P("section", "ep", None),
        P("section", "ep", None),
        P("section", "ep", None),
        P("section", None),
        P("section", None, None),
        P("section", "ep", None, None),
        P("section", "ep", None, None),
        P("section", "ep", None, None),
    )
    return jax.shard_map(
        step,
        mesh=mesh,
        in_specs=placed,
        out_specs=(P("section", "ep", None), P("section", "ep", None)),
        check_vma=False,
    )
```

profile of v0, /device:TPU:57, one launch (start us, length us, event | category | flops | bytes accessed | tf_op | source)
XLA Modules:
  0.0 267.1 jit_solution(11265755746391821090)
XLA Ops:
  0.6 2.8 %collective-permute-start.1 = (bf16[128,3584]{1,0:T(8,128)(2,1)}, bf16[128,3584]{1,0:T(8,128)(2,1)S(1)}, u32[]{:S(2)}, u32[]{:S(2)}) collective-permute-start(bf16[128,3584]{1,0:T(8,128)(2,1)} %bitcast.19), channel_id=1, source_target_pairs={{0,4},{1,5},{2,6},{3,7},{4,0},{5,1},{6,2},{7,3},{8,12},{9,13},{10,... | collective-permute-start | bytes 2752520 | tf_op jit(solution)/shard_map/ppermute | solution.py:305
  7.2 3.5 %shard_map.113 = (bf16[48,3584]{1,0:T(8,128)(2,1)}, bf16[48,3584]{1,0:T(8,128)(2,1)}, bf16[48,3584]{1,0:T(8,128)(2,1)}, bf16[48,3584]{1,0:T(8,128)(2,1)}, f32[128,128]{1,0:T(8,128)}) custom-call(s32[2]{0:T(128)} %pad_add_fusion.1.place_ref.refs_0_, s32[128,4]{1,0:T(8,128)} %copy.16.ids_ref.refs_1_, bf16[128,3584]{1,0:T(8,128)(2,1)} %bitcast.20, ...), custom_call_target="tpu_custom_call" | custom-call | flops 176160768 | bytes 2490376 | tf_op jit(solution)/shard_map/pallas_call | solution.py:45
  11.9 2.4 collective-permute-start.8
  14.4 2.7 %collective-permute-start = (s32[128,4]{1,0:T(8,128)}, s32[128,4]{1,0:T(8,128)S(1)}, u32[]{:S(2)}, u32[]{:S(2)}) collective-permute-start(s32[128,4]{1,0:T(8,128)} %copy.16.ids_ref.refs_1_), channel_id=1, source_target_pairs={{0,4},{1,5},{2,6},{3,7},{4,0},{5,1},{6,2},{7,3},{8,12},{9,13},{10,... | collective-permute-start | bytes 6152 | tf_op jit(solution)/shard_map/ppermute | solution.py:305
  17.1 27.6 %collective-permute-done.refs_1_ = s32[128,4]{1,0:T(8,128)S(1)} collective-permute-done((s32[128,4]{1,0:T(8,128)}, s32[128,4]{1,0:T(8,128)S(1)}, u32[]{:S(2)}, u32[]{:S(2)}) %collective-permute-start) | collective-permute-done | bytes 2080 | tf_op jit(solution)/shard_map/ppermute | solution.py:305
  44.7 2.7 %collective-permute-start.6 = (bf16[128,3584]{1,0:T(8,128)(2,1)}, bf16[128,3584]{1,0:T(8,128)(2,1)S(1)}, u32[]{:S(2)}, u32[]{:S(2)}) collective-permute-start(bf16[128,3584]{1,0:T(8,128)(2,1)} %bitcast.25), channel_id=1, source_target_pairs={{0,4},{1,5},{2,6},{3,7},{4,0},{5,1},{6,2},{7,3},{8,12},{9,13},{10,... | collective-permute-start | bytes 2752520 | tf_op jit(solution)/shard_map/ppermute | solution.py:305
  47.4 3.0 %shard_map.114 = (bf16[48,3584]{1,0:T(8,128)(2,1)}, bf16[48,3584]{1,0:T(8,128)(2,1)}, bf16[48,3584]{1,0:T(8,128)(2,1)}, bf16[48,3584]{1,0:T(8,128)(2,1)}) custom-call(f32[128,128]{1,0:T(8,128)} %get-tuple-element.47.aux_ref.refs_0_, bf16[128,3584]{1,0:T(8,128)(2,1)} %bitcast.23), custom_call_target="tpu_custom_call" | custom-call | flops 176160768 | bytes 2359296 | tf_op jit(solution)/shard_map/pallas_call | solution.py:45
  50.4 2.5 collective-permute-start.9
  54.9 3.6 %shard_map.115 = (bf16[48,3584]{1,0:T(8,128)(2,1)}, bf16[48,3584]{1,0:T(8,128)(2,1)}, bf16[48,3584]{1,0:T(8,128)(2,1)}, bf16[48,3584]{1,0:T(8,128)(2,1)}, f32[128,128]{1,0:T(8,128)}) custom-call(s32[2]{0:T(128)} %pad_add_fusion.1.place_ref.refs_0_, s32[128,4]{1,0:T(8,128)} %copy-done.18, bf16[128,3584]{1,0:T(8,128)(2,1)} %copy-done, f32[1,3584]{1,0:T(1,128)} %refs_2_.3, ...), custom_call_target="tpu_custom_call" | custom-call | flops 176160768 | bytes 2834440 | tf_op jit(solution)/shard_map/pallas_call | solution.py:45
  60.0 2.7 %collective-permute-done.16.refs_1_ = bf16[48,3584]{1,0:T(8,128)(2,1)S(1)} collective-permute-done((bf16[48,3584]{1,0:T(8,128)(2,1)}, bf16[48,3584]{1,0:T(8,128)(2,1)S(1)}, u32[]{:S(2)}, u32[]{:S(2)}) %collective-permute-start.16) | collective-permute-done | bytes 344096 | tf_op jit(solution)/shard_map/ppermute | solution.py:311
  65.7 2.9 %shard_map.116 = (bf16[48,3584]{1,0:T(8,128)(2,1)}, bf16[48,3584]{1,0:T(8,128)(2,1)}, bf16[48,3584]{1,0:T(8,128)(2,1)}, bf16[48,3584]{1,0:T(8,128)(2,1)}) custom-call(f32[128,128]{1,0:T(8,128)} %get-tuple-element.49.aux_ref.refs_0_, bf16[128,3584]{1,0:T(8,128)(2,1)} %copy-done.8), custom_call_target="tpu_custom_call" | custom-call | flops 176160768 | bytes 2359296 | tf_op jit(solution)/shard_map/pallas_call | solution.py:45
  68.6 3.6 %shard_map.117 = (bf16[48,3584]{1,0:T(8,128)(2,1)}, bf16[48,3584]{1,0:T(8,128)(2,1)}, bf16[48,3584]{1,0:T(8,128)(2,1)}, bf16[48,3584]{1,0:T(8,128)(2,1)}, f32[128,128]{1,0:T(8,128)}) custom-call(s32[2]{0:T(128)} %pad_add_fusion.1.place_ref.refs_0_, s32[128,4]{1,0:T(8,128)} %copy.16.ids_ref.refs_1_, bf16[128,3584]{1,0:T(8,128)(2,1)} %bitcast.26, ...), custom_call_target="tpu_custom_call" | custom-call | flops 176160768 | bytes 2834440 | tf_op jit(solution)/shard_map/pallas_call | solution.py:45
  73.7 5.9 %collective-permute-done.10.refs_5_ = bf16[48,3584]{1,0:T(8,128)(2,1)S(1)} collective-permute-done((bf16[48,3584]{1,0:T(8,128)(2,1)}, bf16[48,3584]{1,0:T(8,128)(2,1)S(1)}, u32[]{:S(2)}, u32[]{:S(2)}) %collective-permute-start.10) | collective-permute-done | bytes 344096 | tf_op jit(solution)/shard_map/ppermute | solution.py:311
  79.7 2.1 collective-permute-start.20
  84.0 11.3 %shard_map.118 = (f32[384,1024]{1,0:T(8,128)}, f32[384,1024]{1,0:T(8,128)}) custom-call(bf16[48,3584]{1,0:T(8,128)(2,1)} %get-tuple-element.56.refs_0_, bf16[48,3584]{1,0:T(8,128)(2,1)} %copy-done.20, bf16[48,3584]{1,0:T(8,128)(2,1)} %copy-done.22, bf16[48,3584]{1,0:T(8,128)(2,1)} %collective-permute-done.9.refs_3_, ...), custom_call_target="tpu_custom_call" | custom-call | flops 5637144576 | bytes 20922368 | tf_op jit(solution)/shard_map/pallas_call | solution.py:45
  95.4 3.6 %shard_map.119 = (bf16[48,3584]{1,0:T(8,128)(2,1)}, bf16[48,3584]{1,0:T(8,128)(2,1)}, bf16[48,3584]{1,0:T(8,128)(2,1)}, bf16[48,3584]{1,0:T(8,128)(2,1)}, f32[128,128]{1,0:T(8,128)}) custom-call(s32[2]{0:T(128)} %pad_add_fusion.1.place_ref.refs_0_, s32[128,4]{1,0:T(8,128)} %copy-done.18, bf16[128,3584]{1,0:T(8,128)(2,1)} %copy-done.2, f32[1,3584]{1,0:T(1,128)} %refs_2_.3, ...), custom_call_target="tpu_custom_call" | custom-call | flops 176160768 | bytes 4063240 | tf_op jit(solution)/shard_map/pallas_call | solution.py:45
  103.6 8.8 %shard_map.120 = (bf16[384,1024]{1,0:T(8,128)(2,1)}, bf16[384,1024]{1,0:T(8,128)(2,1)}, f32[384,128]{1,0:T(8,128)}) custom-call(bf16[48,3584]{1,0:T(8,128)(2,1)} %get-tuple-element.48.refs_5_.refs_0_, bf16[48,3584]{1,0:T(8,128)(2,1)} %copy-done.9, bf16[48,3584]{1,0:T(8,128)(2,1)} %copy-done.10, bf16[48,3584]{1,0:T(8,128)(2,1)} %copy-done.11, ...), custom_call_target="tpu_custom_call" | custom-call | flops 2818572288 | bytes 15351808 | tf_op jit(solution)/shard_map/pallas_call | solution.py:45
  113.9 12.5 %shard_map.121 = (bf16[96,3712]{1,0:T(8,128)(2,1)}, bf16[96,3712]{1,0:T(8,128)(2,1)}, bf16[96,3712]{1,0:T(8,128)(2,1)}, bf16[96,3712]{1,0:T(8,128)(2,1)}) custom-call(bf16[384,1024]{1,0:T(8,128)(2,1)} %get-tuple-element.76.d_gate_ref, bf16[384,1024]{1,0:T(8,128)(2,1)} %get-tuple-element.77.d_up_ref, f32[384,128]{1,0:T(8,128)} %get-tuple-element.78.dot_ref, ...), custom_call_target="tpu_custom_call" | custom-call | flops 5637144576 | bytes 19300352 | tf_op jit(solution)/shard_map/pallas_call | solution.py:45
  129.2 10.8 %shard_map.122.active_ref = bf16[384,1024]{1,0:T(8,128)(2,1)} custom-call(bf16[48,3584]{1,0:T(8,128)(2,1)} %get-tuple-element.52.refs_10_.refs_0_, bf16[48,3584]{1,0:T(8,128)(2,1)} %collective-permute-done.3.refs_1_, bf16[48,3584]{1,0:T(8,128)(2,1)} %copy-done.24, bf16[48,3584]{1,0:T(8,128)(2,1)} %copy-done.25, ...), custom_call_target="tpu_custom_call" | custom-call | flops 5637144576 | bytes 18931712 | tf_op jit(solution)/shard_map/pallas_call | solution.py:45
  140.0 9.0 %shard_map.123 = (bf16[48,3584]{1,0:T(8,128)(2,1)}, bf16[48,3584]{1,0:T(8,128)(2,1)}, bf16[48,3584]{1,0:T(8,128)(2,1)}, bf16[48,3584]{1,0:T(8,128)(2,1)}, bf16[4...) custom-call(bf16[384,1024]{1,0:T(8,128)(2,1)} %shard_map.122.active_ref, ...), custom_call_target="tpu_custom_call" | custom-call | flops 2818572288 | bytes 10878976 | tf_op jit(solution)/shard_map/pallas_call | solution.py:45
  149.0 3.8 %collective-permute-start.25 = (bf16[48,3584]{1,0:T(8,128)(2,1)}, bf16[48,3584]{1,0:T(8,128)(2,1)S(1)}, u32[]{:S(2)}, u32[]{:S(2)}) collective-permute-start(bf16[48,3584]{1,0:T(8,128)(2,1)} %get-tuple-element.86), channel_id=1, source_target_pairs={{0,3},{1,0},{2,1},{3,2},{4,7},{5,4},{6,5},{7,6},{8,11},{9,8},{10,9... | collective-permute-start | bytes 1032200 | tf_op jit(solution)/shard_map/ppermute | solution.py:318
  152.8 8.9 %collective-permute-done.25.refs_2_ = bf16[48,3584]{1,0:T(8,128)(2,1)S(1)} collective-permute-done((bf16[48,3584]{1,0:T(8,128)(2,1)}, bf16[48,3584]{1,0:T(8,128)(2,1)S(1)}, u32[]{:S(2)}, u32[]{:S(2)}) %collective-permute-start.25) | collective-permute-done | bytes 344096 | tf_op jit(solution)/shard_map/ppermute | solution.py:318
  161.7 2.8 %collective-permute-start.22 = (bf16[48,3584]{1,0:T(8,128)(2,1)}, bf16[48,3584]{1,0:T(8,128)(2,1)S(1)}, u32[]{:S(2)}, u32[]{:S(2)}) collective-permute-start(bf16[48,3584]{1,0:T(8,128)(2,1)} %get-tuple-element.81), channel_id=1, source_target_pairs={{0,3},{1,0},{2,1},{3,2},{4,7},{5,4},{6,5},{7,6},{8,11},{9,8},{10,9... | collective-permute-start | bytes 1032200 | tf_op jit(solution)/shard_map/ppermute | solution.py:318
  166.7 4.4 %shard_map.124.refs_9_ = bf16[128,3584]{1,0:T(8,128)(2,1)} custom-call(f32[128,128]{1,0:T(8,128)} %get-tuple-element.49.aux_ref.refs_0_, bf16[128,3584]{1,0:T(8,128)(2,1)} %copy-done, f32[1,3584]{1,0:T(1,128)} %refs_2_.3, bf16[16,3584]{1,0:T(8,128)(2,1)} %pad.4.router_ref.refs_4_.refs_3_, bf16[96,3712]{1,0:T(8,128)(2,1)} %get-tuple-element.79.refs_10_.refs_4_, ...), custom_call_target="tpu_custom_call" | custom-call | flops 352321536 | bytes 6141952 | tf_op jit(solution)/shard_map/pallas_call | solution.py:45
  171.1 4.7 %shard_map.125.refs_6_ = bf16[128,3584]{1,0:T(8,128)(2,1)} custom-call(f32[128,128]{1,0:T(8,128)} %get-tuple-element.47.aux_ref.refs_0_, bf16[128,3584]{1,0:T(8,128)(2,1)} %bitcast.21, f32[1,3584]{1,0:T(1,128)} %refs_2_.3, bf16[16,3584]{1,0:T(8,128)(2,1)} %pad.4.router_ref.refs_4_.refs_3_, bf16[96,3712]{1,0:T(8,128)(2,1)} %get-tuple-element.79.refs_10_.refs_4_, ...), custom_call_target="tpu_custom_call" | custom-call | flops 352321536 | bytes 6715392 | tf_op jit(solution)/shard_map/pallas_call | solution.py:45
  176.5 3.1 %shard_map.126.refs_6_ = bf16[128,3584]{1,0:T(8,128)(2,1)} custom-call(f32[128,128]{1,0:T(8,128)} %get-tuple-element.84.refs_0_, bf16[48,3584]{1,0:T(8,128)(2,1)} %get-tuple-element.85.refs_1_, bf16[48,3584]{1,0:T(8,128)(2,1)} %copy-done.15, bf16[48,3584]{1,0:T(8,128)(2,1)} %copy-done.17, bf16[48,3584]{1,0:T(8,128)(2,1)} %collective-permute-done.27.refs_4_, ...), custom_call_target="tpu_custom_call" | custom-call | flops 352321536 | bytes 4194304 | tf_op jit(solution)/shard_map/pallas_call | solution.py:45
  179.6 3.7 %collective-permute-done.22.refs_2_ = bf16[48,3584]{1,0:T(8,128)(2,1)S(1)} collective-permute-done((bf16[48,3584]{1,0:T(8,128)(2,1)}, bf16[48,3584]{1,0:T(8,128)(2,1)S(1)}, u32[]{:S(2)}, u32[]{:S(2)}) %collective-permute-start.22) | collective-permute-done | bytes 344096 | tf_op jit(solution)/shard_map/ppermute | solution.py:318
  184.0 3.5 %shard_map.127 = bf16[128,3584]{1,0:T(8,128)(2,1)} custom-call(f32[128,128]{1,0:T(8,128)} %get-tuple-element.51.refs_0_, bf16[48,3584]{1,0:T(8,128)(2,1)} %get-tuple-element.80.refs_9_.refs_1_, bf16[48,3584]{1,0:T(8,128)(2,1)} %copy-done.16, bf16[48,3584]{1,0:T(8,128)(2,1)} %collective-permute-done.23.refs_3_, ...), custom_call_target="tpu_custom_call" | custom-call | flops 352321536 | bytes 4194304 | tf_op jit(solution)/shard_map/pallas_call | solution.py:45
  187.5 24.3 %collective-permute-start.31 = (bf16[128,3584]{1,0:T(8,128)(2,1)}, bf16[128,3584]{1,0:T(8,128)(2,1)S(1)}, u32[]{:S(2)}, u32[]{:S(2)}) collective-permute-start(bf16[128,3584]{1,0:T(8,128)(2,1)} %shard_map.127), channel_id=1, source_target_pairs={{0,8},{1,9},{2,10},{3,11},{4,12},{5,13},{6,14},{7,15},{8,16},{9,17... | collective-permute-start | bytes 2752520 | tf_op jit(solution)/shard_map/ppermute | solution.py:323
  211.9 4.0 %collective-permute-start.34 = (bf16[128,3584]{1,0:T(8,128)(2,1)S(1)}, bf16[128,3584]{1,0:T(8,128)(2,1)S(1)}, u32[]{:S(2)}, u32[]{:S(2)}) collective-permute-start(bf16[128,3584]{1,0:T(8,128)(2,1)S(1)} %copy-done.1), channel_id=1, source_target_pairs={{0,124},{1,125},{2,126},{3,127},{4,120},{5,121},{6,122},{7,123},{8... | collective-permute-start | bytes 2752520 | tf_op jit(solution)/shard_map/ppermute | solution.py:323
  215.9 6.6 %collective-permute-done.31 = bf16[128,3584]{1,0:T(8,128)(2,1)S(1)} collective-permute-done((bf16[128,3584]{1,0:T(8,128)(2,1)}, bf16[128,3584]{1,0:T(8,128)(2,1)S(1)}, u32[]{:S(2)}, u32[]{:S(2)}) %collective-permute-start.31) | collective-permute-done | bytes 917536 | tf_op jit(solution)/shard_map/ppermute | solution.py:323
  222.5 42.3 %collective-permute-done.32 = bf16[128,3584]{1,0:T(8,128)(2,1)S(1)} collective-permute-done((bf16[128,3584]{1,0:T(8,128)(2,1)S(1)}, bf16[128,3584]{1,0:T(8,128)(2,1)S(1)}, u32[]{:S(2)}, u32[]{:S(2)}) %collective-permute-start.32) | collective-permute-done | bytes 917536 | tf_op jit(solution)/shard_map/ppermute | solution.py:323
  (117 shorter events, 29.8 us)
Async XLA Ops:
  0.6 52.4 %collective-permute-start.1 = (bf16[128,3584]{1,0:T(8,128)(2,1)}, bf16[128,3584]{1,0:T(8,128)(2,1)S(1)}, u32[]{:S(2)}, u32[]{:S(2)}) collective-permute-start(bf16[128,3584]{1,0:T(8,128)(2,1)} %bitcast.19), channel_id=1, source_target_pairs={{0,4},{1,5},{2,6},{3,7},{4,0},{5,1},{6,2},{7,3},{8,12},{9,13},{10,... | collective-permute-start | bytes 2752520 | tf_op jit(solution)/shard_map/ppermute | solution.py:305
  3.4 61.3 %collective-permute-start.2 = (bf16[128,3584]{1,0:T(8,128)(2,1)}, bf16[128,3584]{1,0:T(8,128)(2,1)S(1)}, u32[]{:S(2)}, u32[]{:S(2)}) collective-permute-start(bf16[128,3584]{1,0:T(8,128)(2,1)} %bitcast.22), channel_id=1, source_target_pairs={{0,4},{1,5},{2,6},{3,7},{4,0},{5,1},{6,2},{7,3},{8,12},{9,13},{10,... | collective-permute-start | bytes 2752520 | tf_op jit(solution)/shard_map/ppermute | solution.py:305
  10.7 39.7 %collective-permute-start.7 = (bf16[48,3584]{1,0:T(8,128)(2,1)}, bf16[48,3584]{1,0:T(8,128)(2,1)S(1)}, u32[]{:S(2)}, u32[]{:S(2)}) collective-permute-start(bf16[48,3584]{1,0:T(8,128)(2,1)} %get-tuple-element.57), channel_id=1, source_target_pairs={{0,1},{1,2},{2,3},{3,0},{4,5},{5,6},{6,7},{7,4},{8,9},{9,10},{10,1... | collective-permute-start | bytes 1032200 | tf_op jit(solution)/shard_map/ppermute | solution.py:311
  11.9 41.0 %collective-permute-start.8 = (bf16[48,3584]{1,0:T(8,128)(2,1)}, bf16[48,3584]{1,0:T(8,128)(2,1)S(1)}, u32[]{:S(2)}, u32[]{:S(2)}) collective-permute-start(bf16[48,3584]{1,0:T(8,128)(2,1)} %get-tuple-element.58), channel_id=1, source_target_pairs={{0,2},{1,3},{2,0},{3,1},{4,6},{5,7},{6,4},{7,5},{8,10},{9,11},{10,... | collective-permute-start | bytes 1032200 | tf_op jit(solution)/shard_map/ppermute | solution.py:311
  14.4 30.3 %collective-permute-start = (s32[128,4]{1,0:T(8,128)}, s32[128,4]{1,0:T(8,128)S(1)}, u32[]{:S(2)}, u32[]{:S(2)}) collective-permute-start(s32[128,4]{1,0:T(8,128)} %copy.16.ids_ref.refs_1_), channel_id=1, source_target_pairs={{0,4},{1,5},{2,6},{3,7},{4,0},{5,1},{6,2},{7,3},{8,12},{9,13},{10,... | collective-permute-start | bytes 6152 | tf_op jit(solution)/shard_map/ppermute | solution.py:305
  44.7 27.8 %collective-permute-start.6 = (bf16[128,3584]{1,0:T(8,128)(2,1)}, bf16[128,3584]{1,0:T(8,128)(2,1)S(1)}, u32[]{:S(2)}, u32[]{:S(2)}) collective-permute-start(bf16[128,3584]{1,0:T(8,128)(2,1)} %bitcast.25), channel_id=1, source_target_pairs={{0,4},{1,5},{2,6},{3,7},{4,0},{5,1},{6,2},{7,3},{8,12},{9,13},{10,... | collective-permute-start | bytes 2752520 | tf_op jit(solution)/shard_map/ppermute | solution.py:305
  53.7 18.5 %collective-permute-start.17 = (bf16[48,3584]{1,0:T(8,128)(2,1)}, bf16[48,3584]{1,0:T(8,128)(2,1)S(1)}, u32[]{:S(2)}, u32[]{:S(2)}) collective-permute-start(bf16[48,3584]{1,0:T(8,128)(2,1)} %get-tuple-element.70), channel_id=1, source_target_pairs={{0,2},{1,3},{2,0},{3,1},{4,6},{5,7},{6,4},{7,5},{8,10},{9,11},{10,... | collective-permute-start | bytes 1032200 | tf_op jit(solution)/shard_map/ppermute | solution.py:311
  59.6 20.0 %collective-permute-start.10 = (bf16[48,3584]{1,0:T(8,128)(2,1)}, bf16[48,3584]{1,0:T(8,128)(2,1)S(1)}, u32[]{:S(2)}, u32[]{:S(2)}) collective-permute-start(bf16[48,3584]{1,0:T(8,128)(2,1)} %get-tuple-element.61), channel_id=1, source_target_pairs={{0,1},{1,2},{2,3},{3,0},{4,5},{5,6},{6,7},{7,4},{8,9},{9,10},{10,1... | collective-permute-start | bytes 1032200 | tf_op jit(solution)/shard_map/ppermute | solution.py:311
  62.7 19.1 %collective-permute-start.11 = (bf16[48,3584]{1,0:T(8,128)(2,1)}, bf16[48,3584]{1,0:T(8,128)(2,1)S(1)}, u32[]{:S(2)}, u32[]{:S(2)}) collective-permute-start(bf16[48,3584]{1,0:T(8,128)(2,1)} %get-tuple-element.62), channel_id=1, source_target_pairs={{0,2},{1,3},{2,0},{3,1},{4,6},{5,7},{6,4},{7,5},{8,10},{9,11},{10,... | collective-permute-start | bytes 1032200 | tf_op jit(solution)/shard_map/ppermute | solution.py:311
  64.7 17.8 %collective-permute-start.12 = (bf16[48,3584]{1,0:T(8,128)(2,1)}, bf16[48,3584]{1,0:T(8,128)(2,1)}, u32[]{:S(2)}, u32[]{:S(2)}) collective-permute-start(bf16[48,3584]{1,0:T(8,128)(2,1)} %get-tuple-element.63), channel_id=1, source_target_pairs={{0,3},{1,0},{2,1},{3,2},{4,7},{5,4},{6,5},{7,6},{8,11},{9,8},{10,9... | collective-permute-start | bytes 1032200 | tf_op jit(solution)/shard_map/ppermute | solution.py:311
  72.2 26.8 %collective-permute-start.18 = (bf16[48,3584]{1,0:T(8,128)(2,1)}, bf16[48,3584]{1,0:T(8,128)(2,1)S(1)}, u32[]{:S(2)}, u32[]{:S(2)}) collective-permute-start(bf16[48,3584]{1,0:T(8,128)(2,1)} %get-tuple-element.71), channel_id=1, source_target_pairs={{0,3},{1,0},{2,1},{3,2},{4,7},{5,4},{6,5},{7,6},{8,11},{9,8},{10,9... | collective-permute-start | bytes 1032200 | tf_op jit(solution)/shard_map/ppermute | solution.py:311
  72.5 27.4 %collective-permute-start.19 = (bf16[48,3584]{1,0:T(8,128)(2,1)}, bf16[48,3584]{1,0:T(8,128)(2,1)S(1)}, u32[]{:S(2)}, u32[]{:S(2)}) collective-permute-start(bf16[48,3584]{1,0:T(8,128)(2,1)} %get-tuple-element.72), channel_id=1, source_target_pairs={{0,1},{1,2},{2,3},{3,0},{4,5},{5,6},{6,7},{7,4},{8,9},{9,10},{10,1... | collective-permute-start | bytes 1032200 | tf_op jit(solution)/shard_map/ppermute | solution.py:311
  79.7 21.9 %collective-permute-start.20 = (bf16[48,3584]{1,0:T(8,128)(2,1)}, bf16[48,3584]{1,0:T(8,128)(2,1)S(1)}, u32[]{:S(2)}, u32[]{:S(2)}) collective-permute-start(bf16[48,3584]{1,0:T(8,128)(2,1)} %get-tuple-element.73), channel_id=1, source_target_pairs={{0,2},{1,3},{2,0},{3,1},{4,6},{5,7},{6,4},{7,5},{8,10},{9,11},{10,... | collective-permute-start | bytes 1032200 | tf_op jit(solution)/shard_map/ppermute | solution.py:311
  82.5 19.1 %collective-permute-start.21 = (bf16[48,3584]{1,0:T(8,128)(2,1)}, bf16[48,3584]{1,0:T(8,128)(2,1)S(1)}, u32[]{:S(2)}, u32[]{:S(2)}) collective-permute-start(bf16[48,3584]{1,0:T(8,128)(2,1)} %get-tuple-element.74), channel_id=1, source_target_pairs={{0,3},{1,0},{2,1},{3,2},{4,7},{5,4},{6,5},{7,6},{8,11},{9,8},{10,9... | collective-permute-start | bytes 1032200 | tf_op jit(solution)/shard_map/ppermute | solution.py:311
  82.5 29.9 %collective-permute-start.3 = (bf16[48,3584]{1,0:T(8,128)(2,1)}, bf16[48,3584]{1,0:T(8,128)(2,1)}, u32[]{:S(2)}, u32[]{:S(2)}) collective-permute-start(bf16[48,3584]{1,0:T(8,128)(2,1)} %get-tuple-element.53), channel_id=1, source_target_pairs={{0,1},{1,2},{2,3},{3,0},{4,5},{5,6},{6,7},{7,4},{8,9},{9,10},{10,1... | collective-permute-start | bytes 1032200 | tf_op jit(solution)/shard_map/ppermute | solution.py:311
  99.0 27.4 %collective-permute-start.4 = (bf16[48,3584]{1,0:T(8,128)(2,1)S(1)}, bf16[48,3584]{1,0:T(8,128)(2,1)S(1)}, u32[]{:S(2)}, u32[]{:S(2)}) collective-permute-start(bf16[48,3584]{1,0:T(8,128)(2,1)S(1)} %copy-done.21), channel_id=1, source_target_pairs={{0,2},{1,3},{2,0},{3,1},{4,6},{5,7},{6,4},{7,5},{8,10},{9,11},{10,... | collective-permute-start | bytes 1032200 | tf_op jit(solution)/shard_map/ppermute | solution.py:311
  99.9 26.6 %collective-permute-start.5 = (bf16[48,3584]{1,0:T(8,128)(2,1)S(1)}, bf16[48,3584]{1,0:T(8,128)(2,1)S(1)}, u32[]{:S(2)}, u32[]{:S(2)}) collective-permute-start(bf16[48,3584]{1,0:T(8,128)(2,1)S(1)} %copy-done.19), channel_id=1, source_target_pairs={{0,3},{1,0},{2,1},{3,2},{4,7},{5,4},{6,5},{7,6},{8,11},{9,8},{10,9... | collective-permute-start | bytes 1032200 | tf_op jit(solution)/shard_map/ppermute | solution.py:311
  101.6 26.8 %collective-permute-start.13 = (bf16[48,3584]{1,0:T(8,128)(2,1)}, bf16[48,3584]{1,0:T(8,128)(2,1)S(1)}, u32[]{:S(2)}, u32[]{:S(2)}) collective-permute-start(bf16[48,3584]{1,0:T(8,128)(2,1)} %get-tuple-element.66), channel_id=1, source_target_pairs={{0,1},{1,2},{2,3},{3,0},{4,5},{5,6},{6,7},{7,4},{8,9},{9,10},{10,1... | collective-permute-start | bytes 1032200 | tf_op jit(solution)/shard_map/ppermute | solution.py:311
  101.6 27.4 %collective-permute-start.14 = (bf16[48,3584]{1,0:T(8,128)(2,1)}, bf16[48,3584]{1,0:T(8,128)(2,1)}, u32[]{:S(2)}, u32[]{:S(2)}) collective-permute-start(bf16[48,3584]{1,0:T(8,128)(2,1)} %get-tuple-element.67), channel_id=1, source_target_pairs={{0,2},{1,3},{2,0},{3,1},{4,6},{5,7},{6,4},{7,5},{8,10},{9,11},{10,... | collective-permute-start | bytes 1032200 | tf_op jit(solution)/shard_map/ppermute | solution.py:311
  112.5 16.6 %collective-permute-start.15 = (bf16[48,3584]{1,0:T(8,128)(2,1)S(1)}, bf16[48,3584]{1,0:T(8,128)(2,1)}, u32[]{:S(2)}, u32[]{:S(2)}) collective-permute-start(bf16[48,3584]{1,0:T(8,128)(2,1)S(1)} %copy-done.23), channel_id=1, source_target_pairs={{0,3},{1,0},{2,1},{3,2},{4,7},{5,4},{6,5},{7,6},{8,11},{9,8},{10,9... | collective-permute-start | bytes 1032200 | tf_op jit(solution)/shard_map/ppermute | solution.py:311
  126.4 35.3 %collective-permute-start.28 = (bf16[96,3712]{1,0:T(8,128)(2,1)}, bf16[96,3712]{1,0:T(8,128)(2,1)S(1)}, u32[]{:S(2)}, u32[]{:S(2)}) collective-permute-start(bf16[96,3712]{1,0:T(8,128)(2,1)} %get-tuple-element.89), channel_id=1, source_target_pairs={{0,3},{1,0},{2,1},{3,2},{4,7},{5,4},{6,5},{7,6},{8,11},{9,8},{10,9... | collective-permute-start | bytes 2138120 | tf_op jit(solution)/shard_map/ppermute | solution.py:318
  126.5 38.1 %collective-permute-start.29 = (bf16[96,3712]{1,0:T(8,128)(2,1)}, bf16[96,3712]{1,0:T(8,128)(2,1)S(1)}, u32[]{:S(2)}, u32[]{:S(2)}) collective-permute-start(bf16[96,3712]{1,0:T(8,128)(2,1)} %get-tuple-element.90), channel_id=1, source_target_pairs={{0,2},{1,3},{2,0},{3,1},{4,6},{5,7},{6,4},{7,5},{8,10},{9,11},{10,... | collective-permute-start | bytes 2138120 | tf_op jit(solution)/shard_map/ppermute | solution.py:318
  128.4 37.4 %collective-permute-start.30 = (bf16[96,3712]{1,0:T(8,128)(2,1)}, bf16[96,3712]{1,0:T(8,128)(2,1)S(1)}, u32[]{:S(2)}, u32[]{:S(2)}) collective-permute-start(bf16[96,3712]{1,0:T(8,128)(2,1)} %get-tuple-element.91), channel_id=1, source_target_pairs={{0,1},{1,2},{2,3},{3,0},{4,5},{5,6},{6,7},{7,4},{8,9},{9,10},{10,1... | collective-permute-start | bytes 2138120 | tf_op jit(solution)/shard_map/ppermute | solution.py:318
  152.8 23.0 %collective-permute-start.26 = (bf16[48,3584]{1,0:T(8,128)(2,1)}, bf16[48,3584]{1,0:T(8,128)(2,1)S(1)}, u32[]{:S(2)}, u32[]{:S(2)}) collective-permute-start(bf16[48,3584]{1,0:T(8,128)(2,1)} %get-tuple-element.87), channel_id=1, source_target_pairs={{0,2},{1,3},{2,0},{3,1},{4,6},{5,7},{6,4},{7,5},{8,10},{9,11},{10,... | collective-permute-start | bytes 1032200 | tf_op jit(solution)/shard_map/ppermute | solution.py:318
  161.7 14.1 %collective-permute-start.27 = (bf16[48,3584]{1,0:T(8,128)(2,1)}, bf16[48,3584]{1,0:T(8,128)(2,1)}, u32[]{:S(2)}, u32[]{:S(2)}) collective-permute-start(bf16[48,3584]{1,0:T(8,128)(2,1)} %get-tuple-element.88), channel_id=1, source_target_pairs={{0,1},{1,2},{2,3},{3,0},{4,5},{5,6},{6,7},{7,4},{8,9},{9,10},{10,1... | collective-permute-start | bytes 1032200 | tf_op jit(solution)/shard_map/ppermute | solution.py:318
  161.7 21.5 %collective-permute-start.22 = (bf16[48,3584]{1,0:T(8,128)(2,1)}, bf16[48,3584]{1,0:T(8,128)(2,1)S(1)}, u32[]{:S(2)}, u32[]{:S(2)}) collective-permute-start(bf16[48,3584]{1,0:T(8,128)(2,1)} %get-tuple-element.81), channel_id=1, source_target_pairs={{0,3},{1,0},{2,1},{3,2},{4,7},{5,4},{6,5},{7,6},{8,11},{9,8},{10,9... | collective-permute-start | bytes 1032200 | tf_op jit(solution)/shard_map/ppermute | solution.py:318
  164.6 18.7 %collective-permute-start.23 = (bf16[48,3584]{1,0:T(8,128)(2,1)}, bf16[48,3584]{1,0:T(8,128)(2,1)}, u32[]{:S(2)}, u32[]{:S(2)}) collective-permute-start(bf16[48,3584]{1,0:T(8,128)(2,1)} %get-tuple-element.82), channel_id=1, source_target_pairs={{0,2},{1,3},{2,0},{3,1},{4,6},{5,7},{6,4},{7,5},{8,10},{9,11},{10,... | collective-permute-start | bytes 1032200 | tf_op jit(solution)/shard_map/ppermute | solution.py:318
  165.8 17.5 %collective-permute-start.24 = (bf16[48,3584]{1,0:T(8,128)(2,1)}, bf16[48,3584]{1,0:T(8,128)(2,1)}, u32[]{:S(2)}, u32[]{:S(2)}) collective-permute-start(bf16[48,3584]{1,0:T(8,128)(2,1)} %get-tuple-element.83), channel_id=1, source_target_pairs={{0,1},{1,2},{2,3},{3,0},{4,5},{5,6},{6,7},{7,4},{8,9},{9,10},{10,1... | collective-permute-start | bytes 1032200 | tf_op jit(solution)/shard_map/ppermute | solution.py:318
  187.5 35.0 %collective-permute-start.31 = (bf16[128,3584]{1,0:T(8,128)(2,1)}, bf16[128,3584]{1,0:T(8,128)(2,1)S(1)}, u32[]{:S(2)}, u32[]{:S(2)}) collective-permute-start(bf16[128,3584]{1,0:T(8,128)(2,1)} %shard_map.127), channel_id=1, source_target_pairs={{0,8},{1,9},{2,10},{3,11},{4,12},{5,13},{6,14},{7,15},{8,16},{9,17... | collective-permute-start | bytes 2752520 | tf_op jit(solution)/shard_map/ppermute | solution.py:323
  211.8 53.0 %collective-permute-start.32 = (bf16[128,3584]{1,0:T(8,128)(2,1)S(1)}, bf16[128,3584]{1,0:T(8,128)(2,1)S(1)}, u32[]{:S(2)}, u32[]{:S(2)}) collective-permute-start(bf16[128,3584]{1,0:T(8,128)(2,1)S(1)} %copy-done.4), channel_id=1, source_target_pairs={{0,12},{1,13},{2,14},{3,15},{4,8},{5,9},{6,10},{7,11},{8,20},{9,21... | collective-permute-start | bytes 2752520 | tf_op jit(solution)/shard_map/ppermute | solution.py:323
  211.8 54.1 %collective-permute-start.33 = (bf16[128,3584]{1,0:T(8,128)(2,1)S(1)}, bf16[128,3584]{1,0:T(8,128)(2,1)S(1)}, u32[]{:S(2)}, u32[]{:S(2)}) collective-permute-start(bf16[128,3584]{1,0:T(8,128)(2,1)S(1)} %copy-done.3), channel_id=1, source_target_pairs={{0,120},{1,121},{2,122},{3,123},{4,124},{5,125},{6,126},{7,127},{8... | collective-permute-start | bytes 2752520 | tf_op jit(solution)/shard_map/ppermute | solution.py:323
  211.9 54.1 %collective-permute-start.34 = (bf16[128,3584]{1,0:T(8,128)(2,1)S(1)}, bf16[128,3584]{1,0:T(8,128)(2,1)S(1)}, u32[]{:S(2)}, u32[]{:S(2)}) collective-permute-start(bf16[128,3584]{1,0:T(8,128)(2,1)S(1)} %copy-done.1), channel_id=1, source_target_pairs={{0,124},{1,125},{2,126},{3,127},{4,120},{5,121},{6,122},{7,123},{8... | collective-permute-start | bytes 2752520 | tf_op jit(solution)/shard_map/ppermute | solution.py:323
  (32 other events, 272.9 us)
where the time goes:
time: 268 us; the launch traced here: 267 us
  waiting for transfers between devices  99 us (37%)
  Pallas kernels  88.4 us (33%)
  starting transfers between devices  69 us (26%)
  local copies, waits for them, and re-layouts  6.26 us (2%)
  other arithmetic  3.56 us (1%)
    pallas_call x15, Pallas kernels, call(): pl.pallas_call(body, out_shape=outs, scratch_shapes=list(scratch), cost_e...  88.4 us
    ppermute x4, waiting for transfers between devices, relay(): lax.ppermute(block, ('section', 'ep'), relay_route(lax.axis_size('section...  48.9 us
    ppermute x4, starting transfers between devices, relay(): lax.ppermute(block, ('section', 'ep'), relay_route(lax.axis_size('section...  28.4 us
    ppermute x4, waiting for transfers between devices, across(): return lax.ppermute(block, 'ep', ep_route(1, 0))  27.6 us
    ppermute x18, starting transfers between devices, spread(): moved[dx] = lax.ppermute(pieces[dx], 'ep', ep_route(0, dx))  20.9 us
    ppermute x9, waiting for transfers between devices, collect(): moved[dx] = lax.ppermute(pieces[dx], 'ep', ep_route(0, -dx))  12.6 us
    ppermute x9, starting transfers between devices, collect(): moved[dx] = lax.ppermute(pieces[dx], 'ep', ep_route(0, -dx))  11.2 us
    ppermute x18, waiting for transfers between devices, spread(): moved[dx] = lax.ppermute(pieces[dx], 'ep', ep_route(0, dx))  9.84 us
  transfers between devices with their start and end apart: 35, of which 8 were waited for; matrix products, arithmetic and copies ran while one was open for 2% of the time, Pallas kernels for 32%

commit v1 on v0

v1 whole, which is shorter than its diff:
```python
import functools
import jax
import jax.numpy as jnp
from jax import lax
from jax.experimental import pallas as pl
from jax.experimental.pallas import tpu as pltpu
from jax.sharding import PartitionSpec as P


NORM_EPSILON = 1e-06
ROUTE_SCALE = 2.5

T = 128
D = 3584
F = 1024
CAP = 48
NX = 4
NZ = 2
EXPERTS = NX * NZ
ROWS = NX * NZ * CAP
TF = 512
TB = 1792
TD = 512
EXT = 128
f32 = jnp.float32
bf16 = jnp.bfloat16
NT = (((1,), (1,)), ((), ()))


def call(body, outs, ins, grid=None, in_specs=None, out_specs=None, scratch=(), flops=0, after=None):
    kwargs = {}
    if after is not None:
        inner, count = body, len(ins)
        ins = (*ins, after)
        in_specs = [*in_specs, pl.BlockSpec(memory_space=pl.ANY)]

        def body(*refs):
            inner(*refs[:count], *refs[count + 1 :])

    if grid is not None:
        kwargs["grid"] = grid
    if in_specs is not None:
        kwargs["in_specs"] = in_specs
    if out_specs is not None:
        kwargs["out_specs"] = out_specs
    moved = sum(a.size * a.dtype.itemsize for a in ins) + sum(o.size * o.dtype.itemsize for o in outs)
    return pl.pallas_call(
        body,
        out_shape=outs,
        scratch_shapes=list(scratch),
        cost_estimate=pl.CostEstimate(flops=int(flops), bytes_accessed=int(moved), transcendentals=0),
        **kwargs,
    )(*ins)


def vspec(shape, index=None):
    fixed = index if index is not None else (0,) * len(shape)
    return pl.BlockSpec(shape, lambda *_: fixed)


def chip():
    return pl.BlockSpec(memory_space=pltpu.VMEM)


def sspec():
    return pl.BlockSpec(memory_space=pltpu.SMEM)


def shape(*dims, dtype=bf16):
    return jax.ShapeDtypeStruct(dims, dtype)


def each_tile(body, start=0):
    carry = start
    for n in range(D // TD):
        carry = body(slice(n * TD, (n + 1) * TD), carry)
    return carry


def rows_iota(count):
    return lax.broadcasted_iota(jnp.int32, (count, T), 0)


def slots_of(named, place_ref):
    half, column = place_ref[0] >> 2, place_ref[0] & (NX - 1)
    expert = rows_iota(16)
    member = jnp.where((expert == named[0]) | (expert == named[1]), 1.0, 0.0).astype(bf16)
    before = jnp.where(rows_iota(T) < lax.broadcasted_iota(jnp.int32, (T, T), 1), 1.0, 0.0).astype(bf16)
    rank = jnp.dot(member, before, preferred_element_type=f32)
    slots = []
    for name in named:
        own_rank = jnp.sum(jnp.where(expert == name, rank, 0.0), axis=0, keepdims=True)
        step = ((name - column) & (NX - 1)).astype(f32)
        slots.append(jnp.where((name >> 2) == half, step * CAP + own_rank, -1.0))
    return slots


def hits_of(slots, count):
    slot = rows_iota(count).astype(f32)
    return [slot == own for own in slots]


def pack(slots, row_tile, outs, weights=None):
    hits = hits_of(slots, NX * CAP)
    chosen = jnp.where(hits[0] | hits[1], 1.0, 0.0).astype(bf16)
    if weights is not None:
        scale = jnp.where(hits[0], weights[0], 0.0) + jnp.where(hits[1], weights[1], 0.0)
        scale = ROUTE_SCALE * jnp.sum(scale, axis=1, keepdims=True)

    def tile(cols, carry):
        picked = jnp.dot(chosen, row_tile(cols), preferred_element_type=f32)
        if weights is not None:
            picked = scale * picked
        picked = picked.astype(bf16)
        for step in range(NX):
            outs[step][:, cols] = picked[step * CAP : (step + 1) * CAP]
        return carry

    each_tile(tile)


def prep_grad_body(aux_ref, rows_ref, *outs):
    aux = aux_ref[...]
    pack([aux[0:1], aux[1:2]], lambda cols: rows_ref[:, cols], outs, [aux[2:3], aux[3:4]])


def inverse_of(rows_ref):
    def tile(cols, total):
        values = rows_ref[:, cols].astype(f32)
        return total + jnp.sum(values * values, axis=1, keepdims=True)

    return lax.rsqrt(each_tile(tile, jnp.zeros((T, 1), f32)) / D + NORM_EPSILON)


def prep_norm_body(place_ref, ids_ref, rows_ref, gain_ref, router_ref, *refs):
    outs, aux_ref, normed_ref = refs[:NX], refs[NX], refs[NX + 1]
    named = [ids_ref[k : k + 1, :] for k in range(2)]
    slots = slots_of(named, place_ref)
    inverse = inverse_of(rows_ref)

    def tile(cols, carry):
        normed_ref[:, cols] = (rows_ref[:, cols].astype(f32) * inverse * gain_ref[:, cols]).astype(bf16)
        return carry

    each_tile(tile)
    pack(slots, lambda cols: normed_ref[:, cols], outs)
    logits = lax.dot_general(router_ref[...], normed_ref[...], NT, preferred_element_type=f32)
    scores = jax.nn.sigmoid(logits)
    expert = rows_iota(EXPERTS)
    picked = [jnp.sum(jnp.where(expert == name, scores, 0.0), axis=0, keepdims=True) for name in named]
    both = picked[0] + picked[1]
    lines = slots + [p / both for p in picked] + picked + [name.astype(f32) for name in named]
    for i, line in enumerate(lines):
        aux_ref[i : i + 1, :] = line


def fetch(copies):
    for copy in copies:
        copy.start()
    return copies


def finish(copies):
    for copy in copies:
        copy.wait()


def row_copies(pieces, rows_ref, sems):
    starts = [(i % NX * NZ + i // NX) * CAP for i in range(8)]
    return [
        pltpu.make_async_copy(piece, rows_ref.at[pl.ds(at, CAP), :], sems.at[i])
        for i, (piece, at) in enumerate(zip(pieces, starts))
    ]


def row_copy(source, target, sems, i):
    size = target.shape[1]
    rows = pl.ds(pl.multiple_of(i * size, size), size)
    return pltpu.make_async_copy(source.at[rows, :], target.at[i], sems.at[i])


def put_rows(outs, cols, rows):
    for step in range(NX):
        for z in range(NZ):
            at = (step * NZ + z) * CAP
            outs[z * NX + step][:, cols] = rows[at : at + CAP]


def strip_of(i):
    return pl.ds(pl.multiple_of(i * TF, TF), TF)


def lift_body(*refs):
    pieces, gate_ref, up_ref, a_ref, b_ref = refs[:8], refs[8], refs[9], refs[10], refs[11]
    rows_ref, gate, up, row_sems, gate_sem, up_sem = refs[12:]
    rows_in = fetch(row_copies(pieces, rows_ref, row_sems))
    gate_in = pltpu.make_async_copy(gate_ref, gate, gate_sem)
    up_in = pltpu.make_async_copy(up_ref, up, up_sem)
    gate_in.start()
    finish(rows_in)
    up_in.start()
    for weights, copy, out_ref in ((gate, gate_in, a_ref), (up, up_in, b_ref)):
        copy.wait()

        def strip(i, carry):
            out_ref[i] = jnp.dot(rows_ref[...], weights[:, strip_of(i)], preferred_element_type=f32)
            return carry

        lax.fori_loop(0, F // TF, strip, 0)


def back_body(*refs):
    pieces, down_ref, a_hbm, b_hbm, gate_ref, up_ref = refs[:8], refs[8], refs[9], refs[10], refs[11], refs[12]
    outs = refs[13:21]
    rows_ref, down, a_ref, b_ref, lifts, d_lift_ref, dot_ref = refs[21:28]
    row_sems, down_sems, a_sems, b_sems, gate_sems, up_sems = refs[28:]
    rows_in = fetch(row_copies(pieces, rows_ref, row_sems))

    def act_copies(i):
        return [
            row_copy(down_ref, down, down_sems, i),
            pltpu.make_async_copy(a_hbm.at[i], a_ref.at[i], a_sems.at[i]),
            pltpu.make_async_copy(b_hbm.at[i], b_ref.at[i], b_sems.at[i]),
        ]

    def back_copies(i):
        rows = pl.ds(pl.multiple_of(i * TB, TB), TB)
        return [
            pltpu.make_async_copy(gate_ref.at[rows, :], lifts.at[i, :, :F], gate_sems.at[i]),
            pltpu.make_async_copy(up_ref.at[rows, :], lifts.at[i, :, F:], up_sems.at[i]),
        ]

    for i in range(F // TF):
        fetch(act_copies(i))
    dot_ref[...] = jnp.zeros_like(dot_ref)
    finish(rows_in)

    def strip(i, carry):
        finish(act_copies(i))

        fetch(back_copies(i))
        d_act = lax.dot_general(rows_ref[...], down[i], NT, preferred_element_type=f32)
        a, b = a_ref[i], b_ref[i]
        s = jax.nn.sigmoid(a)
        both = (a * s * b).astype(bf16).astype(f32) * d_act
        dot_ref[...] += sum(both[:, n : n + 128] for n in range(0, TF, 128))
        d_lift_ref[:, strip_of(i)] = (d_act * b * s * (1.0 + a * (1.0 - s))).astype(bf16)
        d_lift_ref[:, pl.ds(pl.multiple_of(F + i * TF, TF), TF)] = (d_act * a * s).astype(bf16)
        return carry

    lax.fori_loop(0, F // TF, strip, 0)
    dots = jnp.sum(dot_ref[...], axis=1, keepdims=True)
    high = dots.astype(bf16).astype(f32)
    lane = lax.broadcasted_iota(jnp.int32, (ROWS, EXT), 1)
    extra = jnp.where(lane == 0, high, jnp.where(lane == 1, dots - high, 0.0)).astype(bf16)
    put_rows(outs, slice(D, D + EXT), extra)

    def tile(i, carry):
        finish(back_copies(i))
        back = lax.dot_general(d_lift_ref[...], lifts[i], NT, preferred_element_type=f32)
        put_rows(outs, pl.ds(pl.multiple_of(i * TB, TB), TB), back.astype(bf16))
        return carry

    lax.fori_loop(0, D // TB, tile, 0)


def forward_body(*refs):
    pieces, gate_ref, up_ref, down_ref = refs[:8], refs[8], refs[9], refs[10]
    outs = refs[11:19]
    rows_ref, gate, up, down, a_ref, active_ref, row_sems, gate_sem, up_sem, down_sem = refs[19:]
    rows_in = fetch(row_copies(pieces, rows_ref, row_sems))
    gate_in = pltpu.make_async_copy(gate_ref, gate, gate_sem)
    up_in = pltpu.make_async_copy(up_ref, up, up_sem)
    down_in = pltpu.make_async_copy(down_ref, down, down_sem)
    gate_in.start()
    finish(rows_in)
    up_in.start()
    gate_in.wait()
    down_in.start()

    def gate_strip(i, carry):
        a_ref[i] = jnp.dot(rows_ref[...], gate[:, strip_of(i)], preferred_element_type=f32)
        return carry

    lax.fori_loop(0, F // TF, gate_strip, 0)
    up_in.wait()

    def up_strip(i, carry):
        a = a_ref[i]
        b = jnp.dot(rows_ref[...], up[:, strip_of(i)], preferred_element_type=f32)
        active_ref[:, strip_of(i)] = (a * jax.nn.sigmoid(a) * b).astype(bf16)
        return carry

    lax.fori_loop(0, F // TF, up_strip, 0)
    down_in.wait()

    def tile(i, carry):
        cols = pl.ds(pl.multiple_of(i * TB, TB), TB)
        put_rows(outs, cols, jnp.dot(active_ref[...], down[:, cols], preferred_element_type=f32).astype(bf16))
        return carry

    lax.fori_loop(0, D // TB, tile, 0)


def split_weights(values):
    high = values.astype(bf16)
    return high, (values - high.astype(f32)).astype(bf16)


def stack_pieces(pieces, rows_ref):
    for step in range(NX):
        rows_ref[step * CAP : (step + 1) * CAP, :] = pieces[step][...]
    rows_ref[NX * CAP :, :] = jnp.zeros((256 - NX * CAP, rows_ref.shape[1]), bf16)


def mix_body(with_input, aux_ref, *refs):
    pieces, base_ref, out_ref, rows_ref = refs[:NX], refs[NX], refs[NX + 1], refs[NX + 2]
    stack_pieces(pieces, rows_ref)
    aux = aux_ref[...]
    hits = hits_of([aux[0:1], aux[1:2]], 256)
    weights = jnp.where(hits[0], aux[2:3], 0.0) + jnp.where(hits[1], aux[3:4], 0.0)
    high, low = split_weights(jnp.transpose(ROUTE_SCALE * weights))

    def tile(cols, carry):
        rows = rows_ref[:, cols]
        total = jnp.dot(high, rows, preferred_element_type=f32) + jnp.dot(low, rows, preferred_element_type=f32)
        if with_input:
            total = total + base_ref[:, cols].astype(f32)
        out_ref[:, cols] = total.astype(bf16)
        return carry

    each_tile(tile)


def grad_input_body(with_input, aux_ref, hidden_ref, gain_ref, router_ref, *refs):
    pieces, base_ref, out_ref, rows_ref, scaled_ref = refs[:NX], refs[NX], refs[NX + 1], refs[NX + 2], refs[NX + 3]
    stack_pieces(pieces, rows_ref)
    aux = aux_ref[...]
    hits = [jnp.where(hit, 1.0, 0.0) for hit in hits_of([aux[0:1], aux[1:2]], 256)]
    extra = jnp.transpose(rows_ref[:, D:].astype(f32))[:16].astype(bf16)
    pulls = []
    for hit in hits:
        found = jnp.dot(extra, hit.astype(bf16), preferred_element_type=f32)
        pulls.append(found[0:1] + found[1:2])
    route = router_ref[...]
    rows_ref[NX * CAP : NX * CAP + 16, :D] = jnp.concatenate([route, route], axis=0)
    slot = rows_iota(256)
    high = jnp.zeros((256, T), f32)
    low = jnp.zeros((256, T), f32)
    for k in range(2):
        weight, score, name = aux[2 + k : 3 + k], aux[4 + k : 5 + k], aux[6 + k : 7 + k].astype(jnp.int32)
        term = (pulls[k] - weight * (pulls[0] + pulls[1])) * (1.0 - score)
        first = term.astype(bf16).astype(f32)
        high = high + jnp.where(slot == name + NX * CAP, first, 0.0)
        low = low + jnp.where(slot == name + NX * CAP + EXPERTS, term - first, 0.0)
    mixing = jnp.transpose(hits[0] + hits[1] + high + low).astype(bf16)
    inverse = inverse_of(hidden_ref)

    def scale_tile(cols, against):
        scaled = jnp.dot(mixing, rows_ref[:, cols], preferred_element_type=f32) * gain_ref[:, cols]
        scaled_ref[:, cols] = scaled
        return against + jnp.sum(scaled * hidden_ref[:, cols].astype(f32), axis=1, keepdims=True)

    against = each_tile(scale_tile, jnp.zeros((T, 1), f32))
    pull = inverse * inverse * inverse * against / D

    def out_tile(cols, carry):
        out = inverse * scaled_ref[:, cols] - hidden_ref[:, cols].astype(f32) * pull
        if with_input:
            out = out + base_ref[:, cols].astype(f32)
        out_ref[:, cols] = out.astype(bf16)
        return carry

    each_tile(out_tile)


def ep_route(dz, dx):
    route = []
    for i in range(NZ * NX):
        z, x = divmod(i, NX)
        route.append((i, ((z + dz) % NZ) * NX + (x + dx) % NX))
    return route


def relay_route(sections, ds, dz):
    route = []
    for s in range(sections):
        for i in range(NZ * NX):
            z, x = divmod(i, NX)
            route.append((s * NZ * NX + i, ((s + ds) % sections) * NZ * NX + ((z + dz) % NZ) * NX + x))
    return route


def across(block):
    return lax.ppermute(block, "ep", ep_route(1, 0))


def spread(pieces):
    moved = list(pieces)
    for dx in (1, 3, 2):
        moved[dx] = lax.ppermute(pieces[dx], "ep", ep_route(0, dx))
    return moved


def collect(pieces):
    moved = list(pieces)
    for dx in (1, 3, 2):
        moved[dx] = lax.ppermute(pieces[dx], "ep", ep_route(0, -dx))
    return moved


def relay(block, ds, dz):
    return lax.ppermute(block, ("section", "ep"), relay_route(lax.axis_size("section"), ds, dz))


def step(
    fwd_input, bwd_input, bwd_grad, fwd_ids, bwd_ids, norm_gain, router, gate_w, up_w, down_w
):
    h_f, h_b, g = fwd_input[0], bwd_input[0], bwd_grad[0]
    gate, up, down = gate_w[0, 0], up_w[0, 0], down_w[0, 0]
    router_t = router[0].T
    ids_b, ids_f = bwd_ids[0].T, fwd_ids[0].T
    place = lax.axis_index("ep").astype(jnp.int32)[None]

    far_ids_b = across(ids_b)
    far_b = across(h_b)
    far_g = across(g)
    far_ids_f = across(ids_f)
    far_f = across(h_f)

    packed = [shape(CAP, D)] * NX
    aux_shape = shape(EXPERTS, T, dtype=f32)
    full = vspec((T, D))
    aux_spec = chip()
    piece_specs = [chip()] * NX
    pack_flops = 2 * NX * CAP * T * D

    def prep_grad(where, rows, aux, after=None):
        return call(
            prep_grad_body, packed, (aux, rows), grid=(1,), in_specs=[aux_spec, chip() if where == "far" else full], out_specs=piece_specs,
            flops=pack_flops, after=after,
        )

    def prep_norm(where, rows, ids, after=None):
        outs = call(
            prep_norm_body, packed + [aux_shape],
            (place, ids, rows, norm_gain, router_t), grid=(1,),
            in_specs=[sspec(), chip(), chip() if "far" in where else full, vspec((1, D)), vspec((EXPERTS, D))],
            out_specs=piece_specs + [aux_spec], scratch=[pltpu.VMEM((T, D), bf16)],
            flops=pack_flops, after=after,
        )
        return outs[:NX], outs[NX]

    packed_b, aux_b = prep_norm("b_own", h_b, ids_b)
    b_own = spread(packed_b)
    packed_g = prep_grad("own", g, aux_b)
    g_own = spread(packed_g)
    packed_bf, aux_b_far = prep_norm("b_far", far_b, far_ids_b, packed_g[0])
    b_far = spread(packed_bf)
    packed_f, aux_f = prep_norm("f_own", h_f, ids_f, packed_bf[0])
    packed_gf = prep_grad("far", far_g, aux_b_far, packed_f[0])
    g_far = spread(packed_gf)
    f_own = spread(packed_f)

    whole = pl.BlockSpec(memory_space=pl.ANY)
    rows_vmem = pltpu.VMEM((ROWS, D), bf16)
    lift_vmem, down_vmem = pltpu.VMEM((D, F), bf16), pltpu.VMEM((F, D), bf16)
    one = pltpu.SemaphoreType.DMA
    act_vmem = pltpu.VMEM((ROWS, F), bf16)
    act_f32_vmem = pltpu.VMEM((F // TF, ROWS, TF), f32)
    mat_flops = 2 * ROWS * D * F

    def sems(count):
        return pltpu.SemaphoreType.DMA((count,))

    def expert(body, outs, pieces, matrices, scratch, flops, after):
        return call(
            body, outs, (*pieces, *matrices), in_specs=[whole] * (8 + len(matrices)),
            out_specs=[chip()] * len(outs), scratch=scratch, flops=flops, after=after,
        )

    a, b = expert(
        lift_body, [shape(F // TF, ROWS, TF, dtype=f32)] * 2, (*b_own, *b_far), (gate, up),
        [rows_vmem, lift_vmem, lift_vmem, sems(8), one, one], 2 * mat_flops, packed_gf[0],
    )
    packed_ff, aux_f_far = prep_norm("f_far", far_f, far_ids_f, a)
    f_far = spread(packed_ff)
    returned = expert(
        back_body, [shape(CAP, D + EXT)] * 8, (*g_own, *g_far), (down, a, b, gate, up),
        [rows_vmem, pltpu.VMEM((F // TF, TF, D), bf16), act_f32_vmem, act_f32_vmem]
        + [pltpu.VMEM((D // TB, TB, 2 * F), bf16), pltpu.VMEM((ROWS, 2 * F), bf16), pltpu.VMEM((ROWS, 128), f32)]
        + [sems(8)] + [sems(F // TF)] * 3 + [sems(D // TB)] * 2, 3 * mat_flops, packed_ff[0],
    )
    back_far = collect(returned[NX:])
    back_own = collect(returned[:NX])
    outputs = expert(
        forward_body, [shape(CAP, D)] * 8, (*f_own, *f_far), (gate, up, down),
        [rows_vmem, lift_vmem, lift_vmem, down_vmem, act_f32_vmem, act_vmem, sems(8), one, one, one],
        3 * mat_flops, returned[0],
    )
    y_far = collect(outputs[NX:])
    y_own = collect(outputs[:NX])

    def mix(pieces, aux, base, with_input, after):
        return call(
            functools.partial(mix_body, with_input), [shape(T, D)], (aux, *pieces, base), grid=(1,),
            in_specs=[aux_spec] + piece_specs + [full if with_input else vspec((16, D))],
            out_specs=[full], scratch=[pltpu.VMEM((256, D), bf16)], flops=2 * pack_flops, after=after,
        )[0]

    def grad_input(pieces, aux, hidden, base, with_input, after):
        return call(
            functools.partial(grad_input_body, with_input), [shape(T, D)],
            (aux, hidden, norm_gain, router_t, *pieces, base), grid=(1,),
            in_specs=[aux_spec, full, vspec((1, D)), vspec((EXPERTS, D))] + piece_specs
            + [full if with_input else vspec((16, D))],
            out_specs=[full], scratch=[pltpu.VMEM((256, D + EXT), bf16), pltpu.VMEM((T, D), f32)],
            flops=2 * pack_flops, after=after,
        )[0]

    part_far = grad_input(back_far, aux_b_far, far_b, far_b, False, outputs[0])
    prev_far = relay(part_far, -1, 1)
    part_own = grad_input(back_own, aux_b, h_b, g, True, part_far)
    prev_own = relay(part_own, -1, 0)
    mix_far = mix(y_far, aux_f_far, far_f, False, part_own)
    next_far = relay(mix_far, 1, 1)
    mix_own = mix(y_own, aux_f, h_f, True, mix_far)
    next_own = relay(mix_own, 1, 0)

    def join(a, b):
        return (a.astype(f32) + b.astype(f32)).astype(bf16)

    return (join(next_own, next_far)[None], join(prev_own, prev_far)[None])


def solution(mesh):
    placed = (
        P("section", "ep", None),
        P("section", "ep", None),
        P("section", "ep", None),
        P("section", "ep", None),
        P("section", "ep", None),
        P("section", None),
        P("section", None, None),
        P("section", "ep", None, None),
        P("section", "ep", None, None),
        P("section", "ep", None, None),
    )
    return jax.shard_map(
        step,
        mesh=mesh,
        in_specs=placed,
        out_specs=(P("section", "ep", None), P("section", "ep", None)),
        check_vma=False,
    )
```

time: 268 us -> 290 us (1.082)
  the two profiles are of different devices: /device:TPU:57 before, /device:TPU:0 now
where the time goes in v1:
time: 290 us; the launch traced here: 288 us
  waiting for transfers between devices  147 us (51%)
  Pallas kernels  74.6 us (26%)
  starting transfers between devices  59.5 us (21%)
  other arithmetic  3.44 us (1%)
    pallas_call x13, Pallas kernels, call(): pl.pallas_call(body, out_shape=outs, scratch_shapes=list(scratch), cost_e...  74.6 us
    ppermute x5, waiting for transfers between devices, across(): return lax.ppermute(block, 'ep', ep_route(1, 0))  53.7 us
    ppermute x18, waiting for transfers between devices, spread(): moved[dx] = lax.ppermute(pieces[dx], 'ep', ep_route(0, dx))  41.6 us
    ppermute x12, waiting for transfers between devices, collect(): moved[dx] = lax.ppermute(pieces[dx], 'ep', ep_route(0, -dx))  34.6 us
    ppermute x18, starting transfers between devices, spread(): moved[dx] = lax.ppermute(pieces[dx], 'ep', ep_route(0, dx))  26.4 us
    ppermute x4, waiting for transfers between devices, relay(): lax.ppermute(block, ('section', 'ep'), relay_route(lax.axis_size('section...  16.9 us
    ppermute x12, starting transfers between devices, collect(): moved[dx] = lax.ppermute(pieces[dx], 'ep', ep_route(0, -dx))  16.5 us
    ppermute x5, starting transfers between devices, across(): return lax.ppermute(block, 'ep', ep_route(1, 0))  10.9 us
  transfers between devices with their start and end apart: 39, of which 18 were waited for; matrix products, arithmetic and copies ran while one was open for 0% of the time, Pallas kernels for 25%

profile of v1, /device:TPU:0, one launch (start us, length us, event | category | flops | bytes accessed | tf_op | source)
XLA Modules:
  0.0 287.6 jit_solution(16704329580731169066)
XLA Ops:
  0.6 4.1 %collective-permute-start.1 = (bf16[128,3584]{1,0:T(8,128)(2,1)}, bf16[128,3584]{1,0:T(8,128)(2,1)S(1)}, u32[]{:S(2)}, u32[]{:S(2)}) collective-permute-start(bf16[128,3584]{1,0:T(8,128)(2,1)} %bitcast.23), channel_id=1, source_target_pairs={{0,4},{1,5},{2,6},{3,7},{4,0},{5,1},{6,2},{7,3},{8,12},{9,13},{10,... | collective-permute-start | bytes 2752520 | tf_op jit(solution)/shard_map/ppermute | solution.py:395
  4.8 3.2 %shard_map.113 = (bf16[48,3584]{1,0:T(8,128)(2,1)}, bf16[48,3584]{1,0:T(8,128)(2,1)}, bf16[48,3584]{1,0:T(8,128)(2,1)}, bf16[48,3584]{1,0:T(8,128)(2,1)}, f32[8,128]{1,0:T(8,128)}) custom-call(s32[1]{0:T(128)} %bitcast.place_ref.refs_0_, s32[2,128]{1,0:T(2,128)} %bitcast.35, bf16[128,3584]{1,0:T(8,128)(2,1)} %bitcast.24, f32[1,3584]{1,0:T(1,128)} %refs_2_.3, ...), custom_call_target="tpu_custom_call" | custom-call | flops 176160768 | bytes 2370564 | tf_op jit(solution)/shard_map/pallas_call | solution.py:47
  9.5 3.4 %collective-permute-start.6 = (bf16[128,3584]{1,0:T(8,128)(2,1)}, bf16[128,3584]{1,0:T(8,128)(2,1)S(1)}, u32[]{:S(2)}, u32[]{:S(2)}) collective-permute-start(bf16[128,3584]{1,0:T(8,128)(2,1)} %bitcast.26), channel_id=1, source_target_pairs={{0,4},{1,5},{2,6},{3,7},{4,0},{5,1},{6,2},{7,3},{8,12},{9,13},{10,... | collective-permute-start | bytes 2752520 | tf_op jit(solution)/shard_map/ppermute | solution.py:395
  13.0 51.6 %collective-permute-done.5.refs_1_ = s32[2,128]{1,0:T(2,128)S(1)} collective-permute-done((s32[2,128]{1,0:T(2,128)}, s32[2,128]{1,0:T(2,128)S(1)}, u32[]{:S(2)}, u32[]{:S(2)}) %collective-permute-start.5) | collective-permute-done | bytes 1056 | tf_op jit(solution)/shard_map/ppermute | solution.py:395
  64.6 3.2 %collective-permute-start = (s32[2,128]{1,0:T(2,128)}, s32[2,128]{1,0:T(2,128)S(1)}, u32[]{:S(2)}, u32[]{:S(2)}) collective-permute-start(s32[2,128]{1,0:T(2,128)} %bitcast.36), channel_id=1, source_target_pairs={{0,4},{1,5},{2,6},{3,7},{4,0},{5,1},{6,2},{7,3},{8,12},{9,13},{10,... | collective-permute-start | bytes 3080 | tf_op jit(solution)/shard_map/ppermute | solution.py:395
  69.9 3.0 %collective-permute-start.8 = (bf16[48,3584]{1,0:T(8,128)(2,1)}, bf16[48,3584]{1,0:T(8,128)(2,1)}, u32[]{:S(2)}, u32[]{:S(2)}) collective-permute-start(bf16[48,3584]{1,0:T(8,128)(2,1)} %get-tuple-element.58), channel_id=1, source_target_pairs={{0,2},{1,3},{2,0},{3,1},{4,6},{5,7},{6,4},{7,5},{8,10},{9,11},{10,... | collective-permute-start | bytes 1032200 | tf_op jit(solution)/shard_map/ppermute | solution.py:401
  74.1 2.7 shard_map.114
  77.8 3.2 %shard_map.115 = (bf16[48,3584]{1,0:T(8,128)(2,1)}, bf16[48,3584]{1,0:T(8,128)(2,1)}, bf16[48,3584]{1,0:T(8,128)(2,1)}, bf16[48,3584]{1,0:T(8,128)(2,1)}, f32[8,128]{1,0:T(8,128)}) custom-call(s32[1]{0:T(128)} %bitcast.place_ref.refs_0_, s32[2,128]{1,0:T(2,128)} %copy-done.13, bf16[128,3584]{1,0:T(8,128)(2,1)} %copy-done, f32[1,3584]{1,0:T(1,128)} %refs_2_.3, ...), custom_call_target="tpu_custom_call" | custom-call | flops 176160768 | bytes 2714628 | tf_op jit(solution)/shard_map/pallas_call | solution.py:47
  84.2 3.1 %collective-permute-done.9.refs_3_ = bf16[48,3584]{1,0:T(8,128)(2,1)} collective-permute-done((bf16[48,3584]{1,0:T(8,128)(2,1)}, bf16[48,3584]{1,0:T(8,128)(2,1)}, u32[]{:S(2)}, u32[]{:S(2)}) %collective-permute-start.9) | collective-permute-done | bytes 344096 | tf_op jit(solution)/shard_map/ppermute | solution.py:401
  91.3 3.2 %shard_map.116 = (bf16[48,3584]{1,0:T(8,128)(2,1)}, bf16[48,3584]{1,0:T(8,128)(2,1)}, bf16[48,3584]{1,0:T(8,128)(2,1)}, bf16[48,3584]{1,0:T(8,128)(2,1)}, f32[8,128]{1,0:T(8,128)}) custom-call(s32[1]{0:T(128)} %bitcast.place_ref.refs_0_, s32[2,128]{1,0:T(2,128)} %bitcast.38, bf16[128,3584]{1,0:T(8,128)(2,1)} %bitcast.27, f32[1,3584]{1,0:T(1,128)} %refs_2_.3, ...), custom_call_target="tpu_custom_call" | custom-call | flops 176160768 | bytes 2714628 | tf_op jit(solution)/shard_map/pallas_call | solution.py:47
  94.6 2.7 shard_map.117
  100.2 10.4 %collective-permute-done.10.refs_5_ = bf16[48,3584]{1,0:T(8,128)(2,1)} collective-permute-done((bf16[48,3584]{1,0:T(8,128)(2,1)}, bf16[48,3584]{1,0:T(8,128)(2,1)}, u32[]{:S(2)}, u32[]{:S(2)}) %collective-permute-start.10) | collective-permute-done | bytes 344096 | tf_op jit(solution)/shard_map/ppermute | solution.py:401
  114.0 11.5 %shard_map.118 = (f32[2,384,512]{2,1,0:T(8,128)}, f32[2,384,512]{2,1,0:T(8,128)}) custom-call(bf16[48,3584]{1,0:T(8,128)(2,1)} %get-tuple-element.56.refs_0_, bf16[48,3584]{1,0:T(8,128)(2,1)} %copy-done.18, bf16[48,3584]{1,0:T(8,128)(2,1)} %collective-permute-done.8.refs_2_, bf16[48,3584]{1,0:T(8,128)(2,1)} %collective-permute-done.9.refs_3_, ...), custom_call_target="tpu_custom_call" | custom-call | flops 5637144576 | bytes 20922368 | tf_op jit(solution)/shard_map/pallas_call | solution.py:47
  125.6 3.3 %shard_map.119 = (bf16[48,3584]{1,0:T(8,128)(2,1)}, bf16[48,3584]{1,0:T(8,128)(2,1)}, bf16[48,3584]{1,0:T(8,128)(2,1)}, bf16[48,3584]{1,0:T(8,128)(2,1)}, f32[8,128]{1,0:T(8,128)}) custom-call(s32[1]{0:T(128)} %bitcast.place_ref.refs_0_, s32[2,128]{1,0:T(2,128)} %copy-done.12, bf16[128,3584]{1,0:T(8,128)(2,1)} %copy-done.1, f32[1,3584]{1,0:T(1,128)} %refs_2_.3, ...), custom_call_target="tpu_custom_call" | custom-call | flops 176160768 | bytes 3943428 | tf_op jit(solution)/shard_map/pallas_call | solution.py:47
  131.8 5.2 %collective-permute-done.22.refs_7_ = bf16[48,3584]{1,0:T(8,128)(2,1)} collective-permute-done((bf16[48,3584]{1,0:T(8,128)(2,1)}, bf16[48,3584]{1,0:T(8,128)(2,1)}, u32[]{:S(2)}, u32[]{:S(2)}) %collective-permute-start.22) | collective-permute-done | bytes 344096 | tf_op jit(solution)/shard_map/ppermute | solution.py:401
  137.0 15.6 %shard_map.120 = (bf16[48,3712]{1,0:T(8,128)(2,1)}, bf16[48,3712]{1,0:T(8,128)(2,1)}, bf16[48,3712]{1,0:T(8,128)(2,1)}, bf16[48,3712]{1,0:T(8,128)(2,1)}, bf16[4...) custom-call(bf16[48,3584]{1,0:T(8,128)(2,1)} %get-tuple-element.49.refs_5_.r, ...), custom_call_target="tpu_custom_call" | custom-call | flops 8455716864 | bytes 31113216 | tf_op jit(solution)/shard_map/pallas_call | solution.py:47
  159.9 18.7 %collective-permute-done.4.refs_3_ = bf16[48,3584]{1,0:T(8,128)(2,1)S(1)} collective-permute-done((bf16[48,3584]{1,0:T(8,128)(2,1)S(1)}, bf16[48,3584]{1,0:T(8,128)(2,1)S(1)}, u32[]{:S(2)}, u32[]{:S(2)}) %collective-permute-start.4) | collective-permute-done | bytes 344096 | tf_op jit(solution)/shard_map/ppermute | solution.py:401
  178.6 3.8 %collective-permute-start.29 = (bf16[48,3712]{1,0:T(8,128)(2,1)}, bf16[48,3712]{1,0:T(8,128)(2,1)S(1)}, u32[]{:S(2)}, u32[]{:S(2)}) collective-permute-start(bf16[48,3712]{1,0:T(8,128)(2,1)} %get-tuple-element.87), channel_id=1, source_target_pairs={{0,3},{1,0},{2,1},{3,2},{4,7},{5,4},{6,5},{7,6},{8,11},{9,8},{10,9... | collective-permute-start | bytes 1069064 | tf_op jit(solution)/shard_map/ppermute | solution.py:408
  183.4 2.8 collective-permute-done.16.refs_7_
  188.3 2.7 collective-permute-start.34
  191.0 15.1 %shard_map.121 = (bf16[48,3584]{1,0:T(8,128)(2,1)}, bf16[48,3584]{1,0:T(8,128)(2,1)}, bf16[48,3584]{1,0:T(8,128)(2,1)}, bf16[48,3584]{1,0:T(8,128)(2,1)}, bf16[4...) custom-call(bf16[48,3584]{1,0:T(8,128)(2,1)} %get-tuple-element.52.refs_2_.r, ...), custom_call_target="tpu_custom_call" | custom-call | flops 8455716864 | bytes 27881472 | tf_op jit(solution)/shard_map/pallas_call | solution.py:47
  206.1 4.1 %collective-permute-done.33.refs_6_ = bf16[48,3712]{1,0:T(8,128)(2,1)S(1)} collective-permute-done((bf16[48,3712]{1,0:T(8,128)(2,1)}, bf16[48,3712]{1,0:T(8,128)(2,1)S(1)}, u32[]{:S(2)}, u32[]{:S(2)}) %collective-permute-start.33) | collective-permute-done | bytes 356384 | tf_op jit(solution)/shard_map/ppermute | solution.py:408
  210.1 3.5 %collective-permute-done.34.refs_7_ = bf16[48,3712]{1,0:T(8,128)(2,1)S(1)} collective-permute-done((bf16[48,3712]{1,0:T(8,128)(2,1)}, bf16[48,3712]{1,0:T(8,128)(2,1)S(1)}, u32[]{:S(2)}, u32[]{:S(2)}) %collective-permute-start.34) | collective-permute-done | bytes 356384 | tf_op jit(solution)/shard_map/ppermute | solution.py:408
  214.4 3.8 %shard_map.122.refs_9_ = bf16[128,3584]{1,0:T(8,128)(2,1)} custom-call(f32[8,128]{1,0:T(8,128)} %get-tuple-element.63.refs_0_, bf16[128,3584]{1,0:T(8,128)(2,1)} %copy-done, f32[1,3584]{1,0:T(1,128)} %refs_2_.3, bf16[8,3584]{1,0:T(8,128)(2,1)} %bitcast.33, bf16[48,3712]{1,0:T(8,128)(2,1)} %get-tuple-element.90.refs_4_, bf16[48,3712]{1,0:T(8,128)(2,1)} %copy-done.4, ...), custom_call_target="tpu_custom_call" | custom-call | flops 352321536 | bytes 4597760 | tf_op jit(solution)/shard_map/pallas_call | solution.py:47
  219.7 4.1 %shard_map.123.refs_6_ = bf16[128,3584]{1,0:T(8,128)(2,1)} custom-call(f32[8,128]{1,0:T(8,128)} %get-tuple-element.48.aux_ref.refs_0_, bf16[128,3584]{1,0:T(8,128)(2,1)} %bitcast.25, f32[1,3584]{1,0:T(1,128)} %refs_2_.3, bf16[8,3584]{1,0:T(8,128)(2,1)} %bitcast.34, bf16[48,3712]{1,0:T(8,128)(2,1)} %get-tuple-element.77.refs_11_.refs_4_, ...), custom_call_target="tpu_custom_call" | custom-call | flops 352321536 | bytes 5171200 | tf_op jit(solution)/shard_map/pallas_call | solution.py:47
  226.4 3.1 %collective-permute-start.38 = (bf16[128,3584]{1,0:T(8,128)(2,1)S(1)}, bf16[128,3584]{1,0:T(8,128)(2,1)S(1)}, u32[]{:S(2)}, u32[]{:S(2)}) collective-permute-start(bf16[128,3584]{1,0:T(8,128)(2,1)S(1)} %copy-done.2), channel_id=1, source_target_pairs={{0,124},{1,125},{2,126},{3,127},{4,120},{5,121},{6,122},{7,123},{8... | collective-permute-start | bytes 2752520 | tf_op jit(solution)/shard_map/ppermute | solution.py:413
  231.6 8.9 %collective-permute-done.26.refs_2_ = bf16[48,3584]{1,0:T(8,128)(2,1)S(1)} collective-permute-done((bf16[48,3584]{1,0:T(8,128)(2,1)S(1)}, bf16[48,3584]{1,0:T(8,128)(2,1)S(1)}, u32[]{:S(2)}, u32[]{:S(2)}) %collective-permute-start.26) | collective-permute-done | bytes 344096 | tf_op jit(solution)/shard_map/ppermute | solution.py:408
  243.4 7.0 %collective-permute-done.28.refs_4_ = bf16[48,3584]{1,0:T(8,128)(2,1)} collective-permute-done((bf16[48,3584]{1,0:T(8,128)(2,1)}, bf16[48,3584]{1,0:T(8,128)(2,1)}, u32[]{:S(2)}, u32[]{:S(2)}) %collective-permute-start.28) | collective-permute-done | bytes 344096 | tf_op jit(solution)/shard_map/ppermute | solution.py:408
  251.5 3.0 %shard_map.124.refs_6_ = bf16[128,3584]{1,0:T(8,128)(2,1)} custom-call(f32[8,128]{1,0:T(8,128)} %get-tuple-element.82.refs_0_, bf16[48,3584]{1,0:T(8,128)(2,1)} %get-tuple-element.83.refs_1_, bf16[48,3584]{1,0:T(8,128)(2,1)} %copy-done.11, bf16[48,3584]{1,0:T(8,128)(2,1)} %collective-permute-done.27.refs_3_, ...), custom_call_target="tpu_custom_call" | custom-call | flops 352321536 | bytes 4132864 | tf_op jit(solution)/shard_map/pallas_call | solution.py:47
  257.9 6.2 %collective-permute-done.25.refs_4_ = bf16[48,3584]{1,0:T(8,128)(2,1)} collective-permute-done((bf16[48,3584]{1,0:T(8,128)(2,1)}, bf16[48,3584]{1,0:T(8,128)(2,1)}, u32[]{:S(2)}, u32[]{:S(2)}) %collective-permute-start.25) | collective-permute-done | bytes 344096 | tf_op jit(solution)/shard_map/ppermute | solution.py:408
  264.1 3.2 %shard_map.125 = bf16[128,3584]{1,0:T(8,128)(2,1)} custom-call(f32[8,128]{1,0:T(8,128)} %get-tuple-element.51.refs_0_, bf16[48,3584]{1,0:T(8,128)(2,1)} %get-tuple-element.78.refs_9_.refs_1_, bf16[48,3584]{1,0:T(8,128)(2,1)} %copy-done.10, bf16[48,3584]{1,0:T(8,128)(2,1)} %collective-permute-done.24.refs_3_, ...), custom_call_target="tpu_custom_call" | custom-call | flops 352321536 | bytes 4132864 | tf_op jit(solution)/shard_map/pallas_call | solution.py:47
  268.4 15.6 %collective-permute-done.35 = bf16[128,3584]{1,0:T(8,128)(2,1)S(1)} collective-permute-done((bf16[128,3584]{1,0:T(8,128)(2,1)}, bf16[128,3584]{1,0:T(8,128)(2,1)S(1)}, u32[]{:S(2)}, u32[]{:S(2)}) %collective-permute-start.35) | collective-permute-done | bytes 917536 | tf_op jit(solution)/shard_map/ppermute | solution.py:413
  (123 shorter events, 51.7 us)
Async XLA Ops:
  0.6 76.2 %collective-permute-start.1 = (bf16[128,3584]{1,0:T(8,128)(2,1)}, bf16[128,3584]{1,0:T(8,128)(2,1)S(1)}, u32[]{:S(2)}, u32[]{:S(2)}) collective-permute-start(bf16[128,3584]{1,0:T(8,128)(2,1)} %bitcast.23), channel_id=1, source_target_pairs={{0,4},{1,5},{2,6},{3,7},{4,0},{5,1},{6,2},{7,3},{8,12},{9,13},{10,... | collective-permute-start | bytes 2752520 | tf_op jit(solution)/shard_map/ppermute | solution.py:395
  4.7 84.6 %collective-permute-start.13 = (bf16[128,3584]{1,0:T(8,128)(2,1)}, bf16[128,3584]{1,0:T(8,128)(2,1)S(1)}, u32[]{:S(2)}, u32[]{:S(2)}) collective-permute-start(bf16[128,3584]{1,0:T(8,128)(2,1)} %bitcast.20), channel_id=1, source_target_pairs={{0,4},{1,5},{2,6},{3,7},{4,0},{5,1},{6,2},{7,3},{8,12},{9,13},{10,... | collective-permute-start | bytes 2752520 | tf_op jit(solution)/shard_map/ppermute | solution.py:395
  8.0 65.0 %collective-permute-start.7 = (bf16[48,3584]{1,0:T(8,128)(2,1)}, bf16[48,3584]{1,0:T(8,128)(2,1)S(1)}, u32[]{:S(2)}, u32[]{:S(2)}) collective-permute-start(bf16[48,3584]{1,0:T(8,128)(2,1)} %get-tuple-element.57), channel_id=1, source_target_pairs={{0,1},{1,2},{2,3},{3,0},{4,5},{5,6},{6,7},{7,4},{8,9},{9,10},{10,1... | collective-permute-start | bytes 1032200 | tf_op jit(solution)/shard_map/ppermute | solution.py:401
  9.5 89.5 %collective-permute-start.6 = (bf16[128,3584]{1,0:T(8,128)(2,1)}, bf16[128,3584]{1,0:T(8,128)(2,1)S(1)}, u32[]{:S(2)}, u32[]{:S(2)}) collective-permute-start(bf16[128,3584]{1,0:T(8,128)(2,1)} %bitcast.26), channel_id=1, source_target_pairs={{0,4},{1,5},{2,6},{3,7},{4,0},{5,1},{6,2},{7,3},{8,12},{9,13},{10,... | collective-permute-start | bytes 2752520 | tf_op jit(solution)/shard_map/ppermute | solution.py:395
  12.9 51.7 %collective-permute-start.5 = (s32[2,128]{1,0:T(2,128)}, s32[2,128]{1,0:T(2,128)S(1)}, u32[]{:S(2)}, u32[]{:S(2)}) collective-permute-start(s32[2,128]{1,0:T(2,128)} %bitcast.37), channel_id=1, source_target_pairs={{0,4},{1,5},{2,6},{3,7},{4,0},{5,1},{6,2},{7,3},{8,12},{9,13},{10,... | collective-permute-start | bytes 3080 | tf_op jit(solution)/shard_map/ppermute | solution.py:395
  76.9 20.5 %collective-permute-start.17 = (bf16[48,3584]{1,0:T(8,128)(2,1)}, bf16[48,3584]{1,0:T(8,128)(2,1)S(1)}, u32[]{:S(2)}, u32[]{:S(2)}) collective-permute-start(bf16[48,3584]{1,0:T(8,128)(2,1)} %get-tuple-element.70), channel_id=1, source_target_pairs={{0,1},{1,2},{2,3},{3,0},{4,5},{5,6},{6,7},{7,4},{8,9},{9,10},{10,1... | collective-permute-start | bytes 1032200 | tf_op jit(solution)/shard_map/ppermute | solution.py:401
  82.4 28.1 %collective-permute-start.10 = (bf16[48,3584]{1,0:T(8,128)(2,1)}, bf16[48,3584]{1,0:T(8,128)(2,1)}, u32[]{:S(2)}, u32[]{:S(2)}) collective-permute-start(bf16[48,3584]{1,0:T(8,128)(2,1)} %get-tuple-element.60), channel_id=1, source_target_pairs={{0,1},{1,2},{2,3},{3,0},{4,5},{5,6},{6,7},{7,4},{8,9},{9,10},{10,1... | collective-permute-start | bytes 1032200 | tf_op jit(solution)/shard_map/ppermute | solution.py:401
  87.3 23.3 %collective-permute-start.11 = (bf16[48,3584]{1,0:T(8,128)(2,1)}, bf16[48,3584]{1,0:T(8,128)(2,1)}, u32[]{:S(2)}, u32[]{:S(2)}) collective-permute-start(bf16[48,3584]{1,0:T(8,128)(2,1)} %get-tuple-element.61), channel_id=1, source_target_pairs={{0,2},{1,3},{2,0},{3,1},{4,6},{5,7},{6,4},{7,5},{8,10},{9,11},{10,... | collective-permute-start | bytes 1032200 | tf_op jit(solution)/shard_map/ppermute | solution.py:401
  89.3 22.1 %collective-permute-start.12 = (bf16[48,3584]{1,0:T(8,128)(2,1)}, bf16[48,3584]{1,0:T(8,128)(2,1)}, u32[]{:S(2)}, u32[]{:S(2)}) collective-permute-start(bf16[48,3584]{1,0:T(8,128)(2,1)} %get-tuple-element.62), channel_id=1, source_target_pairs={{0,3},{1,0},{2,1},{3,2},{4,7},{5,4},{6,5},{7,6},{8,11},{9,8},{10,9... | collective-permute-start | bytes 1032200 | tf_op jit(solution)/shard_map/ppermute | solution.py:401
  97.3 31.6 %collective-permute-start.18 = (bf16[48,3584]{1,0:T(8,128)(2,1)S(1)}, bf16[48,3584]{1,0:T(8,128)(2,1)S(1)}, u32[]{:S(2)}, u32[]{:S(2)}) collective-permute-start(bf16[48,3584]{1,0:T(8,128)(2,1)S(1)} %copy-done.21), channel_id=1, source_target_pairs={{0,2},{1,3},{2,0},{3,1},{4,6},{5,7},{6,4},{7,5},{8,10},{9,11},{10,... | collective-permute-start | bytes 1032200 | tf_op jit(solution)/shard_map/ppermute | solution.py:401
  98.9 30.7 %collective-permute-start.19 = (bf16[48,3584]{1,0:T(8,128)(2,1)S(1)}, bf16[48,3584]{1,0:T(8,128)(2,1)}, u32[]{:S(2)}, u32[]{:S(2)}) collective-permute-start(bf16[48,3584]{1,0:T(8,128)(2,1)S(1)} %copy-done.19), channel_id=1, source_target_pairs={{0,3},{1,0},{2,1},{3,2},{4,7},{5,4},{6,5},{7,6},{8,11},{9,8},{10,9... | collective-permute-start | bytes 1032200 | tf_op jit(solution)/shard_map/ppermute | solution.py:401
  110.6 21.2 %collective-permute-start.20 = (bf16[48,3584]{1,0:T(8,128)(2,1)}, bf16[48,3584]{1,0:T(8,128)(2,1)}, u32[]{:S(2)}, u32[]{:S(2)}) collective-permute-start(bf16[48,3584]{1,0:T(8,128)(2,1)} %get-tuple-element.73), channel_id=1, source_target_pairs={{0,1},{1,2},{2,3},{3,0},{4,5},{5,6},{6,7},{7,4},{8,9},{9,10},{10,1... | collective-permute-start | bytes 1032200 | tf_op jit(solution)/shard_map/ppermute | solution.py:401
  110.6 21.2 %collective-permute-start.21 = (bf16[48,3584]{1,0:T(8,128)(2,1)}, bf16[48,3584]{1,0:T(8,128)(2,1)}, u32[]{:S(2)}, u32[]{:S(2)}) collective-permute-start(bf16[48,3584]{1,0:T(8,128)(2,1)} %get-tuple-element.74), channel_id=1, source_target_pairs={{0,2},{1,3},{2,0},{3,1},{4,6},{5,7},{6,4},{7,5},{8,10},{9,11},{10,... | collective-permute-start | bytes 1032200 | tf_op jit(solution)/shard_map/ppermute | solution.py:401
  111.4 25.6 %collective-permute-start.22 = (bf16[48,3584]{1,0:T(8,128)(2,1)}, bf16[48,3584]{1,0:T(8,128)(2,1)}, u32[]{:S(2)}, u32[]{:S(2)}) collective-permute-start(bf16[48,3584]{1,0:T(8,128)(2,1)} %get-tuple-element.75), channel_id=1, source_target_pairs={{0,3},{1,0},{2,1},{3,2},{4,7},{5,4},{6,5},{7,6},{8,11},{9,8},{10,9... | collective-permute-start | bytes 1032200 | tf_op jit(solution)/shard_map/ppermute | solution.py:401
  128.9 28.2 %collective-permute-start.2 = (bf16[48,3584]{1,0:T(8,128)(2,1)S(1)}, bf16[48,3584]{1,0:T(8,128)(2,1)S(1)}, u32[]{:S(2)}, u32[]{:S(2)}) collective-permute-start(bf16[48,3584]{1,0:T(8,128)(2,1)S(1)} %copy-done.17), channel_id=1, source_target_pairs={{0,1},{1,2},{2,3},{3,0},{4,5},{5,6},{6,7},{7,4},{8,9},{9,10},{10,1... | collective-permute-start | bytes 1032200 | tf_op jit(solution)/shard_map/ppermute | solution.py:401
  129.6 28.4 %collective-permute-start.3 = (bf16[48,3584]{1,0:T(8,128)(2,1)S(1)}, bf16[48,3584]{1,0:T(8,128)(2,1)S(1)}, u32[]{:S(2)}, u32[]{:S(2)}) collective-permute-start(bf16[48,3584]{1,0:T(8,128)(2,1)S(1)} %copy-done.16), channel_id=1, source_target_pairs={{0,2},{1,3},{2,0},{3,1},{4,6},{5,7},{6,4},{7,5},{8,10},{9,11},{10,... | collective-permute-start | bytes 1032200 | tf_op jit(solution)/shard_map/ppermute | solution.py:401
  152.6 35.7 %collective-permute-start.32 = (bf16[48,3712]{1,0:T(8,128)(2,1)}, bf16[48,3712]{1,0:T(8,128)(2,1)S(1)}, u32[]{:S(2)}, u32[]{:S(2)}) collective-permute-start(bf16[48,3712]{1,0:T(8,128)(2,1)} %get-tuple-element.91), channel_id=1, source_target_pairs={{0,3},{1,0},{2,1},{3,2},{4,7},{5,4},{6,5},{7,6},{8,11},{9,8},{10,9... | collective-permute-start | bytes 1069064 | tf_op jit(solution)/shard_map/ppermute | solution.py:408
  155.1 23.5 %collective-permute-start.4 = (bf16[48,3584]{1,0:T(8,128)(2,1)S(1)}, bf16[48,3584]{1,0:T(8,128)(2,1)S(1)}, u32[]{:S(2)}, u32[]{:S(2)}) collective-permute-start(bf16[48,3584]{1,0:T(8,128)(2,1)S(1)} %copy-done.14), channel_id=1, source_target_pairs={{0,3},{1,0},{2,1},{3,2},{4,7},{5,4},{6,5},{7,6},{8,11},{9,8},{10,9... | collective-permute-start | bytes 1032200 | tf_op jit(solution)/shard_map/ppermute | solution.py:401
  155.2 27.2 %collective-permute-start.14 = (bf16[48,3584]{1,0:T(8,128)(2,1)}, bf16[48,3584]{1,0:T(8,128)(2,1)S(1)}, u32[]{:S(2)}, u32[]{:S(2)}) collective-permute-start(bf16[48,3584]{1,0:T(8,128)(2,1)} %get-tuple-element.67), channel_id=1, source_target_pairs={{0,1},{1,2},{2,3},{3,0},{4,5},{5,6},{6,7},{7,4},{8,9},{9,10},{10,1... | collective-permute-start | bytes 1032200 | tf_op jit(solution)/shard_map/ppermute | solution.py:401
  157.1 25.3 %collective-permute-start.15 = (bf16[48,3584]{1,0:T(8,128)(2,1)S(1)}, bf16[48,3584]{1,0:T(8,128)(2,1)S(1)}, u32[]{:S(2)}, u32[]{:S(2)}) collective-permute-start(bf16[48,3584]{1,0:T(8,128)(2,1)S(1)} %copy-done.24), channel_id=1, source_target_pairs={{0,2},{1,3},{2,0},{3,1},{4,6},{5,7},{6,4},{7,5},{8,10},{9,11},{10,... | collective-permute-start | bytes 1032200 | tf_op jit(solution)/shard_map/ppermute | solution.py:401
  158.0 28.2 %collective-permute-start.16 = (bf16[48,3584]{1,0:T(8,128)(2,1)S(1)}, bf16[48,3584]{1,0:T(8,128)(2,1)S(1)}, u32[]{:S(2)}, u32[]{:S(2)}) collective-permute-start(bf16[48,3584]{1,0:T(8,128)(2,1)S(1)} %copy-done.23), channel_id=1, source_target_pairs={{0,3},{1,0},{2,1},{3,2},{4,7},{5,4},{6,5},{7,6},{8,11},{9,8},{10,9... | collective-permute-start | bytes 1032200 | tf_op jit(solution)/shard_map/ppermute | solution.py:401
  178.6 39.5 %collective-permute-start.29 = (bf16[48,3712]{1,0:T(8,128)(2,1)}, bf16[48,3712]{1,0:T(8,128)(2,1)S(1)}, u32[]{:S(2)}, u32[]{:S(2)}) collective-permute-start(bf16[48,3712]{1,0:T(8,128)(2,1)} %get-tuple-element.87), channel_id=1, source_target_pairs={{0,3},{1,0},{2,1},{3,2},{4,7},{5,4},{6,5},{7,6},{8,11},{9,8},{10,9... | collective-permute-start | bytes 1069064 | tf_op jit(solution)/shard_map/ppermute | solution.py:408
  182.4 35.7 %collective-permute-start.30 = (bf16[48,3712]{1,0:T(8,128)(2,1)}, bf16[48,3712]{1,0:T(8,128)(2,1)S(1)}, u32[]{:S(2)}, u32[]{:S(2)}) collective-permute-start(bf16[48,3712]{1,0:T(8,128)(2,1)} %get-tuple-element.88), channel_id=1, source_target_pairs={{0,2},{1,3},{2,0},{3,1},{4,6},{5,7},{6,4},{7,5},{8,10},{9,11},{10,... | collective-permute-start | bytes 1069064 | tf_op jit(solution)/shard_map/ppermute | solution.py:408
  182.5 35.7 %collective-permute-start.31 = (bf16[48,3712]{1,0:T(8,128)(2,1)}, bf16[48,3712]{1,0:T(8,128)(2,1)S(1)}, u32[]{:S(2)}, u32[]{:S(2)}) collective-permute-start(bf16[48,3712]{1,0:T(8,128)(2,1)} %get-tuple-element.89), channel_id=1, source_target_pairs={{0,1},{1,2},{2,3},{3,0},{4,5},{5,6},{6,7},{7,4},{8,9},{9,10},{10,1... | collective-permute-start | bytes 1069064 | tf_op jit(solution)/shard_map/ppermute | solution.py:408
  186.2 23.9 %collective-permute-start.33 = (bf16[48,3712]{1,0:T(8,128)(2,1)}, bf16[48,3712]{1,0:T(8,128)(2,1)S(1)}, u32[]{:S(2)}, u32[]{:S(2)}) collective-permute-start(bf16[48,3712]{1,0:T(8,128)(2,1)} %get-tuple-element.92), channel_id=1, source_target_pairs={{0,2},{1,3},{2,0},{3,1},{4,6},{5,7},{6,4},{7,5},{8,10},{9,11},{10,... | collective-permute-start | bytes 1069064 | tf_op jit(solution)/shard_map/ppermute | solution.py:408
  188.3 25.4 %collective-permute-start.34 = (bf16[48,3712]{1,0:T(8,128)(2,1)}, bf16[48,3712]{1,0:T(8,128)(2,1)S(1)}, u32[]{:S(2)}, u32[]{:S(2)}) collective-permute-start(bf16[48,3712]{1,0:T(8,128)(2,1)} %get-tuple-element.93), channel_id=1, source_target_pairs={{0,1},{1,2},{2,3},{3,0},{4,5},{5,6},{6,7},{7,4},{8,9},{9,10},{10,1... | collective-permute-start | bytes 1069064 | tf_op jit(solution)/shard_map/ppermute | solution.py:408
  223.8 43.5 %collective-permute-start.37 = (bf16[128,3584]{1,0:T(8,128)(2,1)}, bf16[128,3584]{1,0:T(8,128)(2,1)S(1)}, u32[]{:S(2)}, u32[]{:S(2)}) collective-permute-start(bf16[128,3584]{1,0:T(8,128)(2,1)} %shard_map.123.refs_6_), channel_id=1, source_target_pairs={{0,120},{1,121},{2,122},{3,123},{4,124},{5,125},{6,126},{7,127},{8... | collective-permute-start | bytes 2752520 | tf_op jit(solution)/shard_map/ppermute | solution.py:413
  226.4 40.9 %collective-permute-start.38 = (bf16[128,3584]{1,0:T(8,128)(2,1)S(1)}, bf16[128,3584]{1,0:T(8,128)(2,1)S(1)}, u32[]{:S(2)}, u32[]{:S(2)}) collective-permute-start(bf16[128,3584]{1,0:T(8,128)(2,1)S(1)} %copy-done.2), channel_id=1, source_target_pairs={{0,124},{1,125},{2,126},{3,127},{4,120},{5,121},{6,122},{7,123},{8... | collective-permute-start | bytes 2752520 | tf_op jit(solution)/shard_map/ppermute | solution.py:413
  230.6 19.8 %collective-permute-start.28 = (bf16[48,3584]{1,0:T(8,128)(2,1)}, bf16[48,3584]{1,0:T(8,128)(2,1)}, u32[]{:S(2)}, u32[]{:S(2)}) collective-permute-start(bf16[48,3584]{1,0:T(8,128)(2,1)} %get-tuple-element.86), channel_id=1, source_target_pairs={{0,1},{1,2},{2,3},{3,0},{4,5},{5,6},{6,7},{7,4},{8,9},{9,10},{10,1... | collective-permute-start | bytes 1032200 | tf_op jit(solution)/shard_map/ppermute | solution.py:408
  240.5 14.8 %collective-permute-start.23 = (bf16[48,3584]{1,0:T(8,128)(2,1)}, bf16[48,3584]{1,0:T(8,128)(2,1)S(1)}, u32[]{:S(2)}, u32[]{:S(2)}) collective-permute-start(bf16[48,3584]{1,0:T(8,128)(2,1)} %get-tuple-element.79), channel_id=1, source_target_pairs={{0,3},{1,0},{2,1},{3,2},{4,7},{5,4},{6,5},{7,6},{8,11},{9,8},{10,9... | collective-permute-start | bytes 1032200 | tf_op jit(solution)/shard_map/ppermute | solution.py:408
  255.3 30.1 %collective-permute-start.36 = (bf16[128,3584]{1,0:T(8,128)(2,1)}, bf16[128,3584]{1,0:T(8,128)(2,1)}, u32[]{:S(2)}, u32[]{:S(2)}) collective-permute-start(bf16[128,3584]{1,0:T(8,128)(2,1)} %shard_map.124.refs_6_), channel_id=1, source_target_pairs={{0,12},{1,13},{2,14},{3,15},{4,8},{5,9},{6,10},{7,11},{8,20},{9,21... | collective-permute-start | bytes 2752520 | tf_op jit(solution)/shard_map/ppermute | solution.py:413
  267.3 16.8 %collective-permute-start.35 = (bf16[128,3584]{1,0:T(8,128)(2,1)}, bf16[128,3584]{1,0:T(8,128)(2,1)S(1)}, u32[]{:S(2)}, u32[]{:S(2)}) collective-permute-start(bf16[128,3584]{1,0:T(8,128)(2,1)} %shard_map.125), channel_id=1, source_target_pairs={{0,8},{1,9},{2,10},{3,11},{4,12},{5,13},{6,14},{7,15},{8,16},{9,17... | collective-permute-start | bytes 2752520 | tf_op jit(solution)/shard_map/ppermute | solution.py:413
  (38 other events, 478.5 us)

commit v2 on v1

--- a/solution.py
+++ b/solution.py
@@ -21,6 +21,7 @@
 TF = 512
 TB = 1792
 TD = 512
+VMEM_LIMIT = 67043328
 EXT = 128
 f32 = jnp.float32
 bf16 = jnp.bfloat16
@@ -49,6 +50,7 @@
         out_shape=outs,
         scratch_shapes=list(scratch),
         cost_estimate=pl.CostEstimate(flops=int(flops), bytes_accessed=int(moved), transcendentals=0),
+        compiler_params=pltpu.CompilerParams(vmem_limit_bytes=VMEM_LIMIT),
         **kwargs,
     )(*ins)
 
@@ -266,8 +268,8 @@
 
 def forward_body(*refs):
     pieces, gate_ref, up_ref, down_ref = refs[:8], refs[8], refs[9], refs[10]
-    outs = refs[11:19]
-    rows_ref, gate, up, down, a_ref, active_ref, row_sems, gate_sem, up_sem, down_sem = refs[19:]
+    outs = refs[11:27]
+    rows_ref, gate, up, down, a_ref, active_ref, row_sems, gate_sem, up_sem, down_sem = refs[27:]
     rows_in = fetch(row_copies(pieces, rows_ref, row_sems))
     gate_in = pltpu.make_async_copy(gate_ref, gate, gate_sem)
     up_in = pltpu.make_async_copy(up_ref, up, up_sem)
@@ -294,12 +296,9 @@
     lax.fori_loop(0, F // TF, up_strip, 0)
     down_in.wait()
 
-    def tile(i, carry):
-        cols = pl.ds(pl.multiple_of(i * TB, TB), TB)
-        put_rows(outs, cols, jnp.dot(active_ref[...], down[:, cols], preferred_element_type=f32).astype(bf16))
-        return carry
-
-    lax.fori_loop(0, D // TB, tile, 0)
+    for i in range(D // TB):
+        out = jnp.dot(active_ref[...], down[:, i * TB : (i + 1) * TB], preferred_element_type=f32).astype(bf16)
+        put_rows(outs[i * 8 : (i + 1) * 8], slice(None), out)
 
 
 def split_weights(values):
@@ -320,16 +319,20 @@
     hits = hits_of([aux[0:1], aux[1:2]], 256)
     weights = jnp.where(hits[0], aux[2:3], 0.0) + jnp.where(hits[1], aux[3:4], 0.0)
     high, low = split_weights(jnp.transpose(ROUTE_SCALE * weights))
-
-    def tile(cols, carry):
-        rows = rows_ref[:, cols]
-        total = jnp.dot(high, rows, preferred_element_type=f32) + jnp.dot(low, rows, preferred_element_type=f32)
-        if with_input:
-            total = total + base_ref[:, cols].astype(f32)
-        out_ref[:, cols] = total.astype(bf16)
-        return carry
-
-    each_tile(tile)
+    rows = rows_ref[...]
+    total = jnp.dot(high, rows, preferred_element_type=f32) + jnp.dot(low, rows, preferred_element_type=f32)
+    if with_input:
+        total = total + base_ref[...].astype(f32)
+    out_ref[...] = total.astype(bf16)
+
+
+def join_body(a_ref, b_ref, *refs):
+    refs[-1][...] = (a_ref[...].astype(f32) + b_ref[...].astype(f32)).astype(bf16)
+
+
+def join_last_body(a_ref, b_ref, _, c_ref, d_ref, out_ref, other_ref):
+    join_body(a_ref, b_ref, out_ref)
+    join_body(c_ref, d_ref, other_ref)
 
 
 def grad_input_body(with_input, aux_ref, hidden_ref, gain_ref, router_ref, *refs):
@@ -494,18 +497,18 @@
     back_far = collect(returned[NX:])
     back_own = collect(returned[:NX])
     outputs = expert(
-        forward_body, [shape(CAP, D)] * 8, (*f_own, *f_far), (gate, up, down),
+        forward_body, [shape(CAP, TB)] * 16, (*f_own, *f_far), (gate, up, down),
         [rows_vmem, lift_vmem, lift_vmem, down_vmem, act_f32_vmem, act_vmem, sems(8), one, one, one],
         3 * mat_flops, returned[0],
     )
-    y_far = collect(outputs[NX:])
-    y_own = collect(outputs[:NX])
-
-    def mix(pieces, aux, base, with_input, after):
+
+    def mix(where, i, pieces, aux, after):
+        own = where == "own"
         return call(
-            functools.partial(mix_body, with_input), [shape(T, D)], (aux, *pieces, base), grid=(1,),
-            in_specs=[aux_spec] + piece_specs + [full if with_input else vspec((16, D))],
-            out_specs=[full], scratch=[pltpu.VMEM((256, D), bf16)], flops=2 * pack_flops, after=after,
+            functools.partial(mix_body, own), [shape(T, TB)], (aux, *pieces, h_f if own else far_f), grid=(1,),
+            in_specs=[aux_spec] + piece_specs + [vspec((T, TB), (0, i)) if own else vspec((16, TB))],
+            out_specs=[vspec((T, TB))], scratch=[pltpu.VMEM((256, TB), bf16)], flops=pack_flops,
+            after=after,
         )[0]
 
     def grad_input(pieces, aux, hidden, base, with_input, after):
@@ -520,17 +523,34 @@
 
     part_far = grad_input(back_far, aux_b_far, far_b, far_b, False, outputs[0])
     prev_far = relay(part_far, -1, 1)
-    part_own = grad_input(back_own, aux_b, h_b, g, True, part_far)
+    halves = range(D // TB)
+    y_far = [collect(outputs[8 * i + NX : 8 * i + 8]) for i in halves]
+    y_own = [collect(outputs[8 * i : 8 * i + NX]) for i in halves]
+    last, next_far, next_own = part_far, [], []
+    for i in halves:
+        last = mix("far", i, y_far[i], aux_f_far, last)
+        next_far.append(relay(last, 1, 1))
+    last = part_own = grad_input(back_own, aux_b, h_b, g, True, last)
     prev_own = relay(part_own, -1, 0)
-    mix_far = mix(y_far, aux_f_far, far_f, False, part_own)
-    next_far = relay(mix_far, 1, 1)
-    mix_own = mix(y_own, aux_f, h_f, True, mix_far)
-    next_own = relay(mix_own, 1, 0)
-
-    def join(a, b):
-        return (a.astype(f32) + b.astype(f32)).astype(bf16)
-
-    return (join(next_own, next_far)[None], join(prev_own, prev_far)[None])
+    for i in halves:
+        last = mix("own", i, y_own[i], aux_f, last)
+        next_own.append(relay(last, 1, 0))
+
+    half = vspec((T, TB))
+
+    def join(body, i, ins, in_specs, outs, out_specs, aliases):
+        return pl.pallas_call(
+            body, out_shape=[shape(T, D)] * outs, grid=(1,), in_specs=in_specs,
+            out_specs=[vspec((T, TB), (0, i))] + out_specs, input_output_aliases=aliases,
+            compiler_params=pltpu.CompilerParams(vmem_limit_bytes=VMEM_LIMIT),
+        )(*ins)
+
+    (first,) = join(join_body, 0, (next_own[0], next_far[0], last), [half, half, whole], 1, [], {})
+    fwd_next, bwd_prev = join(
+        join_last_body, 1, (next_own[1], next_far[1], first, prev_own, prev_far),
+        [half, half, whole, full, full], 2, [full], {2: 0},
+    )
+    return (fwd_next[None], bwd_prev[None])
 
 
 def solution(mesh):

time: 290 us -> 266 us (0.917)
  waiting for transfers between devices: 147 us -> 96.5 us
  starting transfers between devices: 59.5 us -> 82.9 us
  Pallas kernels: 74.6 us -> 82.8 us
  other arithmetic: 3.44 us -> 0 us
    ppermute x5, waiting for transfers between devices: 53.7 us -> 31.4 us  [across(): return lax.ppermute(block, 'ep', ep_route(1, 0))]
    ppermute x12 -> x18, waiting for transfers between devices: 34.6 us -> 16.9 us  [collect(): moved[dx] = lax.ppermute(pieces[dx], 'ep', ep_route(0, -dx))]
    ppermute x18, waiting for transfers between devices: 41.6 us -> 24.5 us  [spread(): moved[dx] = lax.ppermute(pieces[dx], 'ep', ep_route(0, dx))]
    ppermute x12 -> x18, starting transfers between devices: 16.5 us -> 32.3 us  [collect(): moved[dx] = lax.ppermute(pieces[dx], 'ep', ep_route(0, -dx))]
    ppermute x4 -> x6, waiting for transfers between devices: 16.9 us -> 23.7 us  [relay(): lax.ppermute(block, ('section', 'ep'), relay_route(lax.axis_size('section...]
    pallas_call x0 -> x2, Pallas kernels: none -> 5 us  [join(): pl.pallas_call(body, out_shape=[shape(T, D)] * outs, grid=(1,), in_specs=...]
    broadcast_in_dim x2 -> x0, other arithmetic: 3.44 us -> none  [step(): return (join(next_own, next_far)[None], join(prev_own, prev_far)[None])]
    ppermute x18, starting transfers between devices: 26.4 us -> 29.6 us  [spread(): moved[dx] = lax.ppermute(pieces[dx], 'ep', ep_route(0, dx))]
  transfers between devices with their start and end apart: 39 -> 47, of which waited for: 18 -> 15; matrix products, arithmetic and copies ran while one was open for 0% -> 0% of each run, Pallas kernels for 25% -> 29%
where the time goes in v2:
time: 266 us; the launch traced here: 263 us
  waiting for transfers between devices  96.5 us (36%)
  starting transfers between devices  82.9 us (31%)
  Pallas kernels  82.8 us (31%)
    pallas_call x15, Pallas kernels, call(): pl.pallas_call(body, out_shape=outs, scratch_shapes=list(scratch), cost_e...  77.8 us
    ppermute x18, starting transfers between devices, collect(): moved[dx] = lax.ppermute(pieces[dx], 'ep', ep_route(0, -dx))  32.3 us
    ppermute x5, waiting for transfers between devices, across(): return lax.ppermute(block, 'ep', ep_route(1, 0))  31.4 us
    ppermute x18, starting transfers between devices, spread(): moved[dx] = lax.ppermute(pieces[dx], 'ep', ep_route(0, dx))  29.6 us
    ppermute x18, waiting for transfers between devices, spread(): moved[dx] = lax.ppermute(pieces[dx], 'ep', ep_route(0, dx))  24.5 us
    ppermute x6, waiting for transfers between devices, relay(): lax.ppermute(block, ('section', 'ep'), relay_route(lax.axis_size('section...  23.7 us
    ppermute x18, waiting for transfers between devices, collect(): moved[dx] = lax.ppermute(pieces[dx], 'ep', ep_route(0, -dx))  16.9 us
    ppermute x5, starting transfers between devices, across(): return lax.ppermute(block, 'ep', ep_route(1, 0))  14.1 us
  transfers between devices with their start and end apart: 47, of which 15 were waited for; matrix products, arithmetic and copies ran while one was open for 0% of the time, Pallas kernels for 29%

profile of v2, /device:TPU:0, one launch (start us, length us, event | category | flops | bytes accessed | tf_op | source)
XLA Modules:
  0.0 263.0 jit_solution(8382359768810488065)
XLA Ops:
  0.6 4.1 %collective-permute-start.1 = (bf16[128,3584]{1,0:T(8,128)(2,1)}, bf16[128,3584]{1,0:T(8,128)(2,1)}, u32[]{:S(2)}, u32[]{:S(2)}) collective-permute-start(bf16[128,3584]{1,0:T(8,128)(2,1)} %bitcast.26), channel_id=1, source_target_pairs={{0,4},{1,5},{2,6},{3,7},{4,0},{5,1},{6,2},{7,3},{8,12},{9,13},{10,... | collective-permute-start | bytes 2752520 | tf_op jit(solution)/shard_map/ppermute | solution.py:398
  4.8 3.2 %shard_map.113 = (bf16[48,3584]{1,0:T(8,128)(2,1)}, bf16[48,3584]{1,0:T(8,128)(2,1)}, bf16[48,3584]{1,0:T(8,128)(2,1)}, bf16[48,3584]{1,0:T(8,128)(2,1)}, f32[8,128]{1,0:T(8,128)}) custom-call(s32[1]{0:T(128)} %bitcast.place_ref.refs_0_, s32[2,128]{1,0:T(2,128)} %bitcast.35, bf16[128,3584]{1,0:T(8,128)(2,1)} %bitcast.27, f32[1,3584]{1,0:T(1,128)} %refs_2_.3, ...), custom_call_target="tpu_custom_call" | custom-call | flops 176160768 | bytes 2370564 | tf_op jit(solution)/shard_map/pallas_call | solution.py:48
  12.2 3.4 %collective-permute-start.5 = (s32[2,128]{1,0:T(2,128)}, s32[2,128]{1,0:T(2,128)}, u32[]{:S(2)}, u32[]{:S(2)}) collective-permute-start(s32[2,128]{1,0:T(2,128)} %bitcast.37), channel_id=1, source_target_pairs={{0,4},{1,5},{2,6},{3,7},{4,0},{5,1},{6,2},{7,3},{8,12},{9,13},{10,... | collective-permute-start | bytes 3080 | tf_op jit(solution)/shard_map/ppermute | solution.py:398
  15.7 29.4 %collective-permute-done.5.refs_1_ = s32[2,128]{1,0:T(2,128)} collective-permute-done((s32[2,128]{1,0:T(2,128)}, s32[2,128]{1,0:T(2,128)}, u32[]{:S(2)}, u32[]{:S(2)}) %collective-permute-start.5) | collective-permute-done | bytes 1056 | tf_op jit(solution)/shard_map/ppermute | solution.py:398
  45.0 3.2 %collective-permute-start = (s32[2,128]{1,0:T(2,128)}, s32[2,128]{1,0:T(2,128)}, u32[]{:S(2)}, u32[]{:S(2)}) collective-permute-start(s32[2,128]{1,0:T(2,128)} %bitcast.36), channel_id=1, source_target_pairs={{0,4},{1,5},{2,6},{3,7},{4,0},{5,1},{6,2},{7,3},{8,12},{9,13},{10,... | collective-permute-start | bytes 3080 | tf_op jit(solution)/shard_map/ppermute | solution.py:398
  50.3 3.2 %collective-permute-start.6 = (bf16[128,3584]{1,0:T(8,128)(2,1)}, bf16[128,3584]{1,0:T(8,128)(2,1)}, u32[]{:S(2)}, u32[]{:S(2)}) collective-permute-start(bf16[128,3584]{1,0:T(8,128)(2,1)} %bitcast.18), channel_id=1, source_target_pairs={{0,4},{1,5},{2,6},{3,7},{4,0},{5,1},{6,2},{7,3},{8,12},{9,13},{10,... | collective-permute-start | bytes 2752520 | tf_op jit(solution)/shard_map/ppermute | solution.py:398
  61.4 3.2 %shard_map.115 = (bf16[48,3584]{1,0:T(8,128)(2,1)}, bf16[48,3584]{1,0:T(8,128)(2,1)}, bf16[48,3584]{1,0:T(8,128)(2,1)}, bf16[48,3584]{1,0:T(8,128)(2,1)}, f32[8,128]{1,0:T(8,128)}) custom-call(s32[1]{0:T(128)} %bitcast.place_ref.refs_0_, s32[2,128]{1,0:T(2,128)} %collective-permute-done.refs_1_, ...), custom_call_target="tpu_custom_call" | custom-call | flops 176160768 | bytes 2714628 | tf_op jit(solution)/shard_map/pallas_call | solution.py:48
  64.6 12.3 %collective-permute-done.9.refs_3_ = bf16[48,3584]{1,0:T(8,128)(2,1)} collective-permute-done((bf16[48,3584]{1,0:T(8,128)(2,1)}, bf16[48,3584]{1,0:T(8,128)(2,1)}, u32[]{:S(2)}, u32[]{:S(2)}) %collective-permute-start.9) | collective-permute-done | bytes 344096 | tf_op jit(solution)/shard_map/ppermute | solution.py:404
  77.5 4.5 %collective-permute-start.11 = (bf16[48,3584]{1,0:T(8,128)(2,1)}, bf16[48,3584]{1,0:T(8,128)(2,1)}, u32[]{:S(2)}, u32[]{:S(2)}) collective-permute-start(bf16[48,3584]{1,0:T(8,128)(2,1)} %get-tuple-element.71), channel_id=1, source_target_pairs={{0,2},{1,3},{2,0},{3,1},{4,6},{5,7},{6,4},{7,5},{8,10},{9,11},{10,... | collective-permute-start | bytes 1032200 | tf_op jit(solution)/shard_map/ppermute | solution.py:404
  82.0 3.2 %shard_map.116 = (bf16[48,3584]{1,0:T(8,128)(2,1)}, bf16[48,3584]{1,0:T(8,128)(2,1)}, bf16[48,3584]{1,0:T(8,128)(2,1)}, bf16[48,3584]{1,0:T(8,128)(2,1)}, f32[8,128]{1,0:T(8,128)}) custom-call(s32[1]{0:T(128)} %bitcast.place_ref.refs_0_, s32[2,128]{1,0:T(2,128)} %bitcast.38, bf16[128,3584]{1,0:T(8,128)(2,1)} %bitcast.19, f32[1,3584]{1,0:T(1,128)} %refs_2_.3, ...), custom_call_target="tpu_custom_call" | custom-call | flops 176160768 | bytes 2714628 | tf_op jit(solution)/shard_map/pallas_call | solution.py:48
  92.0 6.7 %collective-permute-done.11.refs_6_ = bf16[48,3584]{1,0:T(8,128)(2,1)} collective-permute-done((bf16[48,3584]{1,0:T(8,128)(2,1)}, bf16[48,3584]{1,0:T(8,128)(2,1)}, u32[]{:S(2)}, u32[]{:S(2)}) %collective-permute-start.11) | collective-permute-done | bytes 344096 | tf_op jit(solution)/shard_map/ppermute | solution.py:404
  100.8 11.5 %shard_map.118 = (f32[2,384,512]{2,1,0:T(8,128)}, f32[2,384,512]{2,1,0:T(8,128)}) custom-call(bf16[48,3584]{1,0:T(8,128)(2,1)} %get-tuple-element.66.refs_0_, bf16[48,3584]{1,0:T(8,128)(2,1)} %collective-permute-done.7.refs_1_, bf16[48,3584]{1,0:T(8,128)(2,1)} %collective-permute-done.8.refs_2_, bf16[48,3584]{1,0:T(8,128)(2,1)} %collective-permute-done.9.refs_3_, ...), custom_call_target="tpu_custom_call" | custom-call | flops 5637144576 | bytes 20922368 | tf_op jit(solution)/shard_map/pallas_call | solution.py:48
  112.3 3.2 %shard_map.119 = (bf16[48,3584]{1,0:T(8,128)(2,1)}, bf16[48,3584]{1,0:T(8,128)(2,1)}, bf16[48,3584]{1,0:T(8,128)(2,1)}, bf16[48,3584]{1,0:T(8,128)(2,1)}, f32[8,128]{1,0:T(8,128)}) custom-call(s32[1]{0:T(128)} %bitcast.place_ref.refs_0_, s32[2,128]{1,0:T(2,128)} %collective-permute-done.5.refs_1_, bf16[128,3584]{1,0:T(8,128)(2,1)} %collective-permute-done.6.refs_2_.refs_5_, ...), custom_call_target="tpu_custom_call" | custom-call | flops 176160768 | bytes 3943428 | tf_op jit(solution)/shard_map/pallas_call | solution.py:48
  121.3 4.2 %collective-permute-start.16 = (bf16[48,3584]{1,0:T(8,128)(2,1)}, bf16[48,3584]{1,0:T(8,128)(2,1)}, u32[]{:S(2)}, u32[]{:S(2)}) collective-permute-start(bf16[48,3584]{1,0:T(8,128)(2,1)} %get-tuple-element.79), channel_id=1, source_target_pairs={{0,3},{1,0},{2,1},{3,2},{4,7},{5,4},{6,5},{7,6},{8,11},{9,8},{10,9... | collective-permute-start | bytes 1032200 | tf_op jit(solution)/shard_map/ppermute | solution.py:404
  125.5 15.5 %shard_map.120 = (bf16[48,3712]{1,0:T(8,128)(2,1)}, bf16[48,3712]{1,0:T(8,128)(2,1)}, bf16[48,3712]{1,0:T(8,128)(2,1)}, bf16[48,3712]{1,0:T(8,128)(2,1)}, bf16[4...) custom-call(bf16[48,3584]{1,0:T(8,128)(2,1)} %get-tuple-element.59.refs_5_.r, ...), custom_call_target="tpu_custom_call" | custom-call | flops 8455716864 | bytes 31113216 | tf_op jit(solution)/shard_map/pallas_call | solution.py:48
  141.2 4.0 %collective-permute-start.39 = (bf16[48,3712]{1,0:T(8,128)(2,1)}, bf16[48,3712]{1,0:T(8,128)(2,1)}, u32[]{:S(2)}, u32[]{:S(2)}) collective-permute-start(bf16[48,3712]{1,0:T(8,128)(2,1)} %get-tuple-element.110), channel_id=1, source_target_pairs={{0,2},{1,3},{2,0},{3,1},{4,6},{5,7},{6,4},{7,5},{8,10},{9,11},{10,... | collective-permute-start | bytes 1069064 | tf_op jit(solution)/shard_map/ppermute | solution.py:411
  145.2 4.5 %collective-permute-done.16.refs_7_ = bf16[48,3584]{1,0:T(8,128)(2,1)} collective-permute-done((bf16[48,3584]{1,0:T(8,128)(2,1)}, bf16[48,3584]{1,0:T(8,128)(2,1)}, u32[]{:S(2)}, u32[]{:S(2)}) %collective-permute-start.16) | collective-permute-done | bytes 344096 | tf_op jit(solution)/shard_map/ppermute | solution.py:404
  149.7 14.5 %shard_map.121 = (bf16[48,1792]{1,0:T(8,128)(2,1)}, bf16[48,1792]{1,0:T(8,128)(2,1)}, bf16[48,1792]{1,0:T(8,128)(2,1)}, bf16[48,1792]{1,0:T(8,128)(2,1)}, bf16[4...) custom-call(bf16[48,3584]{1,0:T(8,128)(2,1)} %get-tuple-element.62.r, ...), custom_call_target="tpu_custom_call" | custom-call | flops 8455716864 | bytes 27881472 | tf_op jit(solution)/shard_map/pallas_call | solution.py:48
  169.6 3.2 %collective-permute-start.30 = (bf16[48,3712]{1,0:T(8,128)(2,1)}, bf16[48,3712]{1,0:T(8,128)(2,1)}, u32[]{:S(2)}, u32[]{:S(2)}) collective-permute-start(bf16[48,3712]{1,0:T(8,128)(2,1)} %get-tuple-element.97), channel_id=1, source_target_pairs={{0,2},{1,3},{2,0},{3,1},{4,6},{5,7},{6,4},{7,5},{8,10},{9,11},{10,... | collective-permute-start | bytes 1069064 | tf_op jit(solution)/shard_map/ppermute | solution.py:411
  176.1 3.7 %collective-permute-start.35 = (bf16[48,1792]{1,0:T(8,128)(2,1)}, bf16[48,1792]{1,0:T(8,128)(2,1)}, u32[]{:S(2)}, u32[]{:S(2)}) collective-permute-start(bf16[48,1792]{1,0:T(8,128)(2,1)} %get-tuple-element.105), channel_id=1, source_target_pairs={{0,3},{1,0},{2,1},{3,2},{4,7},{5,4},{6,5},{7,6},{8,11},{9,8},{10,9... | collective-permute-start | bytes 516104 | tf_op jit(solution)/shard_map/ppermute | solution.py:411
  180.7 8.4 %collective-permute-done.35.refs_2_ = bf16[48,1792]{1,0:T(8,128)(2,1)} collective-permute-done((bf16[48,1792]{1,0:T(8,128)(2,1)}, bf16[48,1792]{1,0:T(8,128)(2,1)}, u32[]{:S(2)}, u32[]{:S(2)}) %collective-permute-start.35) | collective-permute-done | bytes 172064 | tf_op jit(solution)/shard_map/ppermute | solution.py:411
  189.1 3.7 %collective-permute-start.26 = (bf16[48,1792]{1,0:T(8,128)(2,1)}, bf16[48,1792]{1,0:T(8,128)(2,1)}, u32[]{:S(2)}, u32[]{:S(2)}) collective-permute-start(bf16[48,1792]{1,0:T(8,128)(2,1)} %get-tuple-element.93), channel_id=1, source_target_pairs={{0,3},{1,0},{2,1},{3,2},{4,7},{5,4},{6,5},{7,6},{8,11},{9,8},{10,9... | collective-permute-start | bytes 516104 | tf_op jit(solution)/shard_map/ppermute | solution.py:411
  193.6 3.7 %shard_map.122.refs_6_ = bf16[128,3584]{1,0:T(8,128)(2,1)} custom-call(f32[8,128]{1,0:T(8,128)} %get-tuple-element.73.refs_0_, bf16[128,3584]{1,0:T(8,128)(2,1)} %collective-permute-done.1.refs_2_.refs_1_.refs_8_, f32[1,3584]{1,0:T(1,128)} %refs_2_.3, bf16[8,3584]{1,0:T(8,128)(2,1)} %bitcast.33, bf16[48,3712]{1,0:T(8,128)(2,1)} %get-tuple-element.108.refs_4_, ...), custom_call_target="tpu_custom_call" | custom-call | flops 352321536 | bytes 4425728 | tf_op jit(solution)/shard_map/pallas_call | solution.py:48
  202.2 4.1 %shard_map.125.refs_6_ = bf16[128,3584]{1,0:T(8,128)(2,1)} custom-call(f32[8,128]{1,0:T(8,128)} %get-tuple-element.58.aux_ref.refs_0_, bf16[128,3584]{1,0:T(8,128)(2,1)} %bitcast.28, f32[1,3584]{1,0:T(1,128)} %refs_2_.3, bf16[8,3584]{1,0:T(8,128)(2,1)} %bitcast.34, bf16[48,3712]{1,0:T(8,128)(2,1)} %get-tuple-element.87.refs_11_.refs_4_, ...), custom_call_target="tpu_custom_call" | custom-call | flops 352321536 | bytes 4712448 | tf_op jit(solution)/shard_map/pallas_call | solution.py:48
  208.9 3.0 %collective-permute-start.46 = (bf16[128,3584]{1,0:T(8,128)(2,1)}, bf16[128,3584]{1,0:T(8,128)(2,1)}, u32[]{:S(2)}, u32[]{:S(2)}) collective-permute-start(bf16[128,3584]{1,0:T(8,128)(2,1)} %shard_map.122.refs_6_), channel_id=1, source_target_pairs={{0,124},{1,125},{2,126},{3,127},{4,120},{5,121},{6,122},{7,123},{8... | collective-permute-start | bytes 2752520 | tf_op jit(solution)/shard_map/ppermute | solution.py:416
  217.5 3.5 %collective-permute-done.23.refs_2_ = bf16[48,1792]{1,0:T(8,128)(2,1)} collective-permute-done((bf16[48,1792]{1,0:T(8,128)(2,1)}, bf16[48,1792]{1,0:T(8,128)(2,1)}, u32[]{:S(2)}, u32[]{:S(2)}) %collective-permute-start.23) | collective-permute-done | bytes 172064 | tf_op jit(solution)/shard_map/ppermute | solution.py:411
  221.0 4.4 %collective-permute-start.25 = (bf16[48,1792]{1,0:T(8,128)(2,1)}, bf16[48,1792]{1,0:T(8,128)(2,1)}, u32[]{:S(2)}, u32[]{:S(2)}) collective-permute-start(bf16[48,1792]{1,0:T(8,128)(2,1)} %get-tuple-element.91), channel_id=1, source_target_pairs={{0,1},{1,2},{2,3},{3,0},{4,5},{5,6},{6,7},{7,4},{8,9},{9,10},{10,1... | collective-permute-start | bytes 516104 | tf_op jit(solution)/shard_map/ppermute | solution.py:411
  225.3 3.2 %collective-permute-done.25.refs_4_ = bf16[48,1792]{1,0:T(8,128)(2,1)} collective-permute-done((bf16[48,1792]{1,0:T(8,128)(2,1)}, bf16[48,1792]{1,0:T(8,128)(2,1)}, u32[]{:S(2)}, u32[]{:S(2)}) %collective-permute-start.25) | collective-permute-done | bytes 172064 | tf_op jit(solution)/shard_map/ppermute | solution.py:411
  231.2 3.0 %collective-permute-start.42 = (bf16[128,1792]{1,0:T(8,128)(2,1)}, bf16[128,1792]{1,0:T(8,128)(2,1)}, u32[]{:S(2)}, u32[]{:S(2)}) collective-permute-start(bf16[128,1792]{1,0:T(8,128)(2,1)} %shard_map.124.refs_9_), channel_id=1, source_target_pairs={{0,12},{1,13},{2,14},{3,15},{4,8},{5,9},{6,10},{7,11},{8,20},{9,21... | collective-permute-start | bytes 1376264 | tf_op jit(solution)/shard_map/ppermute | solution.py:416
  234.3 15.8 %collective-permute-done.44.b_ref = bf16[128,1792]{1,0:T(8,128)(2,1)} collective-permute-done((bf16[128,1792]{1,0:T(8,128)(2,1)}, bf16[128,1792]{1,0:T(8,128)(2,1)}, u32[]{:S(2)}, u32[]{:S(2)}) %collective-permute-start.44) | collective-permute-done | bytes 458784 | tf_op jit(solution)/shard_map/ppermute | solution.py:416
  252.1 6.1 %collective-permute-done.42.b_ref = bf16[128,1792]{1,0:T(8,128)(2,1)} collective-permute-done((bf16[128,1792]{1,0:T(8,128)(2,1)}, bf16[128,1792]{1,0:T(8,128)(2,1)}, u32[]{:S(2)}, u32[]{:S(2)}) %collective-permute-start.42) | collective-permute-done | bytes 458784 | tf_op jit(solution)/shard_map/ppermute | solution.py:416
  260.0 3.0 %shard_map.129 = (bf16[128,3584]{1,0:T(8,128)(2,1)}, bf16[128,3584]{1,0:T(8,128)(2,1)}) custom-call(bf16[128,1792]{1,0:T(8,128)(2,1)} %collective-permute-done.41.a_ref, bf16[128,1792]{1,0:T(8,128)(2,1)} %collective-permute-done.42.b_ref, bf16[128,3584]{1,0:T(8,128)(2,1)} %shard_map.128._, ...), custom_call_target="tpu_custom_call", output_to_operand_aliasing={{0}: (2, {})} | custom-call | tf_op jit(solution)/shard_map/pallas_call | solution.py:542
  (79 shorter events, 59.6 us)
Async XLA Ops:
  0.6 58.5 %collective-permute-start.1 = (bf16[128,3584]{1,0:T(8,128)(2,1)}, bf16[128,3584]{1,0:T(8,128)(2,1)}, u32[]{:S(2)}, u32[]{:S(2)}) collective-permute-start(bf16[128,3584]{1,0:T(8,128)(2,1)} %bitcast.26), channel_id=1, source_target_pairs={{0,4},{1,5},{2,6},{3,7},{4,0},{5,1},{6,2},{7,3},{8,12},{9,13},{10,... | collective-permute-start | bytes 2752520 | tf_op jit(solution)/shard_map/ppermute | solution.py:398
  4.7 77.3 %collective-permute-start.13 = (bf16[128,3584]{1,0:T(8,128)(2,1)}, bf16[128,3584]{1,0:T(8,128)(2,1)}, u32[]{:S(2)}, u32[]{:S(2)}) collective-permute-start(bf16[128,3584]{1,0:T(8,128)(2,1)} %bitcast.23), channel_id=1, source_target_pairs={{0,4},{1,5},{2,6},{3,7},{4,0},{5,1},{6,2},{7,3},{8,12},{9,13},{10,... | collective-permute-start | bytes 2752520 | tf_op jit(solution)/shard_map/ppermute | solution.py:398
  8.0 48.3 %collective-permute-start.7 = (bf16[48,3584]{1,0:T(8,128)(2,1)}, bf16[48,3584]{1,0:T(8,128)(2,1)}, u32[]{:S(2)}, u32[]{:S(2)}) collective-permute-start(bf16[48,3584]{1,0:T(8,128)(2,1)} %get-tuple-element.67), channel_id=1, source_target_pairs={{0,1},{1,2},{2,3},{3,0},{4,5},{5,6},{6,7},{7,4},{8,9},{9,10},{10,1... | collective-permute-start | bytes 1032200 | tf_op jit(solution)/shard_map/ppermute | solution.py:404
  9.5 49.6 %collective-permute-start.8 = (bf16[48,3584]{1,0:T(8,128)(2,1)}, bf16[48,3584]{1,0:T(8,128)(2,1)}, u32[]{:S(2)}, u32[]{:S(2)}) collective-permute-start(bf16[48,3584]{1,0:T(8,128)(2,1)} %get-tuple-element.68), channel_id=1, source_target_pairs={{0,2},{1,3},{2,0},{3,1},{4,6},{5,7},{6,4},{7,5},{8,10},{9,11},{10,... | collective-permute-start | bytes 1032200 | tf_op jit(solution)/shard_map/ppermute | solution.py:404
  12.2 32.8 %collective-permute-start.5 = (s32[2,128]{1,0:T(2,128)}, s32[2,128]{1,0:T(2,128)}, u32[]{:S(2)}, u32[]{:S(2)}) collective-permute-start(s32[2,128]{1,0:T(2,128)} %bitcast.37), channel_id=1, source_target_pairs={{0,4},{1,5},{2,6},{3,7},{4,0},{5,1},{6,2},{7,3},{8,12},{9,13},{10,... | collective-permute-start | bytes 3080 | tf_op jit(solution)/shard_map/ppermute | solution.py:398
  50.3 38.3 %collective-permute-start.6 = (bf16[128,3584]{1,0:T(8,128)(2,1)}, bf16[128,3584]{1,0:T(8,128)(2,1)}, u32[]{:S(2)}, u32[]{:S(2)}) collective-permute-start(bf16[128,3584]{1,0:T(8,128)(2,1)} %bitcast.18), channel_id=1, source_target_pairs={{0,4},{1,5},{2,6},{3,7},{4,0},{5,1},{6,2},{7,3},{8,12},{9,13},{10,... | collective-permute-start | bytes 2752520 | tf_op jit(solution)/shard_map/ppermute | solution.py:398
  56.3 20.5 %collective-permute-start.9 = (bf16[48,3584]{1,0:T(8,128)(2,1)}, bf16[48,3584]{1,0:T(8,128)(2,1)}, u32[]{:S(2)}, u32[]{:S(2)}) collective-permute-start(bf16[48,3584]{1,0:T(8,128)(2,1)} %get-tuple-element.69), channel_id=1, source_target_pairs={{0,3},{1,0},{2,1},{3,2},{4,7},{5,4},{6,5},{7,6},{8,11},{9,8},{10,9... | collective-permute-start | bytes 1032200 | tf_op jit(solution)/shard_map/ppermute | solution.py:404
  59.1 18.5 %collective-permute-start.17 = (bf16[48,3584]{1,0:T(8,128)(2,1)}, bf16[48,3584]{1,0:T(8,128)(2,1)}, u32[]{:S(2)}, u32[]{:S(2)}) collective-permute-start(bf16[48,3584]{1,0:T(8,128)(2,1)} %get-tuple-element.80), channel_id=1, source_target_pairs={{0,1},{1,2},{2,3},{3,0},{4,5},{5,6},{6,7},{7,4},{8,9},{9,10},{10,1... | collective-permute-start | bytes 1032200 | tf_op jit(solution)/shard_map/ppermute | solution.py:404
  59.1 28.9 %collective-permute-start.18 = (bf16[48,3584]{1,0:T(8,128)(2,1)}, bf16[48,3584]{1,0:T(8,128)(2,1)}, u32[]{:S(2)}, u32[]{:S(2)}) collective-permute-start(bf16[48,3584]{1,0:T(8,128)(2,1)} %get-tuple-element.81), channel_id=1, source_target_pairs={{0,2},{1,3},{2,0},{3,1},{4,6},{5,7},{6,4},{7,5},{8,10},{9,11},{10,... | collective-permute-start | bytes 1032200 | tf_op jit(solution)/shard_map/ppermute | solution.py:404
  77.5 21.1 %collective-permute-start.11 = (bf16[48,3584]{1,0:T(8,128)(2,1)}, bf16[48,3584]{1,0:T(8,128)(2,1)}, u32[]{:S(2)}, u32[]{:S(2)}) collective-permute-start(bf16[48,3584]{1,0:T(8,128)(2,1)} %get-tuple-element.71), channel_id=1, source_target_pairs={{0,2},{1,3},{2,0},{3,1},{4,6},{5,7},{6,4},{7,5},{8,10},{9,11},{10,... | collective-permute-start | bytes 1032200 | tf_op jit(solution)/shard_map/ppermute | solution.py:404
  88.0 27.5 %collective-permute-start.19 = (bf16[48,3584]{1,0:T(8,128)(2,1)}, bf16[48,3584]{1,0:T(8,128)(2,1)}, u32[]{:S(2)}, u32[]{:S(2)}) collective-permute-start(bf16[48,3584]{1,0:T(8,128)(2,1)} %get-tuple-element.82), channel_id=1, source_target_pairs={{0,3},{1,0},{2,1},{3,2},{4,7},{5,4},{6,5},{7,6},{8,11},{9,8},{10,9... | collective-permute-start | bytes 1032200 | tf_op jit(solution)/shard_map/ppermute | solution.py:404
  88.6 28.4 %collective-permute-start.2 = (bf16[48,3584]{1,0:T(8,128)(2,1)}, bf16[48,3584]{1,0:T(8,128)(2,1)}, u32[]{:S(2)}, u32[]{:S(2)}) collective-permute-start(bf16[48,3584]{1,0:T(8,128)(2,1)} %get-tuple-element.63), channel_id=1, source_target_pairs={{0,1},{1,2},{2,3},{3,0},{4,5},{5,6},{6,7},{7,4},{8,9},{9,10},{10,1... | collective-permute-start | bytes 1032200 | tf_op jit(solution)/shard_map/ppermute | solution.py:404
  90.1 28.1 %collective-permute-start.20 = (bf16[48,3584]{1,0:T(8,128)(2,1)}, bf16[48,3584]{1,0:T(8,128)(2,1)}, u32[]{:S(2)}, u32[]{:S(2)}) collective-permute-start(bf16[48,3584]{1,0:T(8,128)(2,1)} %get-tuple-element.83), channel_id=1, source_target_pairs={{0,1},{1,2},{2,3},{3,0},{4,5},{5,6},{6,7},{7,4},{8,9},{9,10},{10,1... | collective-permute-start | bytes 1032200 | tf_op jit(solution)/shard_map/ppermute | solution.py:404
  98.7 20.3 %collective-permute-start.21 = (bf16[48,3584]{1,0:T(8,128)(2,1)}, bf16[48,3584]{1,0:T(8,128)(2,1)}, u32[]{:S(2)}, u32[]{:S(2)}) collective-permute-start(bf16[48,3584]{1,0:T(8,128)(2,1)} %get-tuple-element.84), channel_id=1, source_target_pairs={{0,2},{1,3},{2,0},{3,1},{4,6},{5,7},{6,4},{7,5},{8,10},{9,11},{10,... | collective-permute-start | bytes 1032200 | tf_op jit(solution)/shard_map/ppermute | solution.py:404
  98.7 22.6 %collective-permute-start.22 = (bf16[48,3584]{1,0:T(8,128)(2,1)}, bf16[48,3584]{1,0:T(8,128)(2,1)}, u32[]{:S(2)}, u32[]{:S(2)}) collective-permute-start(bf16[48,3584]{1,0:T(8,128)(2,1)} %get-tuple-element.85), channel_id=1, source_target_pairs={{0,3},{1,0},{2,1},{3,2},{4,7},{5,4},{6,5},{7,6},{8,11},{9,8},{10,9... | collective-permute-start | bytes 1032200 | tf_op jit(solution)/shard_map/ppermute | solution.py:404
  115.5 25.5 %collective-permute-start.3 = (bf16[48,3584]{1,0:T(8,128)(2,1)}, bf16[48,3584]{1,0:T(8,128)(2,1)}, u32[]{:S(2)}, u32[]{:S(2)}) collective-permute-start(bf16[48,3584]{1,0:T(8,128)(2,1)} %get-tuple-element.64), channel_id=1, source_target_pairs={{0,2},{1,3},{2,0},{3,1},{4,6},{5,7},{6,4},{7,5},{8,10},{9,11},{10,... | collective-permute-start | bytes 1032200 | tf_op jit(solution)/shard_map/ppermute | solution.py:404
  117.0 24.1 %collective-permute-start.4 = (bf16[48,3584]{1,0:T(8,128)(2,1)}, bf16[48,3584]{1,0:T(8,128)(2,1)}, u32[]{:S(2)}, u32[]{:S(2)}) collective-permute-start(bf16[48,3584]{1,0:T(8,128)(2,1)} %get-tuple-element.65), channel_id=1, source_target_pairs={{0,3},{1,0},{2,1},{3,2},{4,7},{5,4},{6,5},{7,6},{8,11},{9,8},{10,9... | collective-permute-start | bytes 1032200 | tf_op jit(solution)/shard_map/ppermute | solution.py:404
  118.1 23.0 %collective-permute-start.14 = (bf16[48,3584]{1,0:T(8,128)(2,1)}, bf16[48,3584]{1,0:T(8,128)(2,1)}, u32[]{:S(2)}, u32[]{:S(2)}) collective-permute-start(bf16[48,3584]{1,0:T(8,128)(2,1)} %get-tuple-element.77), channel_id=1, source_target_pairs={{0,1},{1,2},{2,3},{3,0},{4,5},{5,6},{6,7},{7,4},{8,9},{9,10},{10,1... | collective-permute-start | bytes 1032200 | tf_op jit(solution)/shard_map/ppermute | solution.py:404
  119.0 26.2 %collective-permute-start.15 = (bf16[48,3584]{1,0:T(8,128)(2,1)}, bf16[48,3584]{1,0:T(8,128)(2,1)}, u32[]{:S(2)}, u32[]{:S(2)}) collective-permute-start(bf16[48,3584]{1,0:T(8,128)(2,1)} %get-tuple-element.78), channel_id=1, source_target_pairs={{0,2},{1,3},{2,0},{3,1},{4,6},{5,7},{6,4},{7,5},{8,10},{9,11},{10,... | collective-permute-start | bytes 1032200 | tf_op jit(solution)/shard_map/ppermute | solution.py:404
  121.3 28.4 %collective-permute-start.16 = (bf16[48,3584]{1,0:T(8,128)(2,1)}, bf16[48,3584]{1,0:T(8,128)(2,1)}, u32[]{:S(2)}, u32[]{:S(2)}) collective-permute-start(bf16[48,3584]{1,0:T(8,128)(2,1)} %get-tuple-element.79), channel_id=1, source_target_pairs={{0,3},{1,0},{2,1},{3,2},{4,7},{5,4},{6,5},{7,6},{8,11},{9,8},{10,9... | collective-permute-start | bytes 1032200 | tf_op jit(solution)/shard_map/ppermute | solution.py:404
  141.0 23.3 %collective-permute-start.29 = (bf16[48,3712]{1,0:T(8,128)(2,1)}, bf16[48,3712]{1,0:T(8,128)(2,1)}, u32[]{:S(2)}, u32[]{:S(2)}) collective-permute-start(bf16[48,3712]{1,0:T(8,128)(2,1)} %get-tuple-element.96), channel_id=1, source_target_pairs={{0,3},{1,0},{2,1},{3,2},{4,7},{5,4},{6,5},{7,6},{8,11},{9,8},{10,9... | collective-permute-start | bytes 1069064 | tf_op jit(solution)/shard_map/ppermute | solution.py:411
  141.1 26.0 %collective-permute-start.38 = (bf16[48,3712]{1,0:T(8,128)(2,1)}, bf16[48,3712]{1,0:T(8,128)(2,1)}, u32[]{:S(2)}, u32[]{:S(2)}) collective-permute-start(bf16[48,3712]{1,0:T(8,128)(2,1)} %get-tuple-element.109), channel_id=1, source_target_pairs={{0,3},{1,0},{2,1},{3,2},{4,7},{5,4},{6,5},{7,6},{8,11},{9,8},{10,9... | collective-permute-start | bytes 1069064 | tf_op jit(solution)/shard_map/ppermute | solution.py:411
  141.2 28.4 %collective-permute-start.39 = (bf16[48,3712]{1,0:T(8,128)(2,1)}, bf16[48,3712]{1,0:T(8,128)(2,1)}, u32[]{:S(2)}, u32[]{:S(2)}) collective-permute-start(bf16[48,3712]{1,0:T(8,128)(2,1)} %get-tuple-element.110), channel_id=1, source_target_pairs={{0,2},{1,3},{2,0},{3,1},{4,6},{5,7},{6,4},{7,5},{8,10},{9,11},{10,... | collective-permute-start | bytes 1069064 | tf_op jit(solution)/shard_map/ppermute | solution.py:411
  145.2 27.6 %collective-permute-start.40 = (bf16[48,3712]{1,0:T(8,128)(2,1)}, bf16[48,3712]{1,0:T(8,128)(2,1)}, u32[]{:S(2)}, u32[]{:S(2)}) collective-permute-start(bf16[48,3712]{1,0:T(8,128)(2,1)} %get-tuple-element.111), channel_id=1, source_target_pairs={{0,1},{1,2},{2,3},{3,0},{4,5},{5,6},{6,7},{7,4},{8,9},{9,10},{10,1... | collective-permute-start | bytes 1069064 | tf_op jit(solution)/shard_map/ppermute | solution.py:411
  169.6 32.6 %collective-permute-start.30 = (bf16[48,3712]{1,0:T(8,128)(2,1)}, bf16[48,3712]{1,0:T(8,128)(2,1)}, u32[]{:S(2)}, u32[]{:S(2)}) collective-permute-start(bf16[48,3712]{1,0:T(8,128)(2,1)} %get-tuple-element.97), channel_id=1, source_target_pairs={{0,2},{1,3},{2,0},{3,1},{4,6},{5,7},{6,4},{7,5},{8,10},{9,11},{10,... | collective-permute-start | bytes 1069064 | tf_op jit(solution)/shard_map/ppermute | solution.py:411
  172.8 29.4 %collective-permute-start.31 = (bf16[48,3712]{1,0:T(8,128)(2,1)}, bf16[48,3712]{1,0:T(8,128)(2,1)}, u32[]{:S(2)}, u32[]{:S(2)}) collective-permute-start(bf16[48,3712]{1,0:T(8,128)(2,1)} %get-tuple-element.98), channel_id=1, source_target_pairs={{0,1},{1,2},{2,3},{3,0},{4,5},{5,6},{6,7},{7,4},{8,9},{9,10},{10,1... | collective-permute-start | bytes 1069064 | tf_op jit(solution)/shard_map/ppermute | solution.py:411
  208.9 22.3 %collective-permute-start.43 = (bf16[128,1792]{1,0:T(8,128)(2,1)}, bf16[128,1792]{1,0:T(8,128)(2,1)}, u32[]{:S(2)}, u32[]{:S(2)}) collective-permute-start(bf16[128,1792]{1,0:T(8,128)(2,1)} %shard_map.126.refs_6_), channel_id=1, source_target_pairs={{0,8},{1,9},{2,10},{3,11},{4,12},{5,13},{6,14},{7,15},{8,16},{9,17... | collective-permute-start | bytes 1376264 | tf_op jit(solution)/shard_map/ppermute | solution.py:416
  208.9 51.0 %collective-permute-start.46 = (bf16[128,3584]{1,0:T(8,128)(2,1)}, bf16[128,3584]{1,0:T(8,128)(2,1)}, u32[]{:S(2)}, u32[]{:S(2)}) collective-permute-start(bf16[128,3584]{1,0:T(8,128)(2,1)} %shard_map.122.refs_6_), channel_id=1, source_target_pairs={{0,124},{1,125},{2,126},{3,127},{4,120},{5,121},{6,122},{7,123},{8... | collective-permute-start | bytes 2752520 | tf_op jit(solution)/shard_map/ppermute | solution.py:416
  211.9 48.1 %collective-permute-start.45 = (bf16[128,3584]{1,0:T(8,128)(2,1)}, bf16[128,3584]{1,0:T(8,128)(2,1)}, u32[]{:S(2)}, u32[]{:S(2)}) collective-permute-start(bf16[128,3584]{1,0:T(8,128)(2,1)} %shard_map.125.refs_6_), channel_id=1, source_target_pairs={{0,120},{1,121},{2,122},{3,123},{4,124},{5,125},{6,126},{7,127},{8... | collective-permute-start | bytes 2752520 | tf_op jit(solution)/shard_map/ppermute | solution.py:416
  225.3 24.7 %collective-permute-start.44 = (bf16[128,1792]{1,0:T(8,128)(2,1)}, bf16[128,1792]{1,0:T(8,128)(2,1)}, u32[]{:S(2)}, u32[]{:S(2)}) collective-permute-start(bf16[128,1792]{1,0:T(8,128)(2,1)} %shard_map.123.refs_6_), channel_id=1, source_target_pairs={{0,12},{1,13},{2,14},{3,15},{4,8},{5,9},{6,10},{7,11},{8,20},{9,21... | collective-permute-start | bytes 1376264 | tf_op jit(solution)/shard_map/ppermute | solution.py:416
  231.2 20.9 %collective-permute-start.41 = (bf16[128,1792]{1,0:T(8,128)(2,1)}, bf16[128,1792]{1,0:T(8,128)(2,1)}, u32[]{:S(2)}, u32[]{:S(2)}) collective-permute-start(bf16[128,1792]{1,0:T(8,128)(2,1)} %shard_map.127.refs_0_), channel_id=1, source_target_pairs={{0,8},{1,9},{2,10},{3,11},{4,12},{5,13},{6,14},{7,15},{8,16},{9,17... | collective-permute-start | bytes 1376264 | tf_op jit(solution)/shard_map/ppermute | solution.py:416
  231.2 27.0 %collective-permute-start.42 = (bf16[128,1792]{1,0:T(8,128)(2,1)}, bf16[128,1792]{1,0:T(8,128)(2,1)}, u32[]{:S(2)}, u32[]{:S(2)}) collective-permute-start(bf16[128,1792]{1,0:T(8,128)(2,1)} %shard_map.124.refs_9_), channel_id=1, source_target_pairs={{0,12},{1,13},{2,14},{3,15},{4,8},{5,9},{6,10},{7,11},{8,20},{9,21... | collective-permute-start | bytes 1376264 | tf_op jit(solution)/shard_map/ppermute | solution.py:416
  (15 other events, 184.2 us)

commit v3 on v2

--- a/solution.py
+++ b/solution.py
@@ -134,10 +134,7 @@
     return lax.rsqrt(each_tile(tile, jnp.zeros((T, 1), f32)) / D + NORM_EPSILON)
 
 
-def prep_norm_body(place_ref, ids_ref, rows_ref, gain_ref, router_ref, *refs):
-    outs, aux_ref, normed_ref = refs[:NX], refs[NX], refs[NX + 1]
-    named = [ids_ref[k : k + 1, :] for k in range(2)]
-    slots = slots_of(named, place_ref)
+def normalize(rows_ref, gain_ref, normed_ref):
     inverse = inverse_of(rows_ref)
 
     def tile(cols, carry):
@@ -145,14 +142,42 @@
         return carry
 
     each_tile(tile)
-    pack(slots, lambda cols: normed_ref[:, cols], outs)
+
+
+def route(named, slots, normed_ref, router_ref):
     logits = lax.dot_general(router_ref[...], normed_ref[...], NT, preferred_element_type=f32)
     scores = jax.nn.sigmoid(logits)
     expert = rows_iota(EXPERTS)
     picked = [jnp.sum(jnp.where(expert == name, scores, 0.0), axis=0, keepdims=True) for name in named]
     both = picked[0] + picked[1]
-    lines = slots + [p / both for p in picked] + picked + [name.astype(f32) for name in named]
+    return slots + [p / both for p in picked] + picked + [name.astype(f32) for name in named]
+
+
+def prep_first_body(place_ref, ids_ref, rows_ref, gain_ref, *refs):
+    outs, normed_ref = refs[:NX], refs[NX]
+    slots = slots_of([ids_ref[k : k + 1, :] for k in range(2)], place_ref)
+    normalize(rows_ref, gain_ref, normed_ref)
+    pack(slots, lambda cols: normed_ref[:, cols], outs)
+
+
+def prep_second_body(place_ref, ids_ref, rows_ref, gain_ref, router_ref, grad_ref, *refs):
+    outs, aux_ref, normed_ref = refs[:NX], refs[NX], refs[NX + 1]
+    named = [ids_ref[k : k + 1, :] for k in range(2)]
+    slots = slots_of(named, place_ref)
+    normalize(rows_ref, gain_ref, normed_ref)
+    lines = route(named, slots, normed_ref, router_ref)
     for i, line in enumerate(lines):
+        aux_ref[i : i + 1, :] = line
+    pack(slots, lambda cols: grad_ref[:, cols], outs, lines[2:4])
+
+
+def prep_norm_body(place_ref, ids_ref, rows_ref, gain_ref, router_ref, *refs):
+    outs, aux_ref, normed_ref = refs[:NX], refs[NX], refs[NX + 1]
+    named = [ids_ref[k : k + 1, :] for k in range(2)]
+    slots = slots_of(named, place_ref)
+    normalize(rows_ref, gain_ref, normed_ref)
+    pack(slots, lambda cols: normed_ref[:, cols], outs)
+    for i, line in enumerate(route(named, slots, normed_ref, router_ref)):
         aux_ref[i : i + 1, :] = line
 
 
@@ -188,6 +213,24 @@
             outs[z * NX + step][:, cols] = rows[at : at + CAP]
 
 
+def lift_copies(source, target, sems):
+    halves = [pl.ds(i * TB, TB) for i in range(D // TB)]
+    return [pltpu.make_async_copy(source.at[h, :], target.at[h, :], sems.at[i]) for i, h in enumerate(halves)]
+
+
+def lift_strips(rows_ref, matrix, copies, out_ref):
+    for n, copy in enumerate(copies):
+        copy.wait()
+        depth = slice(n * TB, (n + 1) * TB)
+
+        def strip(i, carry):
+            part = jnp.dot(rows_ref[:, depth], matrix[depth, strip_of(i)], preferred_element_type=f32)
+            out_ref[i] = out_ref[i] + part if n else part
+            return carry
+
+        lax.fori_loop(0, F // TF, strip, 0)
+
+
 def strip_of(i):
     return pl.ds(pl.multiple_of(i * TF, TF), TF)
 
@@ -196,19 +239,11 @@
     pieces, gate_ref, up_ref, a_ref, b_ref = refs[:8], refs[8], refs[9], refs[10], refs[11]
     rows_ref, gate, up, row_sems, gate_sem, up_sem = refs[12:]
     rows_in = fetch(row_copies(pieces, rows_ref, row_sems))
-    gate_in = pltpu.make_async_copy(gate_ref, gate, gate_sem)
-    up_in = pltpu.make_async_copy(up_ref, up, up_sem)
-    gate_in.start()
+    gate_in = fetch(lift_copies(gate_ref, gate, gate_sem))
     finish(rows_in)
-    up_in.start()
-    for weights, copy, out_ref in ((gate, gate_in, a_ref), (up, up_in, b_ref)):
-        copy.wait()
-
-        def strip(i, carry):
-            out_ref[i] = jnp.dot(rows_ref[...], weights[:, strip_of(i)], preferred_element_type=f32)
-            return carry
-
-        lax.fori_loop(0, F // TF, strip, 0)
+    up_in = fetch(lift_copies(up_ref, up, up_sem))
+    lift_strips(rows_ref, gate, gate_in, a_ref)
+    lift_strips(rows_ref, up, up_in, b_ref)
 
 
 def back_body(*refs):
@@ -271,20 +306,13 @@
     outs = refs[11:27]
     rows_ref, gate, up, down, a_ref, active_ref, row_sems, gate_sem, up_sem, down_sem = refs[27:]
     rows_in = fetch(row_copies(pieces, rows_ref, row_sems))
-    gate_in = pltpu.make_async_copy(gate_ref, gate, gate_sem)
+    gate_in = fetch(lift_copies(gate_ref, gate, gate_sem))
     up_in = pltpu.make_async_copy(up_ref, up, up_sem)
     down_in = pltpu.make_async_copy(down_ref, down, down_sem)
-    gate_in.start()
     finish(rows_in)
     up_in.start()
-    gate_in.wait()
     down_in.start()
-
-    def gate_strip(i, carry):
-        a_ref[i] = jnp.dot(rows_ref[...], gate[:, strip_of(i)], preferred_element_type=f32)
-        return carry
-
-    lax.fori_loop(0, F // TF, gate_strip, 0)
+    lift_strips(rows_ref, gate, gate_in, a_ref)
     up_in.wait()
 
     def up_strip(i, carry):
@@ -330,11 +358,6 @@
     refs[-1][...] = (a_ref[...].astype(f32) + b_ref[...].astype(f32)).astype(bf16)
 
 
-def join_last_body(a_ref, b_ref, _, c_ref, d_ref, out_ref, other_ref):
-    join_body(a_ref, b_ref, out_ref)
-    join_body(c_ref, d_ref, other_ref)
-
-
 def grad_input_body(with_input, aux_ref, hidden_ref, gain_ref, router_ref, *refs):
     pieces, base_ref, out_ref, rows_ref, scaled_ref = refs[:NX], refs[NX], refs[NX + 1], refs[NX + 2], refs[NX + 3]
     stack_pieces(pieces, rows_ref)
@@ -345,8 +368,8 @@
     for hit in hits:
         found = jnp.dot(extra, hit.astype(bf16), preferred_element_type=f32)
         pulls.append(found[0:1] + found[1:2])
-    route = router_ref[...]
-    rows_ref[NX * CAP : NX * CAP + 16, :D] = jnp.concatenate([route, route], axis=0)
+    router = router_ref[...]
+    rows_ref[NX * CAP : NX * CAP + 16, :D] = jnp.concatenate([router, router], axis=0)
     slot = rows_iota(256)
     high = jnp.zeros((256, T), f32)
     low = jnp.zeros((256, T), f32)
@@ -454,9 +477,18 @@
         )
         return outs[:NX], outs[NX]
 
-    packed_b, aux_b = prep_norm("b_own", h_b, ids_b)
+    packed_b = call(
+        prep_first_body, packed, (place, ids_b, h_b, norm_gain), grid=(1,),
+        in_specs=[sspec(), chip(), full, vspec((1, D))], out_specs=piece_specs, scratch=[pltpu.VMEM((T, D), bf16)],
+        flops=pack_flops,
+    )
     b_own = spread(packed_b)
-    packed_g = prep_grad("own", g, aux_b)
+    outs = call(
+        prep_second_body, packed + [aux_shape], (place, ids_b, h_b, norm_gain, router_t, g), grid=(1,),
+        in_specs=[sspec(), chip(), full, vspec((1, D)), vspec((EXPERTS, D)), full], out_specs=piece_specs + [aux_spec],
+        scratch=[pltpu.VMEM((T, D), bf16)], flops=pack_flops, after=packed_b[0],
+    )
+    packed_g, aux_b = outs[:NX], outs[NX]
     g_own = spread(packed_g)
     packed_bf, aux_b_far = prep_norm("b_far", far_b, far_ids_b, packed_g[0])
     b_far = spread(packed_bf)
@@ -484,7 +516,7 @@
 
     a, b = expert(
         lift_body, [shape(F // TF, ROWS, TF, dtype=f32)] * 2, (*b_own, *b_far), (gate, up),
-        [rows_vmem, lift_vmem, lift_vmem, sems(8), one, one], 2 * mat_flops, packed_gf[0],
+        [rows_vmem, lift_vmem, lift_vmem, sems(8), sems(2), sems(2)], 2 * mat_flops, packed_gf[0],
     )
     packed_ff, aux_f_far = prep_norm("f_far", far_f, far_ids_f, a)
     f_far = spread(packed_ff)
@@ -498,7 +530,7 @@
     back_own = collect(returned[:NX])
     outputs = expert(
         forward_body, [shape(CAP, TB)] * 16, (*f_own, *f_far), (gate, up, down),
-        [rows_vmem, lift_vmem, lift_vmem, down_vmem, act_f32_vmem, act_vmem, sems(8), one, one, one],
+        [rows_vmem, lift_vmem, lift_vmem, down_vmem, act_f32_vmem, act_vmem, sems(8), sems(2), one, one],
         3 * mat_flops, returned[0],
     )
 
@@ -545,11 +577,12 @@
             compiler_params=pltpu.CompilerParams(vmem_limit_bytes=VMEM_LIMIT),
         )(*ins)
 
-    (first,) = join(join_body, 0, (next_own[0], next_far[0], last), [half, half, whole], 1, [], {})
-    fwd_next, bwd_prev = join(
-        join_last_body, 1, (next_own[1], next_far[1], first, prev_own, prev_far),
-        [half, half, whole, full, full], 2, [full], {2: 0},
-    )
+    (bwd_prev,) = call(
+        join_body, [shape(T, D)], (prev_own, prev_far), grid=(1,), in_specs=[full, full], out_specs=[full],
+        after=last,
+    )
+    (first,) = join(join_body, 0, (next_own[0], next_far[0], bwd_prev), [half, half, whole], 1, [], {})
+    (fwd_next,) = join(join_body, 1, (next_own[1], next_far[1], first), [half, half, whole], 1, [], {2: 0})
     return (fwd_next[None], bwd_prev[None])
 
 

time: 266 us -> 260 us (0.977)
  starting transfers between devices: 82.9 us -> 71.9 us
  waiting for transfers between devices: 96.5 us -> 102 us
    ppermute x18, waiting for transfers between devices: 16.9 us -> 25.8 us  [collect(): moved[dx] = lax.ppermute(pieces[dx], 'ep', ep_route(0, -dx))]
    ppermute x18, starting transfers between devices: 32.3 us -> 24.7 us  [collect(): moved[dx] = lax.ppermute(pieces[dx], 'ep', ep_route(0, -dx))]
    ppermute x6, waiting for transfers between devices: 23.7 us -> 20.8 us  [relay(): lax.ppermute(block, ('section', 'ep'), relay_route(lax.axis_size('section...]
    pallas_call x15 -> x16, Pallas kernels: 77.8 us -> 79.8 us  [call(): pl.pallas_call(body, out_shape=outs, scratch_shapes=list(scratch), cost_e...]
  transfers between devices with their start and end apart: 47 -> 47, of which waited for: 15 -> 15; matrix products, arithmetic and copies ran while one was open for 0% -> 0% of each run, Pallas kernels for 29% -> 32%
where the time goes in v3:
time: 260 us; the launch traced here: 259 us
  waiting for transfers between devices  102 us (39%)
  Pallas kernels  83.8 us (32%)
  starting transfers between devices  71.9 us (28%)
    pallas_call x16, Pallas kernels, call(): pl.pallas_call(body, out_shape=outs, scratch_shapes=list(scratch), cost_e...  79.8 us
    ppermute x5, waiting for transfers between devices, across(): return lax.ppermute(block, 'ep', ep_route(1, 0))  31.8 us
    ppermute x18, starting transfers between devices, spread(): moved[dx] = lax.ppermute(pieces[dx], 'ep', ep_route(0, dx))  28.5 us
    ppermute x18, waiting for transfers between devices, collect(): moved[dx] = lax.ppermute(pieces[dx], 'ep', ep_route(0, -dx))  25.8 us
    ppermute x18, starting transfers between devices, collect(): moved[dx] = lax.ppermute(pieces[dx], 'ep', ep_route(0, -dx))  24.7 us
    ppermute x18, waiting for transfers between devices, spread(): moved[dx] = lax.ppermute(pieces[dx], 'ep', ep_route(0, dx))  24.1 us
    ppermute x6, waiting for transfers between devices, relay(): lax.ppermute(block, ('section', 'ep'), relay_route(lax.axis_size('section...  20.8 us
    ppermute x5, starting transfers between devices, across(): return lax.ppermute(block, 'ep', ep_route(1, 0))  14.1 us
  transfers between devices with their start and end apart: 47, of which 15 were waited for; matrix products, arithmetic and copies ran while one was open for 0% of the time, Pallas kernels for 32%

profile of v3, /device:TPU:0, one launch (start us, length us, event | category | flops | bytes accessed | tf_op | source)
XLA Modules:
  0.0 259.0 jit_solution(5873446630579190294)
XLA Ops:
  0.6 4.1 %collective-permute-start.1 = (bf16[128,3584]{1,0:T(8,128)(2,1)}, bf16[128,3584]{1,0:T(8,128)(2,1)}, u32[]{:S(2)}, u32[]{:S(2)}) collective-permute-start(bf16[128,3584]{1,0:T(8,128)(2,1)} %bitcast.22), channel_id=1, source_target_pairs={{0,4},{1,5},{2,6},{3,7},{4,0},{5,1},{6,2},{7,3},{8,12},{9,13},{10,... | collective-permute-start | bytes 2752520 | tf_op jit(solution)/shard_map/ppermute | solution.py:421
  4.8 3.0 %shard_map.113 = (bf16[48,3584]{1,0:T(8,128)(2,1)}, bf16[48,3584]{1,0:T(8,128)(2,1)}, bf16[48,3584]{1,0:T(8,128)(2,1)}, bf16[48,3584]{1,0:T(8,128)(2,1)}) custom-call(s32[1]{0:T(128)} %bitcast.place_ref.refs_0_, s32[2,128]{1,0:T(2,128)} %bitcast.37, bf16[128,3584]{1,0:T(8,128)(2,1)} %bitcast.23, f32[1,3584]{1,0:T(1,128)} %refs_2_.3), custom_call_target="tpu_custom_call" | custom-call | flops 176160768 | bytes 2309124 | tf_op jit(solution)/shard_map/pallas_call | solution.py:48
  9.3 2.7 %collective-permute-start.8 = (bf16[48,3584]{1,0:T(8,128)(2,1)}, bf16[48,3584]{1,0:T(8,128)(2,1)}, u32[]{:S(2)}, u32[]{:S(2)}) collective-permute-start(bf16[48,3584]{1,0:T(8,128)(2,1)} %get-tuple-element.65), channel_id=1, source_target_pairs={{0,2},{1,3},{2,0},{3,1},{4,6},{5,7},{6,4},{7,5},{8,10},{9,11},{10,... | collective-permute-start | bytes 1032200 | tf_op jit(solution)/shard_map/ppermute | solution.py:427
  12.0 3.4 %collective-permute-start.5 = (s32[2,128]{1,0:T(2,128)}, s32[2,128]{1,0:T(2,128)}, u32[]{:S(2)}, u32[]{:S(2)}) collective-permute-start(s32[2,128]{1,0:T(2,128)} %bitcast.40), channel_id=1, source_target_pairs={{0,4},{1,5},{2,6},{3,7},{4,0},{5,1},{6,2},{7,3},{8,12},{9,13},{10,... | collective-permute-start | bytes 3080 | tf_op jit(solution)/shard_map/ppermute | solution.py:421
  15.4 29.6 %collective-permute-done.5.refs_1_ = s32[2,128]{1,0:T(2,128)} collective-permute-done((s32[2,128]{1,0:T(2,128)}, s32[2,128]{1,0:T(2,128)}, u32[]{:S(2)}, u32[]{:S(2)}) %collective-permute-start.5) | collective-permute-done | bytes 1056 | tf_op jit(solution)/shard_map/ppermute | solution.py:421
  45.1 3.2 %collective-permute-start = (s32[2,128]{1,0:T(2,128)}, s32[2,128]{1,0:T(2,128)}, u32[]{:S(2)}, u32[]{:S(2)}) collective-permute-start(s32[2,128]{1,0:T(2,128)} %bitcast.38), channel_id=1, source_target_pairs={{0,4},{1,5},{2,6},{3,7},{4,0},{5,1},{6,2},{7,3},{8,12},{9,13},{10,... | collective-permute-start | bytes 3080 | tf_op jit(solution)/shard_map/ppermute | solution.py:421
  50.5 3.2 %collective-permute-start.6 = (bf16[128,3584]{1,0:T(8,128)(2,1)}, bf16[128,3584]{1,0:T(8,128)(2,1)}, u32[]{:S(2)}, u32[]{:S(2)}) collective-permute-start(bf16[128,3584]{1,0:T(8,128)(2,1)} %bitcast.18), channel_id=1, source_target_pairs={{0,4},{1,5},{2,6},{3,7},{4,0},{5,1},{6,2},{7,3},{8,12},{9,13},{10,... | collective-permute-start | bytes 2752520 | tf_op jit(solution)/shard_map/ppermute | solution.py:421
  53.7 3.7 %shard_map.114 = (bf16[48,3584]{1,0:T(8,128)(2,1)}, bf16[48,3584]{1,0:T(8,128)(2,1)}, bf16[48,3584]{1,0:T(8,128)(2,1)}, bf16[48,3584]{1,0:T(8,128)(2,1)}, f32[8,128]{1,0:T(8,128)}) custom-call(s32[1]{0:T(128)} %bitcast.place_ref.refs_0_, s32[2,128]{1,0:T(2,128)} %bitcast.39, bf16[128,3584]{1,0:T(8,128)(2,1)} %bitcast.24, f32[1,3584]{1,0:T(1,128)} %refs_2_.3, ...), custom_call_target="tpu_custom_call" | custom-call | flops 176160768 | bytes 3632132 | tf_op jit(solution)/shard_map/pallas_call | solution.py:48
  57.4 2.8 %collective-permute-start.9 = (bf16[48,3584]{1,0:T(8,128)(2,1)}, bf16[48,3584]{1,0:T(8,128)(2,1)}, u32[]{:S(2)}, u32[]{:S(2)}) collective-permute-start(bf16[48,3584]{1,0:T(8,128)(2,1)} %get-tuple-element.66), channel_id=1, source_target_pairs={{0,3},{1,0},{2,1},{3,2},{4,7},{5,4},{6,5},{7,6},{8,11},{9,8},{10,9... | collective-permute-start | bytes 1032200 | tf_op jit(solution)/shard_map/ppermute | solution.py:427
  62.5 3.2 %shard_map.115 = (bf16[48,3584]{1,0:T(8,128)(2,1)}, bf16[48,3584]{1,0:T(8,128)(2,1)}, bf16[48,3584]{1,0:T(8,128)(2,1)}, bf16[48,3584]{1,0:T(8,128)(2,1)}, f32[8,128]{1,0:T(8,128)}) custom-call(s32[1]{0:T(128)} %bitcast.place_ref.refs_0_, s32[2,128]{1,0:T(2,128)} %collective-permute-done.refs_1_, ...), custom_call_target="tpu_custom_call" | custom-call | flops 176160768 | bytes 2714628 | tf_op jit(solution)/shard_map/pallas_call | solution.py:48
  65.7 11.9 %collective-permute-done.9.refs_3_ = bf16[48,3584]{1,0:T(8,128)(2,1)} collective-permute-done((bf16[48,3584]{1,0:T(8,128)(2,1)}, bf16[48,3584]{1,0:T(8,128)(2,1)}, u32[]{:S(2)}, u32[]{:S(2)}) %collective-permute-start.9) | collective-permute-done | bytes 344096 | tf_op jit(solution)/shard_map/ppermute | solution.py:427
  78.7 4.1 %collective-permute-start.11 = (bf16[48,3584]{1,0:T(8,128)(2,1)}, bf16[48,3584]{1,0:T(8,128)(2,1)}, u32[]{:S(2)}, u32[]{:S(2)}) collective-permute-start(bf16[48,3584]{1,0:T(8,128)(2,1)} %get-tuple-element.68), channel_id=1, source_target_pairs={{0,2},{1,3},{2,0},{3,1},{4,6},{5,7},{6,4},{7,5},{8,10},{9,11},{10,... | collective-permute-start | bytes 1032200 | tf_op jit(solution)/shard_map/ppermute | solution.py:427
  82.8 3.2 %shard_map.116 = (bf16[48,3584]{1,0:T(8,128)(2,1)}, bf16[48,3584]{1,0:T(8,128)(2,1)}, bf16[48,3584]{1,0:T(8,128)(2,1)}, bf16[48,3584]{1,0:T(8,128)(2,1)}, f32[8,128]{1,0:T(8,128)}) custom-call(s32[1]{0:T(128)} %bitcast.place_ref.refs_0_, s32[2,128]{1,0:T(2,128)} %bitcast.41, bf16[128,3584]{1,0:T(8,128)(2,1)} %bitcast.19, f32[1,3584]{1,0:T(1,128)} %refs_2_.3, ...), custom_call_target="tpu_custom_call" | custom-call | flops 176160768 | bytes 2714628 | tf_op jit(solution)/shard_map/pallas_call | solution.py:48
  86.0 2.7 %shard_map.117 = (bf16[48,3584]{1,0:T(8,128)(2,1)}, bf16[48,3584]{1,0:T(8,128)(2,1)}, bf16[48,3584]{1,0:T(8,128)(2,1)}, bf16[48,3584]{1,0:T(8,128)(2,1)}) custom-call(f32[8,128]{1,0:T(8,128)} %get-tuple-element.70.refs_0_, bf16[128,3584]{1,0:T(8,128)(2,1)} %collective-permute-done.13.refs_1_, bf16[48,3584]{1,0:T(8,128)(2,1)} %get-tuple-element.60.refs_2_.refs_0_), custom_call_target="tpu_custom_call" | custom-call | flops 176160768 | bytes 2641920 | tf_op jit(solution)/shard_map/pallas_call | solution.py:48
  92.8 6.6 %collective-permute-done.11.refs_6_ = bf16[48,3584]{1,0:T(8,128)(2,1)} collective-permute-done((bf16[48,3584]{1,0:T(8,128)(2,1)}, bf16[48,3584]{1,0:T(8,128)(2,1)}, u32[]{:S(2)}, u32[]{:S(2)}) %collective-permute-start.11) | collective-permute-done | bytes 344096 | tf_op jit(solution)/shard_map/ppermute | solution.py:427
  101.5 11.1 %shard_map.118 = (f32[2,384,512]{2,1,0:T(8,128)}, f32[2,384,512]{2,1,0:T(8,128)}) custom-call(bf16[48,3584]{1,0:T(8,128)(2,1)} %get-tuple-element.56.refs_6_.refs_0_, bf16[48,3584]{1,0:T(8,128)(2,1)} %collective-permute-done.7.refs_1_, bf16[48,3584]{1,0:T(8,128)(2,1)} %collective-permute-done.8.refs_2_, bf16[48,3584]{1,0:T(8,128)(2,1)} %collective-permute-done.9.refs_3_, ...), custom_call_target="tpu_custom_call" | custom-call | flops 5637144576 | bytes 20922368 | tf_op jit(solution)/shard_map/pallas_call | solution.py:48
  112.6 3.2 %shard_map.119 = (bf16[48,3584]{1,0:T(8,128)(2,1)}, bf16[48,3584]{1,0:T(8,128)(2,1)}, bf16[48,3584]{1,0:T(8,128)(2,1)}, bf16[48,3584]{1,0:T(8,128)(2,1)}, f32[8,128]{1,0:T(8,128)}) custom-call(s32[1]{0:T(128)} %bitcast.place_ref.refs_0_, s32[2,128]{1,0:T(2,128)} %collective-permute-done.5.refs_1_, bf16[128,3584]{1,0:T(8,128)(2,1)} %collective-permute-done.6.refs_2_.refs_5_, ...), custom_call_target="tpu_custom_call" | custom-call | flops 176160768 | bytes 3943428 | tf_op jit(solution)/shard_map/pallas_call | solution.py:48
  122.6 4.2 %collective-permute-start.16 = (bf16[48,3584]{1,0:T(8,128)(2,1)}, bf16[48,3584]{1,0:T(8,128)(2,1)}, u32[]{:S(2)}, u32[]{:S(2)}) collective-permute-start(bf16[48,3584]{1,0:T(8,128)(2,1)} %get-tuple-element.76), channel_id=1, source_target_pairs={{0,3},{1,0},{2,1},{3,2},{4,7},{5,4},{6,5},{7,6},{8,11},{9,8},{10,9... | collective-permute-start | bytes 1032200 | tf_op jit(solution)/shard_map/ppermute | solution.py:427
  126.8 15.5 %shard_map.120 = (bf16[48,3712]{1,0:T(8,128)(2,1)}, bf16[48,3712]{1,0:T(8,128)(2,1)}, bf16[48,3712]{1,0:T(8,128)(2,1)}, bf16[48,3712]{1,0:T(8,128)(2,1)}, bf16[4...) custom-call(bf16[48,3584]{1,0:T(8,128)(2,1)} %get-tuple-element.57.refs_5_.r, ...), custom_call_target="tpu_custom_call" | custom-call | flops 8455716864 | bytes 31113216 | tf_op jit(solution)/shard_map/pallas_call | solution.py:48
  147.1 13.7 %shard_map.121 = (bf16[48,1792]{1,0:T(8,128)(2,1)}, bf16[48,1792]{1,0:T(8,128)(2,1)}, bf16[48,1792]{1,0:T(8,128)(2,1)}, bf16[48,1792]{1,0:T(8,128)(2,1)}, bf16[4...) custom-call(bf16[48,3584]{1,0:T(8,128)(2,1)} %get-tuple-element.60.r, ...), custom_call_target="tpu_custom_call" | custom-call | flops 8455716864 | bytes 27881472 | tf_op jit(solution)/shard_map/pallas_call | solution.py:48
  160.9 3.4 %collective-permute-start.32 = (bf16[48,1792]{1,0:T(8,128)(2,1)}, bf16[48,1792]{1,0:T(8,128)(2,1)}, u32[]{:S(2)}, u32[]{:S(2)}) collective-permute-start(bf16[48,1792]{1,0:T(8,128)(2,1)} %get-tuple-element.99), channel_id=1, source_target_pairs={{0,3},{1,0},{2,1},{3,2},{4,7},{5,4},{6,5},{7,6},{8,11},{9,8},{10,9... | collective-permute-start | bytes 516104 | tf_op jit(solution)/shard_map/ppermute | solution.py:434
  167.8 3.7 %shard_map.122.refs_6_ = bf16[128,3584]{1,0:T(8,128)(2,1)} custom-call(f32[8,128]{1,0:T(8,128)} %get-tuple-element.70.refs_0_, bf16[128,3584]{1,0:T(8,128)(2,1)} %collective-permute-done.1.refs_2_.refs_1_.refs_8_, f32[1,3584]{1,0:T(1,128)} %refs_2_.3, bf16[8,3584]{1,0:T(8,128)(2,1)} %bitcast.35, bf16[48,3712]{1,0:T(8,128)(2,1)} %get-tuple-element.106.refs_4_, ...), custom_call_target="tpu_custom_call" | custom-call | flops 352321536 | bytes 4425728 | tf_op jit(solution)/shard_map/pallas_call | solution.py:48
  177.5 10.5 %collective-permute-done.37.refs_4_ = bf16[48,1792]{1,0:T(8,128)(2,1)} collective-permute-done((bf16[48,1792]{1,0:T(8,128)(2,1)}, bf16[48,1792]{1,0:T(8,128)(2,1)}, u32[]{:S(2)}, u32[]{:S(2)}) %collective-permute-start.37) | collective-permute-done | bytes 172064 | tf_op jit(solution)/shard_map/ppermute | solution.py:434
  190.5 8.5 %collective-permute-done.34.refs_4_ = bf16[48,1792]{1,0:T(8,128)(2,1)} collective-permute-done((bf16[48,1792]{1,0:T(8,128)(2,1)}, bf16[48,1792]{1,0:T(8,128)(2,1)}, u32[]{:S(2)}, u32[]{:S(2)}) %collective-permute-start.34) | collective-permute-done | bytes 172064 | tf_op jit(solution)/shard_map/ppermute | solution.py:434
  201.4 4.1 %shard_map.125.refs_6_ = bf16[128,3584]{1,0:T(8,128)(2,1)} custom-call(f32[8,128]{1,0:T(8,128)} %get-tuple-element.93.refs_0_, bf16[128,3584]{1,0:T(8,128)(2,1)} %bitcast.25, f32[1,3584]{1,0:T(1,128)} %refs_2_.3, bf16[8,3584]{1,0:T(8,128)(2,1)} %bitcast.36, bf16[48,3712]{1,0:T(8,128)(2,1)} %get-tuple-element.84.refs_11_.refs_4_, ...), custom_call_target="tpu_custom_call" | custom-call | flops 352321536 | bytes 4712448 | tf_op jit(solution)/shard_map/pallas_call | solution.py:48
  205.5 2.8 %collective-permute-start.45 = (bf16[128,3584]{1,0:T(8,128)(2,1)}, bf16[128,3584]{1,0:T(8,128)(2,1)}, u32[]{:S(2)}, u32[]{:S(2)}) collective-permute-start(bf16[128,3584]{1,0:T(8,128)(2,1)} %shard_map.125.refs_6_), channel_id=1, source_target_pairs={{0,120},{1,121},{2,122},{3,123},{4,124},{5,125},{6,126},{7,127},{8... | collective-permute-start | bytes 2752520 | tf_op jit(solution)/shard_map/ppermute | solution.py:439
  210.6 4.9 %collective-permute-done.26.refs_2_ = bf16[48,1792]{1,0:T(8,128)(2,1)} collective-permute-done((bf16[48,1792]{1,0:T(8,128)(2,1)}, bf16[48,1792]{1,0:T(8,128)(2,1)}, u32[]{:S(2)}, u32[]{:S(2)}) %collective-permute-start.26) | collective-permute-done | bytes 172064 | tf_op jit(solution)/shard_map/ppermute | solution.py:434
  222.6 2.6 %shard_map.126.refs_6_ = bf16[128,1792]{1,0:T(8,128)(2,1)} custom-call(f32[8,128]{1,0:T(8,128)} %get-tuple-element.59.refs_0_, bf16[48,1792]{1,0:T(8,128)(2,1)} %get-tuple-element.89.refs_9_.refs_1_, bf16[48,1792]{1,0:T(8,128)(2,1)} %collective-permute-done.26.refs_2_, bf16[48,1792]{1,0:T(8,128)(2,1)} %collective-permute-done.27.refs_3_, ...), custom_call_target="tpu_custom_call" | custom-call | flops 176160768 | bytes 2985984 | tf_op jit(solution)/shard_map/pallas_call | solution.py:48
  227.1 2.6 %shard_map.127.refs_2_ = bf16[128,1792]{1,0:T(8,128)(2,1)} custom-call(f32[8,128]{1,0:T(8,128)} %get-tuple-element.59.refs_0_, bf16[48,1792]{1,0:T(8,128)(2,1)} %get-tuple-element.85.refs_1_, bf16[48,1792]{1,0:T(8,128)(2,1)} %collective-permute-done.23.refs_2_, bf16[48,1792]{1,0:T(8,128)(2,1)} %collective-permute-done.24.refs_3_, ...), custom_call_target="tpu_custom_call" | custom-call | flops 176160768 | bytes 2527232 | tf_op jit(solution)/shard_map/pallas_call | solution.py:48
  234.2 8.4 %collective-permute-done.43.a_ref = bf16[128,1792]{1,0:T(8,128)(2,1)} collective-permute-done((bf16[128,1792]{1,0:T(8,128)(2,1)}, bf16[128,1792]{1,0:T(8,128)(2,1)}, u32[]{:S(2)}, u32[]{:S(2)}) %collective-permute-start.43) | collective-permute-done | bytes 458784 | tf_op jit(solution)/shard_map/ppermute | solution.py:439
  244.6 2.9 %collective-permute-done.41.a_ref = bf16[128,1792]{1,0:T(8,128)(2,1)} collective-permute-done((bf16[128,1792]{1,0:T(8,128)(2,1)}, bf16[128,1792]{1,0:T(8,128)(2,1)}, u32[]{:S(2)}, u32[]{:S(2)}) %collective-permute-start.41) | collective-permute-done | bytes 458784 | tf_op jit(solution)/shard_map/ppermute | solution.py:439
  247.5 9.5 %collective-permute-done.42.b_ref = bf16[128,1792]{1,0:T(8,128)(2,1)} collective-permute-done((bf16[128,1792]{1,0:T(8,128)(2,1)}, bf16[128,1792]{1,0:T(8,128)(2,1)}, u32[]{:S(2)}, u32[]{:S(2)}) %collective-permute-start.42) | collective-permute-done | bytes 458784 | tf_op jit(solution)/shard_map/ppermute | solution.py:439
  (80 shorter events, 59.1 us)
Async XLA Ops:
  0.6 59.6 %collective-permute-start.1 = (bf16[128,3584]{1,0:T(8,128)(2,1)}, bf16[128,3584]{1,0:T(8,128)(2,1)}, u32[]{:S(2)}, u32[]{:S(2)}) collective-permute-start(bf16[128,3584]{1,0:T(8,128)(2,1)} %bitcast.22), channel_id=1, source_target_pairs={{0,4},{1,5},{2,6},{3,7},{4,0},{5,1},{6,2},{7,3},{8,12},{9,13},{10,... | collective-permute-start | bytes 2752520 | tf_op jit(solution)/shard_map/ppermute | solution.py:421
  4.7 78.1 %collective-permute-start.13 = (bf16[128,3584]{1,0:T(8,128)(2,1)}, bf16[128,3584]{1,0:T(8,128)(2,1)}, u32[]{:S(2)}, u32[]{:S(2)}) collective-permute-start(bf16[128,3584]{1,0:T(8,128)(2,1)} %bitcast.26), channel_id=1, source_target_pairs={{0,4},{1,5},{2,6},{3,7},{4,0},{5,1},{6,2},{7,3},{8,12},{9,13},{10,... | collective-permute-start | bytes 2752520 | tf_op jit(solution)/shard_map/ppermute | solution.py:421
  7.8 49.6 %collective-permute-start.7 = (bf16[48,3584]{1,0:T(8,128)(2,1)}, bf16[48,3584]{1,0:T(8,128)(2,1)}, u32[]{:S(2)}, u32[]{:S(2)}) collective-permute-start(bf16[48,3584]{1,0:T(8,128)(2,1)} %get-tuple-element.64), channel_id=1, source_target_pairs={{0,1},{1,2},{2,3},{3,0},{4,5},{5,6},{6,7},{7,4},{8,9},{9,10},{10,1... | collective-permute-start | bytes 1032200 | tf_op jit(solution)/shard_map/ppermute | solution.py:427
  9.3 50.9 %collective-permute-start.8 = (bf16[48,3584]{1,0:T(8,128)(2,1)}, bf16[48,3584]{1,0:T(8,128)(2,1)}, u32[]{:S(2)}, u32[]{:S(2)}) collective-permute-start(bf16[48,3584]{1,0:T(8,128)(2,1)} %get-tuple-element.65), channel_id=1, source_target_pairs={{0,2},{1,3},{2,0},{3,1},{4,6},{5,7},{6,4},{7,5},{8,10},{9,11},{10,... | collective-permute-start | bytes 1032200 | tf_op jit(solution)/shard_map/ppermute | solution.py:427
  12.0 33.1 %collective-permute-start.5 = (s32[2,128]{1,0:T(2,128)}, s32[2,128]{1,0:T(2,128)}, u32[]{:S(2)}, u32[]{:S(2)}) collective-permute-start(s32[2,128]{1,0:T(2,128)} %bitcast.40), channel_id=1, source_target_pairs={{0,4},{1,5},{2,6},{3,7},{4,0},{5,1},{6,2},{7,3},{8,12},{9,13},{10,... | collective-permute-start | bytes 3080 | tf_op jit(solution)/shard_map/ppermute | solution.py:421
  50.5 38.9 %collective-permute-start.6 = (bf16[128,3584]{1,0:T(8,128)(2,1)}, bf16[128,3584]{1,0:T(8,128)(2,1)}, u32[]{:S(2)}, u32[]{:S(2)}) collective-permute-start(bf16[128,3584]{1,0:T(8,128)(2,1)} %bitcast.18), channel_id=1, source_target_pairs={{0,4},{1,5},{2,6},{3,7},{4,0},{5,1},{6,2},{7,3},{8,12},{9,13},{10,... | collective-permute-start | bytes 2752520 | tf_op jit(solution)/shard_map/ppermute | solution.py:421
  57.4 20.2 %collective-permute-start.9 = (bf16[48,3584]{1,0:T(8,128)(2,1)}, bf16[48,3584]{1,0:T(8,128)(2,1)}, u32[]{:S(2)}, u32[]{:S(2)}) collective-permute-start(bf16[48,3584]{1,0:T(8,128)(2,1)} %get-tuple-element.66), channel_id=1, source_target_pairs={{0,3},{1,0},{2,1},{3,2},{4,7},{5,4},{6,5},{7,6},{8,11},{9,8},{10,9... | collective-permute-start | bytes 1032200 | tf_op jit(solution)/shard_map/ppermute | solution.py:427
  60.2 18.5 %collective-permute-start.17 = (bf16[48,3584]{1,0:T(8,128)(2,1)}, bf16[48,3584]{1,0:T(8,128)(2,1)}, u32[]{:S(2)}, u32[]{:S(2)}) collective-permute-start(bf16[48,3584]{1,0:T(8,128)(2,1)} %get-tuple-element.77), channel_id=1, source_target_pairs={{0,1},{1,2},{2,3},{3,0},{4,5},{5,6},{6,7},{7,4},{8,9},{9,10},{10,1... | collective-permute-start | bytes 1032200 | tf_op jit(solution)/shard_map/ppermute | solution.py:427
  60.2 28.6 %collective-permute-start.18 = (bf16[48,3584]{1,0:T(8,128)(2,1)}, bf16[48,3584]{1,0:T(8,128)(2,1)}, u32[]{:S(2)}, u32[]{:S(2)}) collective-permute-start(bf16[48,3584]{1,0:T(8,128)(2,1)} %get-tuple-element.78), channel_id=1, source_target_pairs={{0,2},{1,3},{2,0},{3,1},{4,6},{5,7},{6,4},{7,5},{8,10},{9,11},{10,... | collective-permute-start | bytes 1032200 | tf_op jit(solution)/shard_map/ppermute | solution.py:427
  78.7 20.8 %collective-permute-start.11 = (bf16[48,3584]{1,0:T(8,128)(2,1)}, bf16[48,3584]{1,0:T(8,128)(2,1)}, u32[]{:S(2)}, u32[]{:S(2)}) collective-permute-start(bf16[48,3584]{1,0:T(8,128)(2,1)} %get-tuple-element.68), channel_id=1, source_target_pairs={{0,2},{1,3},{2,0},{3,1},{4,6},{5,7},{6,4},{7,5},{8,10},{9,11},{10,... | collective-permute-start | bytes 1032200 | tf_op jit(solution)/shard_map/ppermute | solution.py:427
  88.8 27.0 %collective-permute-start.19 = (bf16[48,3584]{1,0:T(8,128)(2,1)}, bf16[48,3584]{1,0:T(8,128)(2,1)}, u32[]{:S(2)}, u32[]{:S(2)}) collective-permute-start(bf16[48,3584]{1,0:T(8,128)(2,1)} %get-tuple-element.79), channel_id=1, source_target_pairs={{0,3},{1,0},{2,1},{3,2},{4,7},{5,4},{6,5},{7,6},{8,11},{9,8},{10,9... | collective-permute-start | bytes 1032200 | tf_op jit(solution)/shard_map/ppermute | solution.py:427
  89.4 27.9 %collective-permute-start.2 = (bf16[48,3584]{1,0:T(8,128)(2,1)}, bf16[48,3584]{1,0:T(8,128)(2,1)}, u32[]{:S(2)}, u32[]{:S(2)}) collective-permute-start(bf16[48,3584]{1,0:T(8,128)(2,1)} %get-tuple-element.61), channel_id=1, source_target_pairs={{0,1},{1,2},{2,3},{3,0},{4,5},{5,6},{6,7},{7,4},{8,9},{9,10},{10,1... | collective-permute-start | bytes 1032200 | tf_op jit(solution)/shard_map/ppermute | solution.py:427
  90.9 28.3 %collective-permute-start.20 = (bf16[48,3584]{1,0:T(8,128)(2,1)}, bf16[48,3584]{1,0:T(8,128)(2,1)}, u32[]{:S(2)}, u32[]{:S(2)}) collective-permute-start(bf16[48,3584]{1,0:T(8,128)(2,1)} %get-tuple-element.80), channel_id=1, source_target_pairs={{0,1},{1,2},{2,3},{3,0},{4,5},{5,6},{6,7},{7,4},{8,9},{9,10},{10,1... | collective-permute-start | bytes 1032200 | tf_op jit(solution)/shard_map/ppermute | solution.py:427
  99.5 19.8 %collective-permute-start.21 = (bf16[48,3584]{1,0:T(8,128)(2,1)}, bf16[48,3584]{1,0:T(8,128)(2,1)}, u32[]{:S(2)}, u32[]{:S(2)}) collective-permute-start(bf16[48,3584]{1,0:T(8,128)(2,1)} %get-tuple-element.81), channel_id=1, source_target_pairs={{0,2},{1,3},{2,0},{3,1},{4,6},{5,7},{6,4},{7,5},{8,10},{9,11},{10,... | collective-permute-start | bytes 1032200 | tf_op jit(solution)/shard_map/ppermute | solution.py:427
  99.5 23.1 %collective-permute-start.22 = (bf16[48,3584]{1,0:T(8,128)(2,1)}, bf16[48,3584]{1,0:T(8,128)(2,1)}, u32[]{:S(2)}, u32[]{:S(2)}) collective-permute-start(bf16[48,3584]{1,0:T(8,128)(2,1)} %get-tuple-element.82), channel_id=1, source_target_pairs={{0,3},{1,0},{2,1},{3,2},{4,7},{5,4},{6,5},{7,6},{8,11},{9,8},{10,9... | collective-permute-start | bytes 1032200 | tf_op jit(solution)/shard_map/ppermute | solution.py:427
  115.8 26.4 %collective-permute-start.3 = (bf16[48,3584]{1,0:T(8,128)(2,1)}, bf16[48,3584]{1,0:T(8,128)(2,1)}, u32[]{:S(2)}, u32[]{:S(2)}) collective-permute-start(bf16[48,3584]{1,0:T(8,128)(2,1)} %get-tuple-element.62), channel_id=1, source_target_pairs={{0,2},{1,3},{2,0},{3,1},{4,6},{5,7},{6,4},{7,5},{8,10},{9,11},{10,... | collective-permute-start | bytes 1032200 | tf_op jit(solution)/shard_map/ppermute | solution.py:427
  117.3 25.0 %collective-permute-start.4 = (bf16[48,3584]{1,0:T(8,128)(2,1)}, bf16[48,3584]{1,0:T(8,128)(2,1)}, u32[]{:S(2)}, u32[]{:S(2)}) collective-permute-start(bf16[48,3584]{1,0:T(8,128)(2,1)} %get-tuple-element.63), channel_id=1, source_target_pairs={{0,3},{1,0},{2,1},{3,2},{4,7},{5,4},{6,5},{7,6},{8,11},{9,8},{10,9... | collective-permute-start | bytes 1032200 | tf_op jit(solution)/shard_map/ppermute | solution.py:427
  119.2 23.2 %collective-permute-start.14 = (bf16[48,3584]{1,0:T(8,128)(2,1)}, bf16[48,3584]{1,0:T(8,128)(2,1)}, u32[]{:S(2)}, u32[]{:S(2)}) collective-permute-start(bf16[48,3584]{1,0:T(8,128)(2,1)} %get-tuple-element.74), channel_id=1, source_target_pairs={{0,1},{1,2},{2,3},{3,0},{4,5},{5,6},{6,7},{7,4},{8,9},{9,10},{10,1... | collective-permute-start | bytes 1032200 | tf_op jit(solution)/shard_map/ppermute | solution.py:427
  119.3 25.3 %collective-permute-start.15 = (bf16[48,3584]{1,0:T(8,128)(2,1)}, bf16[48,3584]{1,0:T(8,128)(2,1)}, u32[]{:S(2)}, u32[]{:S(2)}) collective-permute-start(bf16[48,3584]{1,0:T(8,128)(2,1)} %get-tuple-element.75), channel_id=1, source_target_pairs={{0,2},{1,3},{2,0},{3,1},{4,6},{5,7},{6,4},{7,5},{8,10},{9,11},{10,... | collective-permute-start | bytes 1032200 | tf_op jit(solution)/shard_map/ppermute | solution.py:427
  122.6 24.6 %collective-permute-start.16 = (bf16[48,3584]{1,0:T(8,128)(2,1)}, bf16[48,3584]{1,0:T(8,128)(2,1)}, u32[]{:S(2)}, u32[]{:S(2)}) collective-permute-start(bf16[48,3584]{1,0:T(8,128)(2,1)} %get-tuple-element.76), channel_id=1, source_target_pairs={{0,3},{1,0},{2,1},{3,2},{4,7},{5,4},{6,5},{7,6},{8,11},{9,8},{10,9... | collective-permute-start | bytes 1032200 | tf_op jit(solution)/shard_map/ppermute | solution.py:427
  142.2 22.6 %collective-permute-start.38 = (bf16[48,3712]{1,0:T(8,128)(2,1)}, bf16[48,3712]{1,0:T(8,128)(2,1)}, u32[]{:S(2)}, u32[]{:S(2)}) collective-permute-start(bf16[48,3712]{1,0:T(8,128)(2,1)} %get-tuple-element.107), channel_id=1, source_target_pairs={{0,3},{1,0},{2,1},{3,2},{4,7},{5,4},{6,5},{7,6},{8,11},{9,8},{10,9... | collective-permute-start | bytes 1069064 | tf_op jit(solution)/shard_map/ppermute | solution.py:434
  142.3 23.3 %collective-permute-start.39 = (bf16[48,3712]{1,0:T(8,128)(2,1)}, bf16[48,3712]{1,0:T(8,128)(2,1)}, u32[]{:S(2)}, u32[]{:S(2)}) collective-permute-start(bf16[48,3712]{1,0:T(8,128)(2,1)} %get-tuple-element.108), channel_id=1, source_target_pairs={{0,2},{1,3},{2,0},{3,1},{4,6},{5,7},{6,4},{7,5},{8,10},{9,11},{10,... | collective-permute-start | bytes 1069064 | tf_op jit(solution)/shard_map/ppermute | solution.py:434
  142.4 25.4 %collective-permute-start.40 = (bf16[48,3712]{1,0:T(8,128)(2,1)}, bf16[48,3712]{1,0:T(8,128)(2,1)}, u32[]{:S(2)}, u32[]{:S(2)}) collective-permute-start(bf16[48,3712]{1,0:T(8,128)(2,1)} %get-tuple-element.109), channel_id=1, source_target_pairs={{0,1},{1,2},{2,3},{3,0},{4,5},{5,6},{6,7},{7,4},{8,9},{9,10},{10,1... | collective-permute-start | bytes 1069064 | tf_op jit(solution)/shard_map/ppermute | solution.py:434
  171.5 58.2 %collective-permute-start.46 = (bf16[128,3584]{1,0:T(8,128)(2,1)}, bf16[128,3584]{1,0:T(8,128)(2,1)}, u32[]{:S(2)}, u32[]{:S(2)}) collective-permute-start(bf16[128,3584]{1,0:T(8,128)(2,1)} %shard_map.122.refs_6_), channel_id=1, source_target_pairs={{0,124},{1,125},{2,126},{3,127},{4,120},{5,121},{6,122},{7,123},{8... | collective-permute-start | bytes 2752520 | tf_op jit(solution)/shard_map/ppermute | solution.py:439
  172.9 28.4 %collective-permute-start.29 = (bf16[48,3712]{1,0:T(8,128)(2,1)}, bf16[48,3712]{1,0:T(8,128)(2,1)}, u32[]{:S(2)}, u32[]{:S(2)}) collective-permute-start(bf16[48,3712]{1,0:T(8,128)(2,1)} %get-tuple-element.94), channel_id=1, source_target_pairs={{0,3},{1,0},{2,1},{3,2},{4,7},{5,4},{6,5},{7,6},{8,11},{9,8},{10,9... | collective-permute-start | bytes 1069064 | tf_op jit(solution)/shard_map/ppermute | solution.py:434
  174.9 26.5 %collective-permute-start.30 = (bf16[48,3712]{1,0:T(8,128)(2,1)}, bf16[48,3712]{1,0:T(8,128)(2,1)}, u32[]{:S(2)}, u32[]{:S(2)}) collective-permute-start(bf16[48,3712]{1,0:T(8,128)(2,1)} %get-tuple-element.95), channel_id=1, source_target_pairs={{0,2},{1,3},{2,0},{3,1},{4,6},{5,7},{6,4},{7,5},{8,10},{9,11},{10,... | collective-permute-start | bytes 1069064 | tf_op jit(solution)/shard_map/ppermute | solution.py:434
  175.1 26.3 %collective-permute-start.31 = (bf16[48,3712]{1,0:T(8,128)(2,1)}, bf16[48,3712]{1,0:T(8,128)(2,1)}, u32[]{:S(2)}, u32[]{:S(2)}) collective-permute-start(bf16[48,3712]{1,0:T(8,128)(2,1)} %get-tuple-element.96), channel_id=1, source_target_pairs={{0,1},{1,2},{2,3},{3,0},{4,5},{5,6},{6,7},{7,4},{8,9},{9,10},{10,1... | collective-permute-start | bytes 1069064 | tf_op jit(solution)/shard_map/ppermute | solution.py:434
  205.5 26.1 %collective-permute-start.45 = (bf16[128,3584]{1,0:T(8,128)(2,1)}, bf16[128,3584]{1,0:T(8,128)(2,1)}, u32[]{:S(2)}, u32[]{:S(2)}) collective-permute-start(bf16[128,3584]{1,0:T(8,128)(2,1)} %shard_map.125.refs_6_), channel_id=1, source_target_pairs={{0,120},{1,121},{2,122},{3,123},{4,124},{5,125},{6,126},{7,127},{8... | collective-permute-start | bytes 2752520 | tf_op jit(solution)/shard_map/ppermute | solution.py:439
  225.2 17.4 %collective-permute-start.44 = (bf16[128,1792]{1,0:T(8,128)(2,1)}, bf16[128,1792]{1,0:T(8,128)(2,1)}, u32[]{:S(2)}, u32[]{:S(2)}) collective-permute-start(bf16[128,1792]{1,0:T(8,128)(2,1)} %shard_map.123.refs_6_), channel_id=1, source_target_pairs={{0,12},{1,13},{2,14},{3,15},{4,8},{5,9},{6,10},{7,11},{8,20},{9,21... | collective-permute-start | bytes 1376264 | tf_op jit(solution)/shard_map/ppermute | solution.py:439
  225.2 17.4 %collective-permute-start.43 = (bf16[128,1792]{1,0:T(8,128)(2,1)}, bf16[128,1792]{1,0:T(8,128)(2,1)}, u32[]{:S(2)}, u32[]{:S(2)}) collective-permute-start(bf16[128,1792]{1,0:T(8,128)(2,1)} %shard_map.126.refs_6_), channel_id=1, source_target_pairs={{0,8},{1,9},{2,10},{3,11},{4,12},{5,13},{6,14},{7,15},{8,16},{9,17... | collective-permute-start | bytes 1376264 | tf_op jit(solution)/shard_map/ppermute | solution.py:439
  229.8 17.8 %collective-permute-start.41 = (bf16[128,1792]{1,0:T(8,128)(2,1)}, bf16[128,1792]{1,0:T(8,128)(2,1)}, u32[]{:S(2)}, u32[]{:S(2)}) collective-permute-start(bf16[128,1792]{1,0:T(8,128)(2,1)} %shard_map.127.refs_2_), channel_id=1, source_target_pairs={{0,8},{1,9},{2,10},{3,11},{4,12},{5,13},{6,14},{7,15},{8,16},{9,17... | collective-permute-start | bytes 1376264 | tf_op jit(solution)/shard_map/ppermute | solution.py:439
  229.8 27.2 %collective-permute-start.42 = (bf16[128,1792]{1,0:T(8,128)(2,1)}, bf16[128,1792]{1,0:T(8,128)(2,1)}, u32[]{:S(2)}, u32[]{:S(2)}) collective-permute-start(bf16[128,1792]{1,0:T(8,128)(2,1)} %shard_map.124.refs_9_), channel_id=1, source_target_pairs={{0,12},{1,13},{2,14},{3,15},{4,8},{5,9},{6,10},{7,11},{8,20},{9,21... | collective-permute-start | bytes 1376264 | tf_op jit(solution)/shard_map/ppermute | solution.py:439
  (15 other events, 151.5 us)

commit v4 on v3

--- a/solution.py
+++ b/solution.py
@@ -20,7 +20,7 @@
 ROWS = NX * NZ * CAP
 TF = 512
 TB = 1792
-TD = 512
+TD = 256
 VMEM_LIMIT = 67043328
 EXT = 128
 f32 = jnp.float32
@@ -358,8 +358,12 @@
     refs[-1][...] = (a_ref[...].astype(f32) + b_ref[...].astype(f32)).astype(bf16)
 
 
-def grad_input_body(with_input, aux_ref, hidden_ref, gain_ref, router_ref, *refs):
-    pieces, base_ref, out_ref, rows_ref, scaled_ref = refs[:NX], refs[NX], refs[NX + 1], refs[NX + 2], refs[NX + 3]
+def grad_input_body(own, aux_ref, hidden_ref, gain_ref, *refs):
+    pieces, refs = refs[:NX], refs[NX:]
+    if own:
+        router_ref, base_ref, far_pulls_ref, out_ref, rows_ref, scaled_ref = refs
+    else:
+        out_ref, pulls_ref, rows_ref, scaled_ref = refs
     stack_pieces(pieces, rows_ref)
     aux = aux_ref[...]
     hits = [jnp.where(hit, 1.0, 0.0) for hit in hits_of([aux[0:1], aux[1:2]], 256)]
@@ -368,18 +372,20 @@
     for hit in hits:
         found = jnp.dot(extra, hit.astype(bf16), preferred_element_type=f32)
         pulls.append(found[0:1] + found[1:2])
-    router = router_ref[...]
-    rows_ref[NX * CAP : NX * CAP + 16, :D] = jnp.concatenate([router, router], axis=0)
-    slot = rows_iota(256)
-    high = jnp.zeros((256, T), f32)
-    low = jnp.zeros((256, T), f32)
-    for k in range(2):
-        weight, score, name = aux[2 + k : 3 + k], aux[4 + k : 5 + k], aux[6 + k : 7 + k].astype(jnp.int32)
-        term = (pulls[k] - weight * (pulls[0] + pulls[1])) * (1.0 - score)
-        first = term.astype(bf16).astype(f32)
-        high = high + jnp.where(slot == name + NX * CAP, first, 0.0)
-        low = low + jnp.where(slot == name + NX * CAP + EXPERTS, term - first, 0.0)
-    mixing = jnp.transpose(hits[0] + hits[1] + high + low).astype(bf16)
+    mixing = hits[0] + hits[1]
+    if own:
+        pulls = [pulls[k] + far_pulls_ref[k : k + 1, :] for k in range(2)]
+        rows_ref[NX * CAP : NX * CAP + 16, :D] = jnp.concatenate([router_ref[...]] * 2, axis=0)
+        slot = rows_iota(256)
+        for k in range(2):
+            weight, score, name = aux[2 + k : 3 + k], aux[4 + k : 5 + k], aux[6 + k : 7 + k].astype(jnp.int32)
+            d_logit = (pulls[k] - weight * (pulls[0] + pulls[1])) * (1.0 - score)
+            mixing = mixing + jnp.where(slot == name + NX * CAP, d_logit, 0.0)
+    else:
+        for k in range(2):
+            pulls_ref[k : k + 1, :] = pulls[k]
+        pulls_ref[2:, :] = jnp.zeros((EXPERTS - 2, T), f32)
+    mixing = jnp.transpose(mixing).astype(bf16)
     inverse = inverse_of(hidden_ref)
 
     def scale_tile(cols, against):
@@ -392,7 +398,7 @@
 
     def out_tile(cols, carry):
         out = inverse * scaled_ref[:, cols] - hidden_ref[:, cols].astype(f32) * pull
-        if with_input:
+        if own:
             out = out + base_ref[:, cols].astype(f32)
         out_ref[:, cols] = out.astype(bf16)
         return carry
@@ -543,18 +549,18 @@
             after=after,
         )[0]
 
-    def grad_input(pieces, aux, hidden, base, with_input, after):
+    def grad_input(pieces, aux, hidden, more, outs, after):
+        own = len(more) > 0
         return call(
-            functools.partial(grad_input_body, with_input), [shape(T, D)],
-            (aux, hidden, norm_gain, router_t, *pieces, base), grid=(1,),
-            in_specs=[aux_spec, full, vspec((1, D)), vspec((EXPERTS, D))] + piece_specs
-            + [full if with_input else vspec((16, D))],
-            out_specs=[full], scratch=[pltpu.VMEM((256, D + EXT), bf16), pltpu.VMEM((T, D), f32)],
+            functools.partial(grad_input_body, own), outs, (aux, hidden, norm_gain, *pieces, *more), grid=(1,),
+            in_specs=[aux_spec, full, vspec((1, D))] + piece_specs + ([vspec((EXPERTS, D)), full, aux_spec] if own else []),
+            out_specs=[full, aux_spec][: len(outs)], scratch=[pltpu.VMEM((256, D + EXT), bf16), pltpu.VMEM((T, D), f32)],
             flops=2 * pack_flops, after=after,
-        )[0]
-
-    part_far = grad_input(back_far, aux_b_far, far_b, far_b, False, outputs[0])
+        )
+
+    part_far, pulls = grad_input(back_far, aux_b_far, far_b, (), [shape(T, D), aux_shape], outputs[0])
     prev_far = relay(part_far, -1, 1)
+    far_pulls = across(pulls)
     halves = range(D // TB)
     y_far = [collect(outputs[8 * i + NX : 8 * i + 8]) for i in halves]
     y_own = [collect(outputs[8 * i : 8 * i + NX]) for i in halves]
@@ -562,7 +568,7 @@
     for i in halves:
         last = mix("far", i, y_far[i], aux_f_far, last)
         next_far.append(relay(last, 1, 1))
-    last = part_own = grad_input(back_own, aux_b, h_b, g, True, last)
+    (last,) = (part_own,) = grad_input(back_own, aux_b, h_b, (router_t, g, far_pulls), [shape(T, D)], last)
     prev_own = relay(part_own, -1, 0)
     for i in halves:
         last = mix("own", i, y_own[i], aux_f, last)

time: 260 us -> 262 us (level)
  waiting for transfers between devices: 102 us -> 105 us
    ppermute x5 -> x6, waiting for transfers between devices: 31.8 us -> 33.8 us  [across(): return lax.ppermute(block, 'ep', ep_route(1, 0))]
    ppermute x5 -> x6, starting transfers between devices: 14.1 us -> 14.8 us  [across(): return lax.ppermute(block, 'ep', ep_route(1, 0))]
  transfers between devices with their start and end apart: 47 -> 48, of which waited for: 15 -> 19; matrix products, arithmetic and copies ran while one was open for 0% -> 0% of each run, Pallas kernels for 32% -> 31%
where the time goes in v4:
time: 262 us; the launch traced here: 261 us
  waiting for transfers between devices  105 us (40%)
  Pallas kernels  84 us (32%)
  starting transfers between devices  71 us (27%)
    pallas_call x16, Pallas kernels, call(): pl.pallas_call(body, out_shape=outs, scratch_shapes=list(scratch), cost_e...  79.9 us
    ppermute x6, waiting for transfers between devices, across(): return lax.ppermute(block, 'ep', ep_route(1, 0))  33.8 us
    ppermute x18, starting transfers between devices, spread(): moved[dx] = lax.ppermute(pieces[dx], 'ep', ep_route(0, dx))  29 us
    ppermute x18, waiting for transfers between devices, collect(): moved[dx] = lax.ppermute(pieces[dx], 'ep', ep_route(0, -dx))  27.9 us
    ppermute x18, waiting for transfers between devices, spread(): moved[dx] = lax.ppermute(pieces[dx], 'ep', ep_route(0, dx))  23.7 us
    ppermute x18, starting transfers between devices, collect(): moved[dx] = lax.ppermute(pieces[dx], 'ep', ep_route(0, -dx))  23.1 us
    ppermute x6, waiting for transfers between devices, relay(): lax.ppermute(block, ('section', 'ep'), relay_route(lax.axis_size('section...  19.7 us
    ppermute x6, starting transfers between devices, across(): return lax.ppermute(block, 'ep', ep_route(1, 0))  14.8 us
  transfers between devices with their start and end apart: 48, of which 19 were waited for; matrix products, arithmetic and copies ran while one was open for 0% of the time, Pallas kernels for 31%

profile of v4, /device:TPU:0, one launch (start us, length us, event | category | flops | bytes accessed | tf_op | source)
XLA Modules:
  0.0 261.0 jit_solution(12906533644751303128)
XLA Ops:
  0.6 4.1 %collective-permute-start.1 = (bf16[128,3584]{1,0:T(8,128)(2,1)}, bf16[128,3584]{1,0:T(8,128)(2,1)}, u32[]{:S(2)}, u32[]{:S(2)}) collective-permute-start(bf16[128,3584]{1,0:T(8,128)(2,1)} %bitcast.18), channel_id=1, source_target_pairs={{0,4},{1,5},{2,6},{3,7},{4,0},{5,1},{6,2},{7,3},{8,12},{9,13},{10,... | collective-permute-start | bytes 2752520 | tf_op jit(solution)/shard_map/ppermute | solution.py:427
  4.8 3.0 %shard_map.113 = (bf16[48,3584]{1,0:T(8,128)(2,1)}, bf16[48,3584]{1,0:T(8,128)(2,1)}, bf16[48,3584]{1,0:T(8,128)(2,1)}, bf16[48,3584]{1,0:T(8,128)(2,1)}) custom-call(s32[1]{0:T(128)} %bitcast.place_ref.refs_0_, s32[2,128]{1,0:T(2,128)} %bitcast.36, bf16[128,3584]{1,0:T(8,128)(2,1)} %bitcast.19, f32[1,3584]{1,0:T(1,128)} %refs_2_.3), custom_call_target="tpu_custom_call" | custom-call | flops 176160768 | bytes 2309124 | tf_op jit(solution)/shard_map/pallas_call | solution.py:48
  9.3 2.7 %collective-permute-start.8 = (bf16[48,3584]{1,0:T(8,128)(2,1)}, bf16[48,3584]{1,0:T(8,128)(2,1)}, u32[]{:S(2)}, u32[]{:S(2)}) collective-permute-start(bf16[48,3584]{1,0:T(8,128)(2,1)} %get-tuple-element.67), channel_id=1, source_target_pairs={{0,2},{1,3},{2,0},{3,1},{4,6},{5,7},{6,4},{7,5},{8,10},{9,11},{10,... | collective-permute-start | bytes 1032200 | tf_op jit(solution)/shard_map/ppermute | solution.py:433
  12.1 3.4 %collective-permute-start.5 = (s32[2,128]{1,0:T(2,128)}, s32[2,128]{1,0:T(2,128)}, u32[]{:S(2)}, u32[]{:S(2)}) collective-permute-start(s32[2,128]{1,0:T(2,128)} %bitcast.39), channel_id=1, source_target_pairs={{0,4},{1,5},{2,6},{3,7},{4,0},{5,1},{6,2},{7,3},{8,12},{9,13},{10,... | collective-permute-start | bytes 3080 | tf_op jit(solution)/shard_map/ppermute | solution.py:427
  15.5 29.6 %collective-permute-done.5.refs_1_ = s32[2,128]{1,0:T(2,128)} collective-permute-done((s32[2,128]{1,0:T(2,128)}, s32[2,128]{1,0:T(2,128)}, u32[]{:S(2)}, u32[]{:S(2)}) %collective-permute-start.5) | collective-permute-done | bytes 1056 | tf_op jit(solution)/shard_map/ppermute | solution.py:427
  45.0 3.2 %collective-permute-start = (s32[2,128]{1,0:T(2,128)}, s32[2,128]{1,0:T(2,128)}, u32[]{:S(2)}, u32[]{:S(2)}) collective-permute-start(s32[2,128]{1,0:T(2,128)} %bitcast.37), channel_id=1, source_target_pairs={{0,4},{1,5},{2,6},{3,7},{4,0},{5,1},{6,2},{7,3},{8,12},{9,13},{10,... | collective-permute-start | bytes 3080 | tf_op jit(solution)/shard_map/ppermute | solution.py:427
  50.3 3.2 %collective-permute-start.6 = (bf16[128,3584]{1,0:T(8,128)(2,1)}, bf16[128,3584]{1,0:T(8,128)(2,1)}, u32[]{:S(2)}, u32[]{:S(2)}) collective-permute-start(bf16[128,3584]{1,0:T(8,128)(2,1)} %bitcast.22), channel_id=1, source_target_pairs={{0,4},{1,5},{2,6},{3,7},{4,0},{5,1},{6,2},{7,3},{8,12},{9,13},{10,... | collective-permute-start | bytes 2752520 | tf_op jit(solution)/shard_map/ppermute | solution.py:427
  53.5 3.8 %shard_map.114 = (bf16[48,3584]{1,0:T(8,128)(2,1)}, bf16[48,3584]{1,0:T(8,128)(2,1)}, bf16[48,3584]{1,0:T(8,128)(2,1)}, bf16[48,3584]{1,0:T(8,128)(2,1)}, f32[8,128]{1,0:T(8,128)}) custom-call(s32[1]{0:T(128)} %bitcast.place_ref.refs_0_, s32[2,128]{1,0:T(2,128)} %bitcast.38, bf16[128,3584]{1,0:T(8,128)(2,1)} %bitcast.20, f32[1,3584]{1,0:T(1,128)} %refs_2_.3, ...), custom_call_target="tpu_custom_call" | custom-call | flops 176160768 | bytes 3632132 | tf_op jit(solution)/shard_map/pallas_call | solution.py:48
  57.3 2.8 %collective-permute-start.9 = (bf16[48,3584]{1,0:T(8,128)(2,1)}, bf16[48,3584]{1,0:T(8,128)(2,1)}, u32[]{:S(2)}, u32[]{:S(2)}) collective-permute-start(bf16[48,3584]{1,0:T(8,128)(2,1)} %get-tuple-element.68), channel_id=1, source_target_pairs={{0,3},{1,0},{2,1},{3,2},{4,7},{5,4},{6,5},{7,6},{8,11},{9,8},{10,9... | collective-permute-start | bytes 1032200 | tf_op jit(solution)/shard_map/ppermute | solution.py:433
  62.3 3.3 %shard_map.115 = (bf16[48,3584]{1,0:T(8,128)(2,1)}, bf16[48,3584]{1,0:T(8,128)(2,1)}, bf16[48,3584]{1,0:T(8,128)(2,1)}, bf16[48,3584]{1,0:T(8,128)(2,1)}, f32[8,128]{1,0:T(8,128)}) custom-call(s32[1]{0:T(128)} %bitcast.place_ref.refs_0_, s32[2,128]{1,0:T(2,128)} %collective-permute-done.refs_1_, bf16[128,3584]{1,0:T(8,128)(2,1)} %collective-permute-done.1.refs_2_.refs_1_, ...), custom_call_target="tpu_custom_call" | custom-call | flops 176160768 | bytes 2714628 | tf_op jit(solution)/shard_map/pallas_call | solution.py:48
  65.6 12.2 %collective-permute-done.9.refs_3_ = bf16[48,3584]{1,0:T(8,128)(2,1)} collective-permute-done((bf16[48,3584]{1,0:T(8,128)(2,1)}, bf16[48,3584]{1,0:T(8,128)(2,1)}, u32[]{:S(2)}, u32[]{:S(2)}) %collective-permute-start.9) | collective-permute-done | bytes 344096 | tf_op jit(solution)/shard_map/ppermute | solution.py:433
  78.5 4.4 %collective-permute-start.11 = (bf16[48,3584]{1,0:T(8,128)(2,1)}, bf16[48,3584]{1,0:T(8,128)(2,1)}, u32[]{:S(2)}, u32[]{:S(2)}) collective-permute-start(bf16[48,3584]{1,0:T(8,128)(2,1)} %get-tuple-element.70), channel_id=1, source_target_pairs={{0,2},{1,3},{2,0},{3,1},{4,6},{5,7},{6,4},{7,5},{8,10},{9,11},{10,... | collective-permute-start | bytes 1032200 | tf_op jit(solution)/shard_map/ppermute | solution.py:433
  83.0 3.3 %shard_map.116 = (bf16[48,3584]{1,0:T(8,128)(2,1)}, bf16[48,3584]{1,0:T(8,128)(2,1)}, bf16[48,3584]{1,0:T(8,128)(2,1)}, bf16[48,3584]{1,0:T(8,128)(2,1)}, f32[8,128]{1,0:T(8,128)}) custom-call(s32[1]{0:T(128)} %bitcast.place_ref.refs_0_, s32[2,128]{1,0:T(2,128)} %bitcast.40, bf16[128,3584]{1,0:T(8,128)(2,1)} %bitcast.23, f32[1,3584]{1,0:T(1,128)} %refs_2_.3, ...), custom_call_target="tpu_custom_call" | custom-call | flops 176160768 | bytes 2714628 | tf_op jit(solution)/shard_map/pallas_call | solution.py:48
  86.3 2.8 %shard_map.117 = (bf16[48,3584]{1,0:T(8,128)(2,1)}, bf16[48,3584]{1,0:T(8,128)(2,1)}, bf16[48,3584]{1,0:T(8,128)(2,1)}, bf16[48,3584]{1,0:T(8,128)(2,1)}) custom-call(f32[8,128]{1,0:T(8,128)} %get-tuple-element.72.refs_0_, bf16[128,3584]{1,0:T(8,128)(2,1)} %collective-permute-done.13.refs_1_, bf16[48,3584]{1,0:T(8,128)(2,1)} %get-tuple-element.62.refs_2_.refs_0_), custom_call_target="tpu_custom_call" | custom-call | flops 176160768 | bytes 2641920 | tf_op jit(solution)/shard_map/pallas_call | solution.py:48
  93.1 6.6 %collective-permute-done.11.refs_6_ = bf16[48,3584]{1,0:T(8,128)(2,1)} collective-permute-done((bf16[48,3584]{1,0:T(8,128)(2,1)}, bf16[48,3584]{1,0:T(8,128)(2,1)}, u32[]{:S(2)}, u32[]{:S(2)}) %collective-permute-start.11) | collective-permute-done | bytes 344096 | tf_op jit(solution)/shard_map/ppermute | solution.py:433
  101.7 11.1 %shard_map.118 = (f32[2,384,512]{2,1,0:T(8,128)}, f32[2,384,512]{2,1,0:T(8,128)}) custom-call(bf16[48,3584]{1,0:T(8,128)(2,1)} %get-tuple-element.58.refs_6_.refs_0_, bf16[48,3584]{1,0:T(8,128)(2,1)} %collective-permute-done.7.refs_1_, bf16[48,3584]{1,0:T(8,128)(2,1)} %collective-permute-done.8.refs_2_, bf16[48,3584]{1,0:T(8,128)(2,1)} %collective-permute-done.9.refs_3_, ...), custom_call_target="tpu_custom_call" | custom-call | flops 5637144576 | bytes 20922368 | tf_op jit(solution)/shard_map/pallas_call | solution.py:48
  112.8 3.3 %shard_map.119 = (bf16[48,3584]{1,0:T(8,128)(2,1)}, bf16[48,3584]{1,0:T(8,128)(2,1)}, bf16[48,3584]{1,0:T(8,128)(2,1)}, bf16[48,3584]{1,0:T(8,128)(2,1)}, f32[8,128]{1,0:T(8,128)}) custom-call(s32[1]{0:T(128)} %bitcast.place_ref.refs_0_, s32[2,128]{1,0:T(2,128)} %collective-permute-done.5.refs_1_, bf16[128,3584]{1,0:T(8,128)(2,1)} %collective-permute-done.6.refs_2_.refs_5_, ...), custom_call_target="tpu_custom_call" | custom-call | flops 176160768 | bytes 3943428 | tf_op jit(solution)/shard_map/pallas_call | solution.py:48
  122.7 4.2 %collective-permute-start.16 = (bf16[48,3584]{1,0:T(8,128)(2,1)}, bf16[48,3584]{1,0:T(8,128)(2,1)}, u32[]{:S(2)}, u32[]{:S(2)}) collective-permute-start(bf16[48,3584]{1,0:T(8,128)(2,1)} %get-tuple-element.78), channel_id=1, source_target_pairs={{0,3},{1,0},{2,1},{3,2},{4,7},{5,4},{6,5},{7,6},{8,11},{9,8},{10,9... | collective-permute-start | bytes 1032200 | tf_op jit(solution)/shard_map/ppermute | solution.py:433
  126.9 15.4 %shard_map.120 = (bf16[48,3712]{1,0:T(8,128)(2,1)}, bf16[48,3712]{1,0:T(8,128)(2,1)}, bf16[48,3712]{1,0:T(8,128)(2,1)}, bf16[48,3712]{1,0:T(8,128)(2,1)}, bf16[4...) custom-call(bf16[48,3584]{1,0:T(8,128)(2,1)} %get-tuple-element.59.refs_5_.r, ...), custom_call_target="tpu_custom_call" | custom-call | flops 8455716864 | bytes 31113216 | tf_op jit(solution)/shard_map/pallas_call | solution.py:48
  144.7 2.6 collective-permute-done.16.refs_7_
  147.3 13.7 %shard_map.121 = (bf16[48,1792]{1,0:T(8,128)(2,1)}, bf16[48,1792]{1,0:T(8,128)(2,1)}, bf16[48,1792]{1,0:T(8,128)(2,1)}, bf16[48,1792]{1,0:T(8,128)(2,1)}, bf16[4...) custom-call(bf16[48,3584]{1,0:T(8,128)(2,1)} %get-tuple-element.62.r, ...), custom_call_target="tpu_custom_call" | custom-call | flops 8455716864 | bytes 27881472 | tf_op jit(solution)/shard_map/pallas_call | solution.py:48
  161.1 3.4 %collective-permute-start.36 = (bf16[48,1792]{1,0:T(8,128)(2,1)}, bf16[48,1792]{1,0:T(8,128)(2,1)}, u32[]{:S(2)}, u32[]{:S(2)}) collective-permute-start(bf16[48,1792]{1,0:T(8,128)(2,1)} %get-tuple-element.106), channel_id=1, source_target_pairs={{0,3},{1,0},{2,1},{3,2},{4,7},{5,4},{6,5},{7,6},{8,11},{9,8},{10,9... | collective-permute-start | bytes 516104 | tf_op jit(solution)/shard_map/ppermute | solution.py:440
  168.0 3.6 %shard_map.122 = (bf16[128,3584]{1,0:T(8,128)(2,1)}, f32[8,128]{1,0:T(8,128)}) custom-call(f32[8,128]{1,0:T(8,128)} %get-tuple-element.72.refs_0_, bf16[128,3584]{1,0:T(8,128)(2,1)} %collective-permute-done.1.refs_2_.refs_1_, f32[1,3584]{1,0:T(1,128)} %refs_2_.3, bf16[48,3712]{1,0:T(8,128)(2,1)} %get-tuple-element.99.refs_3_, ...), custom_call_target="tpu_custom_call" | custom-call | flops 352321536 | bytes 3454976 | tf_op jit(solution)/shard_map/pallas_call | solution.py:48
  177.7 10.4 %collective-permute-done.41.refs_4_ = bf16[48,1792]{1,0:T(8,128)(2,1)} collective-permute-done((bf16[48,1792]{1,0:T(8,128)(2,1)}, bf16[48,1792]{1,0:T(8,128)(2,1)}, u32[]{:S(2)}, u32[]{:S(2)}) %collective-permute-start.41) | collective-permute-done | bytes 172064 | tf_op jit(solution)/shard_map/ppermute | solution.py:440
  190.6 8.5 %collective-permute-done.38.refs_4_ = bf16[48,1792]{1,0:T(8,128)(2,1)} collective-permute-done((bf16[48,1792]{1,0:T(8,128)(2,1)}, bf16[48,1792]{1,0:T(8,128)(2,1)}, u32[]{:S(2)}, u32[]{:S(2)}) %collective-permute-start.38) | collective-permute-done | bytes 172064 | tf_op jit(solution)/shard_map/ppermute | solution.py:440
  204.6 4.1 %shard_map.125.refs_6_ = bf16[128,3584]{1,0:T(8,128)(2,1)} custom-call(f32[8,128]{1,0:T(8,128)} %get-tuple-element.95.refs_0_, bf16[128,3584]{1,0:T(8,128)(2,1)} %bitcast.21, f32[1,3584]{1,0:T(1,128)} %refs_2_.3, bf16[48,3712]{1,0:T(8,128)(2,1)} %get-tuple-element.86.refs_11_.refs_3_, bf16[48,3712]{1,0:T(8,128)(2,1)} %collective-permute-done.29.refs_4_, ...), custom_call_target="tpu_custom_call" | custom-call | flops 352321536 | bytes 4716544 | tf_op jit(solution)/shard_map/pallas_call | solution.py:48
  212.5 5.3 %collective-permute-done.26.refs_2_ = bf16[48,1792]{1,0:T(8,128)(2,1)} collective-permute-done((bf16[48,1792]{1,0:T(8,128)(2,1)}, bf16[48,1792]{1,0:T(8,128)(2,1)}, u32[]{:S(2)}, u32[]{:S(2)}) %collective-permute-start.26) | collective-permute-done | bytes 172064 | tf_op jit(solution)/shard_map/ppermute | solution.py:440
  224.8 2.6 %shard_map.126.refs_6_ = bf16[128,1792]{1,0:T(8,128)(2,1)} custom-call(f32[8,128]{1,0:T(8,128)} %get-tuple-element.61.refs_0_, bf16[48,1792]{1,0:T(8,128)(2,1)} %get-tuple-element.91.refs_7_.refs_1_, bf16[48,1792]{1,0:T(8,128)(2,1)} %collective-permute-done.26.refs_2_, bf16[48,1792]{1,0:T(8,128)(2,1)} %collective-permute-done.27.refs_3_, ...), custom_call_target="tpu_custom_call" | custom-call | flops 176160768 | bytes 2985984 | tf_op jit(solution)/shard_map/pallas_call | solution.py:48
  229.7 2.6 %shard_map.127.refs_2_ = bf16[128,1792]{1,0:T(8,128)(2,1)} custom-call(f32[8,128]{1,0:T(8,128)} %get-tuple-element.61.refs_0_, bf16[48,1792]{1,0:T(8,128)(2,1)} %get-tuple-element.87.refs_1_, bf16[48,1792]{1,0:T(8,128)(2,1)} %collective-permute-done.23.refs_2_, bf16[48,1792]{1,0:T(8,128)(2,1)} %collective-permute-done.24.refs_3_, ...), custom_call_target="tpu_custom_call" | custom-call | flops 176160768 | bytes 2527232 | tf_op jit(solution)/shard_map/pallas_call | solution.py:48
  237.2 7.2 %collective-permute-done.44.a_ref = bf16[128,1792]{1,0:T(8,128)(2,1)} collective-permute-done((bf16[128,1792]{1,0:T(8,128)(2,1)}, bf16[128,1792]{1,0:T(8,128)(2,1)}, u32[]{:S(2)}, u32[]{:S(2)}) %collective-permute-start.44) | collective-permute-done | bytes 458784 | tf_op jit(solution)/shard_map/ppermute | solution.py:445
  246.4 2.9 %collective-permute-done.42.a_ref = bf16[128,1792]{1,0:T(8,128)(2,1)} collective-permute-done((bf16[128,1792]{1,0:T(8,128)(2,1)}, bf16[128,1792]{1,0:T(8,128)(2,1)}, u32[]{:S(2)}, u32[]{:S(2)}) %collective-permute-start.42) | collective-permute-done | bytes 458784 | tf_op jit(solution)/shard_map/ppermute | solution.py:445
  249.3 9.6 %collective-permute-done.43.b_ref = bf16[128,1792]{1,0:T(8,128)(2,1)} collective-permute-done((bf16[128,1792]{1,0:T(8,128)(2,1)}, bf16[128,1792]{1,0:T(8,128)(2,1)}, u32[]{:S(2)}, u32[]{:S(2)}) %collective-permute-start.43) | collective-permute-done | bytes 458784 | tf_op jit(solution)/shard_map/ppermute | solution.py:445
  (82 shorter events, 61.3 us)
Async XLA Ops:
  0.6 59.4 %collective-permute-start.1 = (bf16[128,3584]{1,0:T(8,128)(2,1)}, bf16[128,3584]{1,0:T(8,128)(2,1)}, u32[]{:S(2)}, u32[]{:S(2)}) collective-permute-start(bf16[128,3584]{1,0:T(8,128)(2,1)} %bitcast.18), channel_id=1, source_target_pairs={{0,4},{1,5},{2,6},{3,7},{4,0},{5,1},{6,2},{7,3},{8,12},{9,13},{10,... | collective-permute-start | bytes 2752520 | tf_op jit(solution)/shard_map/ppermute | solution.py:427
  4.7 78.3 %collective-permute-start.13 = (bf16[128,3584]{1,0:T(8,128)(2,1)}, bf16[128,3584]{1,0:T(8,128)(2,1)}, u32[]{:S(2)}, u32[]{:S(2)}) collective-permute-start(bf16[128,3584]{1,0:T(8,128)(2,1)} %bitcast.26), channel_id=1, source_target_pairs={{0,4},{1,5},{2,6},{3,7},{4,0},{5,1},{6,2},{7,3},{8,12},{9,13},{10,... | collective-permute-start | bytes 2752520 | tf_op jit(solution)/shard_map/ppermute | solution.py:427
  7.8 49.4 %collective-permute-start.7 = (bf16[48,3584]{1,0:T(8,128)(2,1)}, bf16[48,3584]{1,0:T(8,128)(2,1)}, u32[]{:S(2)}, u32[]{:S(2)}) collective-permute-start(bf16[48,3584]{1,0:T(8,128)(2,1)} %get-tuple-element.66), channel_id=1, source_target_pairs={{0,1},{1,2},{2,3},{3,0},{4,5},{5,6},{6,7},{7,4},{8,9},{9,10},{10,1... | collective-permute-start | bytes 1032200 | tf_op jit(solution)/shard_map/ppermute | solution.py:433
  9.3 50.7 %collective-permute-start.8 = (bf16[48,3584]{1,0:T(8,128)(2,1)}, bf16[48,3584]{1,0:T(8,128)(2,1)}, u32[]{:S(2)}, u32[]{:S(2)}) collective-permute-start(bf16[48,3584]{1,0:T(8,128)(2,1)} %get-tuple-element.67), channel_id=1, source_target_pairs={{0,2},{1,3},{2,0},{3,1},{4,6},{5,7},{6,4},{7,5},{8,10},{9,11},{10,... | collective-permute-start | bytes 1032200 | tf_op jit(solution)/shard_map/ppermute | solution.py:433
  12.1 33.0 %collective-permute-start.5 = (s32[2,128]{1,0:T(2,128)}, s32[2,128]{1,0:T(2,128)}, u32[]{:S(2)}, u32[]{:S(2)}) collective-permute-start(s32[2,128]{1,0:T(2,128)} %bitcast.39), channel_id=1, source_target_pairs={{0,4},{1,5},{2,6},{3,7},{4,0},{5,1},{6,2},{7,3},{8,12},{9,13},{10,... | collective-permute-start | bytes 3080 | tf_op jit(solution)/shard_map/ppermute | solution.py:427
  50.3 39.4 %collective-permute-start.6 = (bf16[128,3584]{1,0:T(8,128)(2,1)}, bf16[128,3584]{1,0:T(8,128)(2,1)}, u32[]{:S(2)}, u32[]{:S(2)}) collective-permute-start(bf16[128,3584]{1,0:T(8,128)(2,1)} %bitcast.22), channel_id=1, source_target_pairs={{0,4},{1,5},{2,6},{3,7},{4,0},{5,1},{6,2},{7,3},{8,12},{9,13},{10,... | collective-permute-start | bytes 2752520 | tf_op jit(solution)/shard_map/ppermute | solution.py:427
  57.3 20.5 %collective-permute-start.9 = (bf16[48,3584]{1,0:T(8,128)(2,1)}, bf16[48,3584]{1,0:T(8,128)(2,1)}, u32[]{:S(2)}, u32[]{:S(2)}) collective-permute-start(bf16[48,3584]{1,0:T(8,128)(2,1)} %get-tuple-element.68), channel_id=1, source_target_pairs={{0,3},{1,0},{2,1},{3,2},{4,7},{5,4},{6,5},{7,6},{8,11},{9,8},{10,9... | collective-permute-start | bytes 1032200 | tf_op jit(solution)/shard_map/ppermute | solution.py:433
  60.0 18.5 %collective-permute-start.17 = (bf16[48,3584]{1,0:T(8,128)(2,1)}, bf16[48,3584]{1,0:T(8,128)(2,1)}, u32[]{:S(2)}, u32[]{:S(2)}) collective-permute-start(bf16[48,3584]{1,0:T(8,128)(2,1)} %get-tuple-element.79), channel_id=1, source_target_pairs={{0,1},{1,2},{2,3},{3,0},{4,5},{5,6},{6,7},{7,4},{8,9},{9,10},{10,1... | collective-permute-start | bytes 1032200 | tf_op jit(solution)/shard_map/ppermute | solution.py:433
  60.0 29.0 %collective-permute-start.18 = (bf16[48,3584]{1,0:T(8,128)(2,1)}, bf16[48,3584]{1,0:T(8,128)(2,1)}, u32[]{:S(2)}, u32[]{:S(2)}) collective-permute-start(bf16[48,3584]{1,0:T(8,128)(2,1)} %get-tuple-element.80), channel_id=1, source_target_pairs={{0,2},{1,3},{2,0},{3,1},{4,6},{5,7},{6,4},{7,5},{8,10},{9,11},{10,... | collective-permute-start | bytes 1032200 | tf_op jit(solution)/shard_map/ppermute | solution.py:433
  78.5 21.1 %collective-permute-start.11 = (bf16[48,3584]{1,0:T(8,128)(2,1)}, bf16[48,3584]{1,0:T(8,128)(2,1)}, u32[]{:S(2)}, u32[]{:S(2)}) collective-permute-start(bf16[48,3584]{1,0:T(8,128)(2,1)} %get-tuple-element.70), channel_id=1, source_target_pairs={{0,2},{1,3},{2,0},{3,1},{4,6},{5,7},{6,4},{7,5},{8,10},{9,11},{10,... | collective-permute-start | bytes 1032200 | tf_op jit(solution)/shard_map/ppermute | solution.py:433
  83.0 16.7 %collective-permute-start.12 = (bf16[48,3584]{1,0:T(8,128)(2,1)}, bf16[48,3584]{1,0:T(8,128)(2,1)}, u32[]{:S(2)}, u32[]{:S(2)}) collective-permute-start(bf16[48,3584]{1,0:T(8,128)(2,1)} %get-tuple-element.71), channel_id=1, source_target_pairs={{0,3},{1,0},{2,1},{3,2},{4,7},{5,4},{6,5},{7,6},{8,11},{9,8},{10,9... | collective-permute-start | bytes 1032200 | tf_op jit(solution)/shard_map/ppermute | solution.py:433
  89.0 27.0 %collective-permute-start.19 = (bf16[48,3584]{1,0:T(8,128)(2,1)}, bf16[48,3584]{1,0:T(8,128)(2,1)}, u32[]{:S(2)}, u32[]{:S(2)}) collective-permute-start(bf16[48,3584]{1,0:T(8,128)(2,1)} %get-tuple-element.81), channel_id=1, source_target_pairs={{0,3},{1,0},{2,1},{3,2},{4,7},{5,4},{6,5},{7,6},{8,11},{9,8},{10,9... | collective-permute-start | bytes 1032200 | tf_op jit(solution)/shard_map/ppermute | solution.py:433
  89.7 27.9 %collective-permute-start.2 = (bf16[48,3584]{1,0:T(8,128)(2,1)}, bf16[48,3584]{1,0:T(8,128)(2,1)}, u32[]{:S(2)}, u32[]{:S(2)}) collective-permute-start(bf16[48,3584]{1,0:T(8,128)(2,1)} %get-tuple-element.63), channel_id=1, source_target_pairs={{0,1},{1,2},{2,3},{3,0},{4,5},{5,6},{6,7},{7,4},{8,9},{9,10},{10,1... | collective-permute-start | bytes 1032200 | tf_op jit(solution)/shard_map/ppermute | solution.py:433
  91.2 28.2 %collective-permute-start.20 = (bf16[48,3584]{1,0:T(8,128)(2,1)}, bf16[48,3584]{1,0:T(8,128)(2,1)}, u32[]{:S(2)}, u32[]{:S(2)}) collective-permute-start(bf16[48,3584]{1,0:T(8,128)(2,1)} %get-tuple-element.82), channel_id=1, source_target_pairs={{0,1},{1,2},{2,3},{3,0},{4,5},{5,6},{6,7},{7,4},{8,9},{9,10},{10,1... | collective-permute-start | bytes 1032200 | tf_op jit(solution)/shard_map/ppermute | solution.py:433
  99.7 19.9 %collective-permute-start.21 = (bf16[48,3584]{1,0:T(8,128)(2,1)}, bf16[48,3584]{1,0:T(8,128)(2,1)}, u32[]{:S(2)}, u32[]{:S(2)}) collective-permute-start(bf16[48,3584]{1,0:T(8,128)(2,1)} %get-tuple-element.83), channel_id=1, source_target_pairs={{0,2},{1,3},{2,0},{3,1},{4,6},{5,7},{6,4},{7,5},{8,10},{9,11},{10,... | collective-permute-start | bytes 1032200 | tf_op jit(solution)/shard_map/ppermute | solution.py:433
  99.7 23.0 %collective-permute-start.22 = (bf16[48,3584]{1,0:T(8,128)(2,1)}, bf16[48,3584]{1,0:T(8,128)(2,1)}, u32[]{:S(2)}, u32[]{:S(2)}) collective-permute-start(bf16[48,3584]{1,0:T(8,128)(2,1)} %get-tuple-element.84), channel_id=1, source_target_pairs={{0,3},{1,0},{2,1},{3,2},{4,7},{5,4},{6,5},{7,6},{8,11},{9,8},{10,9... | collective-permute-start | bytes 1032200 | tf_op jit(solution)/shard_map/ppermute | solution.py:433
  116.1 26.3 %collective-permute-start.3 = (bf16[48,3584]{1,0:T(8,128)(2,1)}, bf16[48,3584]{1,0:T(8,128)(2,1)}, u32[]{:S(2)}, u32[]{:S(2)}) collective-permute-start(bf16[48,3584]{1,0:T(8,128)(2,1)} %get-tuple-element.64), channel_id=1, source_target_pairs={{0,2},{1,3},{2,0},{3,1},{4,6},{5,7},{6,4},{7,5},{8,10},{9,11},{10,... | collective-permute-start | bytes 1032200 | tf_op jit(solution)/shard_map/ppermute | solution.py:433
  117.5 24.9 %collective-permute-start.4 = (bf16[48,3584]{1,0:T(8,128)(2,1)}, bf16[48,3584]{1,0:T(8,128)(2,1)}, u32[]{:S(2)}, u32[]{:S(2)}) collective-permute-start(bf16[48,3584]{1,0:T(8,128)(2,1)} %get-tuple-element.65), channel_id=1, source_target_pairs={{0,3},{1,0},{2,1},{3,2},{4,7},{5,4},{6,5},{7,6},{8,11},{9,8},{10,9... | collective-permute-start | bytes 1032200 | tf_op jit(solution)/shard_map/ppermute | solution.py:433
  119.3 23.2 %collective-permute-start.14 = (bf16[48,3584]{1,0:T(8,128)(2,1)}, bf16[48,3584]{1,0:T(8,128)(2,1)}, u32[]{:S(2)}, u32[]{:S(2)}) collective-permute-start(bf16[48,3584]{1,0:T(8,128)(2,1)} %get-tuple-element.76), channel_id=1, source_target_pairs={{0,1},{1,2},{2,3},{3,0},{4,5},{5,6},{6,7},{7,4},{8,9},{9,10},{10,1... | collective-permute-start | bytes 1032200 | tf_op jit(solution)/shard_map/ppermute | solution.py:433
  119.6 25.2 %collective-permute-start.15 = (bf16[48,3584]{1,0:T(8,128)(2,1)}, bf16[48,3584]{1,0:T(8,128)(2,1)}, u32[]{:S(2)}, u32[]{:S(2)}) collective-permute-start(bf16[48,3584]{1,0:T(8,128)(2,1)} %get-tuple-element.77), channel_id=1, source_target_pairs={{0,2},{1,3},{2,0},{3,1},{4,6},{5,7},{6,4},{7,5},{8,10},{9,11},{10,... | collective-permute-start | bytes 1032200 | tf_op jit(solution)/shard_map/ppermute | solution.py:433
  122.7 24.6 %collective-permute-start.16 = (bf16[48,3584]{1,0:T(8,128)(2,1)}, bf16[48,3584]{1,0:T(8,128)(2,1)}, u32[]{:S(2)}, u32[]{:S(2)}) collective-permute-start(bf16[48,3584]{1,0:T(8,128)(2,1)} %get-tuple-element.78), channel_id=1, source_target_pairs={{0,3},{1,0},{2,1},{3,2},{4,7},{5,4},{6,5},{7,6},{8,11},{9,8},{10,9... | collective-permute-start | bytes 1032200 | tf_op jit(solution)/shard_map/ppermute | solution.py:433
  142.3 22.7 %collective-permute-start.32 = (bf16[48,3712]{1,0:T(8,128)(2,1)}, bf16[48,3712]{1,0:T(8,128)(2,1)}, u32[]{:S(2)}, u32[]{:S(2)}) collective-permute-start(bf16[48,3712]{1,0:T(8,128)(2,1)} %get-tuple-element.100), channel_id=1, source_target_pairs={{0,3},{1,0},{2,1},{3,2},{4,7},{5,4},{6,5},{7,6},{8,11},{9,8},{10,9... | collective-permute-start | bytes 1069064 | tf_op jit(solution)/shard_map/ppermute | solution.py:440
  142.4 23.4 %collective-permute-start.33 = (bf16[48,3712]{1,0:T(8,128)(2,1)}, bf16[48,3712]{1,0:T(8,128)(2,1)}, u32[]{:S(2)}, u32[]{:S(2)}) collective-permute-start(bf16[48,3712]{1,0:T(8,128)(2,1)} %get-tuple-element.101), channel_id=1, source_target_pairs={{0,2},{1,3},{2,0},{3,1},{4,6},{5,7},{6,4},{7,5},{8,10},{9,11},{10,... | collective-permute-start | bytes 1069064 | tf_op jit(solution)/shard_map/ppermute | solution.py:440
  142.5 25.5 %collective-permute-start.34 = (bf16[48,3712]{1,0:T(8,128)(2,1)}, bf16[48,3712]{1,0:T(8,128)(2,1)}, u32[]{:S(2)}, u32[]{:S(2)}) collective-permute-start(bf16[48,3712]{1,0:T(8,128)(2,1)} %get-tuple-element.102), channel_id=1, source_target_pairs={{0,1},{1,2},{2,3},{3,0},{4,5},{5,6},{6,7},{7,4},{8,9},{9,10},{10,1... | collective-permute-start | bytes 1069064 | tf_op jit(solution)/shard_map/ppermute | solution.py:440
  171.7 60.6 %collective-permute-start.47 = (bf16[128,3584]{1,0:T(8,128)(2,1)}, bf16[128,3584]{1,0:T(8,128)(2,1)}, u32[]{:S(2)}, u32[]{:S(2)}) collective-permute-start(bf16[128,3584]{1,0:T(8,128)(2,1)} %get-tuple-element.113.refs_6_), channel_id=1, source_target_pairs={{0,124},{1,125},{2,126},{3,127},{4,120},{5,121},{6,122},{7,123},{8... | collective-permute-start | bytes 2752520 | tf_op jit(solution)/shard_map/ppermute | solution.py:445
  173.1 29.2 %collective-permute-start.29 = (bf16[48,3712]{1,0:T(8,128)(2,1)}, bf16[48,3712]{1,0:T(8,128)(2,1)}, u32[]{:S(2)}, u32[]{:S(2)}) collective-permute-start(bf16[48,3712]{1,0:T(8,128)(2,1)} %get-tuple-element.96), channel_id=1, source_target_pairs={{0,3},{1,0},{2,1},{3,2},{4,7},{5,4},{6,5},{7,6},{8,11},{9,8},{10,9... | collective-permute-start | bytes 1069064 | tf_op jit(solution)/shard_map/ppermute | solution.py:440
  175.0 27.3 %collective-permute-start.30 = (bf16[48,3712]{1,0:T(8,128)(2,1)}, bf16[48,3712]{1,0:T(8,128)(2,1)}, u32[]{:S(2)}, u32[]{:S(2)}) collective-permute-start(bf16[48,3712]{1,0:T(8,128)(2,1)} %get-tuple-element.97), channel_id=1, source_target_pairs={{0,2},{1,3},{2,0},{3,1},{4,6},{5,7},{6,4},{7,5},{8,10},{9,11},{10,... | collective-permute-start | bytes 1069064 | tf_op jit(solution)/shard_map/ppermute | solution.py:440
  175.3 27.0 %collective-permute-start.31 = (bf16[48,3712]{1,0:T(8,128)(2,1)}, bf16[48,3712]{1,0:T(8,128)(2,1)}, u32[]{:S(2)}, u32[]{:S(2)}) collective-permute-start(bf16[48,3712]{1,0:T(8,128)(2,1)} %get-tuple-element.98), channel_id=1, source_target_pairs={{0,1},{1,2},{2,3},{3,0},{4,5},{5,6},{6,7},{7,4},{8,9},{9,10},{10,1... | collective-permute-start | bytes 1069064 | tf_op jit(solution)/shard_map/ppermute | solution.py:440
  208.6 26.0 %collective-permute-start.46 = (bf16[128,3584]{1,0:T(8,128)(2,1)}, bf16[128,3584]{1,0:T(8,128)(2,1)}, u32[]{:S(2)}, u32[]{:S(2)}) collective-permute-start(bf16[128,3584]{1,0:T(8,128)(2,1)} %shard_map.125.refs_6_), channel_id=1, source_target_pairs={{0,120},{1,121},{2,122},{3,123},{4,124},{5,125},{6,126},{7,127},{8... | collective-permute-start | bytes 2752520 | tf_op jit(solution)/shard_map/ppermute | solution.py:445
  227.4 17.0 %collective-permute-start.45 = (bf16[128,1792]{1,0:T(8,128)(2,1)}, bf16[128,1792]{1,0:T(8,128)(2,1)}, u32[]{:S(2)}, u32[]{:S(2)}) collective-permute-start(bf16[128,1792]{1,0:T(8,128)(2,1)} %shard_map.123.refs_6_), channel_id=1, source_target_pairs={{0,12},{1,13},{2,14},{3,15},{4,8},{5,9},{6,10},{7,11},{8,20},{9,21... | collective-permute-start | bytes 1376264 | tf_op jit(solution)/shard_map/ppermute | solution.py:445
  232.3 17.0 %collective-permute-start.42 = (bf16[128,1792]{1,0:T(8,128)(2,1)}, bf16[128,1792]{1,0:T(8,128)(2,1)}, u32[]{:S(2)}, u32[]{:S(2)}) collective-permute-start(bf16[128,1792]{1,0:T(8,128)(2,1)} %shard_map.127.refs_2_), channel_id=1, source_target_pairs={{0,8},{1,9},{2,10},{3,11},{4,12},{5,13},{6,14},{7,15},{8,16},{9,17... | collective-permute-start | bytes 1376264 | tf_op jit(solution)/shard_map/ppermute | solution.py:445
  232.3 26.6 %collective-permute-start.43 = (bf16[128,1792]{1,0:T(8,128)(2,1)}, bf16[128,1792]{1,0:T(8,128)(2,1)}, u32[]{:S(2)}, u32[]{:S(2)}) collective-permute-start(bf16[128,1792]{1,0:T(8,128)(2,1)} %shard_map.124.refs_10_), channel_id=1, source_target_pairs={{0,12},{1,13},{2,14},{3,15},{4,8},{5,9},{6,10},{7,11},{8,20},{9,21... | collective-permute-start | bytes 1376264 | tf_op jit(solution)/shard_map/ppermute | solution.py:445
  (16 other events, 158.1 us)
